TPU v7x, 64 devices: a 2x2x8 block of a 4x4x8 slice. The times are simulated.
64 devices in a mesh: member: 4 (over x, y), lat: 16 (over z, core).
Axes of the slice: x: 2, y: 2, z: 8, core: 2. Of those that a mesh axis runs over, the one named last changes fastest.
The devices are a block of a 4x4x8 slice.
Arguments:
- field_in: float32 [48, 128, 96, 192], P('member', None, 'lat'), parts along dimension 0
- grad_out: float32 [48, 128, 96, 192], P('member', None, 'lat'), parts along dimension 0
- p_fwd: float32 [96, 96, 96], replicated
- p_inv: float32 [96, 96, 96], replicated
- w_mix: float32 [96, 128, 128, 2], replicated
Outputs:
- output 1: float32 [48, 128, 96, 192], P('member', None, 'lat'), parts along dimension 0
- output 2: float32 [384, 128, 128, 2], P('member'), parts along dimension 0
There are 4 independent parts. A program takes and returns all parts, laid end to end along the dimension named above; an argument that names none is the same for every part.
All inputs are finite; a program needn't handle non-finite values.
Results may differ from a plain program's by a relative error of at most 0.0062904.
Values are sent between devices in bfloat16 or wider.
A program may use at most 768 MiB of HBM per device.

v0:
```python
import math
import jax
import jax.numpy as jnp
from jax import lax
from jax.sharding import PartitionSpec as P


def gelu_grad(values):
    cumulative = 0.5 * (1.0 + lax.erf(values * math.sqrt(0.5)))
    density = jnp.exp(-0.5 * values * values) / math.sqrt(2.0 * math.pi)
    return cumulative + values * density


def mix_matrix(w_mix):
    w_real = w_mix[..., 0]
    w_imag = w_mix[..., 1]
    upper_half = jnp.stack([w_real, -w_imag], axis=-1)
    lower_half = jnp.stack([w_imag, w_real], axis=-1)
    return jnp.stack([upper_half, lower_half], axis=2).astype(jnp.bfloat16)


def analysis(values, mode_count, mode_gains):
    spectrum = jnp.fft.rfft(values, axis=-1)[..., :mode_count] * mode_gains
    return jnp.stack([spectrum.real, spectrum.imag], axis=-2).astype(jnp.bfloat16)


def synthesis(spec_pair, lon_count, mode_gains):
    complex_spec = lax.complex(spec_pair[..., 0, :].astype(jnp.float32), spec_pair[..., 1, :].astype(jnp.float32)) * mode_gains
    pad_width = [(0, 0)] * (complex_spec.ndim - 1) + [(0, lon_count // 2 + 1 - complex_spec.shape[-1])]
    return jnp.fft.irfft(jnp.pad(complex_spec, pad_width), n=lon_count, axis=-1)


def solution(mesh):
    lat_size = mesh.shape['lat']
    field_spec = P('member', None, 'lat', None)

    def local_step(field_loc, grad_loc, p_fwd, p_inv, w_mix):
        lon_count = field_loc.shape[-1]
        lat_count = p_fwd.shape[-1]
        m_local = lat_count // lat_size
        m_start = lax.axis_index('lat') * m_local
        root_lon = math.sqrt(lon_count)
        is_mean = jnp.arange(lat_count) == 0
        pw_own = lax.dynamic_slice_in_dim(p_fwd, m_start, m_local, axis=0).astype(jnp.bfloat16)
        pi_own = lax.dynamic_slice_in_dim(p_inv, m_start, m_local, axis=0).astype(jnp.bfloat16)
        w_big = mix_matrix(w_mix)
        four_lat = analysis(field_loc, lat_count, 1.0 / root_lon)
        four_own = lax.all_to_all(four_lat, 'lat', 4, 2, tiled=True)
        coeffs = jnp.einsum('mlt,bctrm->bclrm', pw_own, four_own, preferred_element_type=jnp.float32).astype(jnp.bfloat16)
        mixed_coef = jnp.einsum('losir,bilrm->bolsm', w_big, coeffs, preferred_element_type=jnp.float32).astype(jnp.bfloat16)
        back_own = jnp.einsum('mlt,bclrm->bctrm', pi_own, mixed_coef, preferred_element_type=jnp.float32).astype(jnp.bfloat16)
        back_lat = lax.all_to_all(back_own, 'lat', 2, 4, tiled=True)
        hidden = synthesis(back_lat, lon_count, root_lon)
        grad_hidden = grad_loc * gelu_grad(hidden)
        grad_back_lat = analysis(grad_hidden, lat_count, jnp.where(is_mean, 1.0, 2.0) / root_lon)
        grad_back_own = lax.all_to_all(grad_back_lat, 'lat', 4, 2, tiled=True)
        grad_mixed = jnp.einsum('mlt,bctrm->bclrm', pi_own, grad_back_own, preferred_element_type=jnp.float32).astype(jnp.bfloat16)
        gw_part = jnp.einsum('bolsm,bilrm->losir', grad_mixed, coeffs, preferred_element_type=jnp.float32)
        gw_total = lax.psum(gw_part, 'lat')
        grad_coef = jnp.einsum('losir,bolsm->bilrm', w_big, grad_mixed, preferred_element_type=jnp.float32).astype(jnp.bfloat16)
        grad_four_own = jnp.einsum('mlt,bclrm->bctrm', pw_own, grad_coef, preferred_element_type=jnp.float32).astype(jnp.bfloat16)
        grad_four_lat = lax.all_to_all(grad_four_own, 'lat', 2, 4, tiled=True)
        grad_field = grad_loc + synthesis(grad_four_lat, lon_count, jnp.where(is_mean, 1.0, 0.5) * root_lon)
        grad_wmix = jnp.stack([gw_total[:, :, 0, :, 0] + gw_total[:, :, 1, :, 1], gw_total[:, :, 1, :, 0] - gw_total[:, :, 0, :, 1]], axis=-1)
        return grad_field, grad_wmix

    return jax.shard_map(local_step, mesh=mesh, in_specs=(field_spec, field_spec, P(), P(), P()), out_specs=(field_spec, P('member', None, None, None)), check_vma=False)
```

profile of v0, /device:TPU:21, one launch (start us, length us, event | category | flops | bytes accessed | tf_op | source)
XLA Modules:
  0.0 1253.1 jit_solution(9332270851431530587)
XLA Ops:
  35.6 17.4 %fusion.280 = (f32[12,128,6,64,3]{1,3,4,2,0:T(8,128)}, f32[12,128,6,64,3]{1,3,4,2,0:T(8,128)}, f32[12,128,6,64,3]{1,3,4,2,0:T(8,128)}) fusion(f32[64,3]{0,1:T(4,128)S(1)} %get-tuple-element.60, f32[64,3]{0,1:T(4,128)S(1)} %get-tuple-element.59, f32[12,128,6,3,64]{1,4,3,2,0:T(8,128)S(1)} %copy-done, f32[64,12,128,6,3]{2,0,4,3,1:T(8,128)} %fusion.62, ...), kind=kOutput, calls=%fused_computation.297 | convolution fusion | flops 1374900224 | bytes 42468864 | tf_op jit(solution)/shard_map/jit(fft)/dot.13 | solution.py:23
  53.0 24.1 %fusion.26 = f32[12,128,6,64,3]{1,4,3,2,0:T(4,128)S(1)} fusion(f32[12,128,6,64,3]{1,3,4,2,0:T(8,128)} %get-tuple-element.38), kind=kOutput, calls=%fused_computation.31 | convolution fusion | flops 63701028 | bytes 14155776 | tf_op jit(solution)/shard_map/jit(fft)/dot.3 | solution.py:23
  77.1 21.0 %add_bitcast_fusion.1 = f32[12,128,6,3,64]{1,3,4,2,0:T(4,128)} fusion(f32[12,128,6,64,3]{1,4,3,2,0:T(4,128)S(1)} %fusion.26, f32[12,128,6,64,3]{1,3,4,2,0:T(8,128)S(1)} %copy-done.6), kind=kOutput, calls=%fused_computation.37 | convolution fusion | flops 65470508 | bytes 21233664 | tf_op jit(solution)/shard_map/jit(fft)/dot.4 | solution.py:23
  98.1 21.5 %subtract_bitcast_fusion.1 = f32[12,128,6,3,64]{1,3,4,2,0:T(4,128)} fusion(f32[12,128,6,64,3]{1,4,3,2,0:T(4,128)S(1)} %fusion.26, f32[12,128,6,64,3]{1,3,4,2,0:T(8,128)S(1)} %bitcast.395), kind=kOutput, calls=%fused_computation.38 | convolution fusion | flops 65470508 | bytes 21233664 | tf_op jit(solution)/shard_map/jit(fft)/dot.5 | solution.py:23
  173.6 53.3 %all-to-all-done = bf16[12,128,6,2,96]{1,3,2,0,4:T(2,128)(2,1)S(1)} async-done(((bf16[12,128,6,2,96]{1,3,2,0,4:T(2,128)(2,1)}), bf16[12,128,6,2,96]{1,3,2,0,4:T(2,128)(2,1)S(1)}, u32[]{:S(2)}, u32[]{:S(2)}) %all-to-all-start) | async-done | bytes 3538976 | tf_op jit(solution)/shard_map/all_to_all | solution.py:48
  263.4 77.7 %all-to-all-done.1 = bf16[12,128,96,2,6]{1,3,0,4,2:T(2,128)(2,1)S(1)} async-done(((bf16[12,128,96,2,6]{1,3,0,4,2:T(2,128)(2,1)}), bf16[12,128,96,2,6]{1,3,0,4,2:T(2,128)(2,1)S(1)}, u32[]{:S(2)}, u32[]{:S(2)}) %all-to-all-start.1) | async-done | bytes 3538976 | tf_op jit(solution)/shard_map/all_to_all | solution.py:52
  358.4 35.1 %reverse.9 = f32[12,128,6,95]{1,3,2,0:T(8,128)} reverse(f32[12,128,6,95]{1,3,2,0:T(8,128)} %slice.83), dimensions={3} | reverse | bytes 7004160 | tf_op jit(solution)/shard_map/jit(fft)/reverse.1 | solution.py:30
  414.2 35.1 %reverse.8 = f32[12,128,6,95]{1,3,2,0:T(8,128)} reverse(f32[12,128,6,95]{1,3,2,0:T(8,128)} %slice.82), dimensions={3} | reverse | bytes 7004160 | tf_op jit(solution)/shard_map/jit(fft)/reverse | solution.py:30
  515.7 23.9 %fusion.18 = f32[12,128,6,64,3]{1,4,3,2,0:T(4,128)S(1)} fusion(f32[12,128,6,64,3]{1,3,4,2,0:T(8,128)} %get-tuple-element.36), kind=kOutput, calls=%fused_computation.23 | convolution fusion | flops 63701036 | bytes 14155776 | tf_op jit(solution)/shard_map/jit(fft)/dot.10 | solution.py:30
  539.7 20.5 %fusion.16 = f32[12,128,6,64,3]{1,4,3,2,0:T(4,128)} fusion(f32[12,128,6,64,3]{1,3,4,2,0:T(8,128)S(1)} %get-tuple-element.37), kind=kOutput, calls=%fused_computation.21 | convolution fusion | flops 63701036 | bytes 14155776 | tf_op jit(solution)/shard_map/jit(fft)/dot.11 | solution.py:30
  560.2 29.3 %multiply_bitcast_fusion.1 = f32[12,128,6,3,64]{1,3,4,2,0:T(4,128)S(1)} fusion(f32[12,128,6,64,3]{1,4,3,2,0:T(4,128)} %fusion.16, f32[12,128,6,64,3]{1,4,3,2,0:T(4,128)S(1)} %fusion.18, f32[12,128,6,64,3]{1,3,4,2,0:T(8,128)} %get-tuple-element.35), kind=kOutput, calls=%fused_computation.36 | convolution fusion | flops 72548384 | bytes 28311552 | tf_op jit(solution)/shard_map/jit(fft)/dot.9 | solution.py:30
  622.0 17.3 %fusion.276 = (f32[12,128,6,64,3]{1,3,4,2,0:T(8,128)S(1)}, f32[12,128,6,64,3]{1,3,4,2,0:T(8,128)}, f32[12,128,6,64,3]{1,3,4,2,0:T(8,128)}) fusion(f32[64,3]{0,1:T(4,128)S(1)} %copy-done.20, f32[64,3]{0,1:T(4,128)S(1)} %copy-done.18, f32[12,128,6,3,64]{1,4,3,2,0:T(8,128)} %fusion.96, f32[64,12,128,6,3]{2,0,4,3,1:T(8,128)} %fusion.58, ...), kind=kOutput, calls=%fused_computation.295 | convolution fusion | flops 1374900224 | bytes 42468864 | tf_op jit(solution)/shard_map/jit(fft)/dot.13 | solution.py:23
  639.3 19.0 %fusion.14 = f32[12,128,6,64,3]{1,4,3,2,0:T(4,128)S(1)} fusion(f32[12,128,6,64,3]{1,3,4,2,0:T(8,128)S(1)} %get-tuple-element.32), kind=kOutput, calls=%fused_computation.19 | convolution fusion | flops 63701028 | bytes 14155776 | tf_op jit(solution)/shard_map/jit(fft)/dot.3 | solution.py:23
  658.3 24.6 %add_bitcast_fusion = f32[12,128,6,3,64]{1,3,4,2,0:T(4,128)S(1)} fusion(f32[12,128,6,64,3]{1,4,3,2,0:T(4,128)S(1)} %fusion.14, f32[12,128,6,64,3]{1,3,4,2,0:T(8,128)} %get-tuple-element.34), kind=kOutput, calls=%fused_computation.34 | convolution fusion | flops 65470508 | bytes 21233664 | tf_op jit(solution)/shard_map/jit(fft)/dot.4 | solution.py:23
  683.0 21.4 %subtract_bitcast_fusion = f32[12,128,6,3,64]{1,3,4,2,0:T(4,128)} fusion(f32[12,128,6,64,3]{1,4,3,2,0:T(4,128)S(1)} %fusion.14, f32[12,128,6,64,3]{1,3,4,2,0:T(8,128)S(1)} %bitcast.393), kind=kOutput, calls=%fused_computation.35 | convolution fusion | flops 65470508 | bytes 21233664 | tf_op jit(solution)/shard_map/jit(fft)/dot.5 | solution.py:23
  720.2 89.3 %all_to_all.68 = bf16[12,128,6,2,96]{1,3,2,0,4:T(2,128)(2,1)S(1)} all-to-all(bf16[12,128,6,2,96]{1,3,2,0,4:T(2,128)(2,1)S(1)} %copy.235), channel_id=1, replica_groups=mesh['member'=4,'lat'=16] {'lat'}, dimensions={4} | all-to-all | bytes 7077888 | tf_op jit(solution)/shard_map/all_to_all | solution.py:56
  844.4 17.6 %convolution_bitcast_fusion = f32[96,128,2,128,2]{3,1,4,2,0:T(8,128)} fusion(bf16[12,128,96,2,6,1]{1,2,3,0,4,5:T(8,128)(2,1)S(1)} %copy-done.4, bf16[12,128,96,2,6,1]{1,2,3,0,4,5:T(8,128)(2,1)} %copy-done.5), kind=kOutput, calls=%fused_computation.39 | convolution fusion | flops 905969664 | bytes 32243712 | tf_op jit(solution)/shard_map/bolsm,bilrm->losir/dot_general | solution.py:58
  862.0 72.9 %all-to-all-done.3 = bf16[12,128,96,2,6]{1,3,0,4,2:T(2,128)(2,1)} async-done(((bf16[12,128,96,2,6]{1,3,0,4,2:T(2,128)(2,1)}), bf16[12,128,96,2,6]{1,3,0,4,2:T(2,128)(2,1)}, u32[]{:S(2)}, u32[]{:S(2)}) %all-to-all-start.3) | async-done | bytes 3538976 | tf_op jit(solution)/shard_map/all_to_all | solution.py:62
  954.9 35.1 %reverse.11 = f32[12,128,6,95]{1,3,2,0:T(8,128)} reverse(f32[12,128,6,95]{1,3,2,0:T(8,128)} %slice.89), dimensions={3} | reverse | bytes 7004160 | tf_op jit(solution)/shard_map/jit(fft)/reverse.1 | solution.py:30
  1010.7 35.2 %reverse.10 = f32[12,128,6,95]{1,3,2,0:T(8,128)} reverse(f32[12,128,6,95]{1,3,2,0:T(8,128)} %slice.88), dimensions={3} | reverse | bytes 7004160 | tf_op jit(solution)/shard_map/jit(fft)/reverse | solution.py:30
  1111.9 23.9 %fusion.6 = f32[12,128,6,64,3]{1,4,3,2,0:T(4,128)S(1)} fusion(f32[12,128,6,64,3]{1,3,4,2,0:T(8,128)} %get-tuple-element.30), kind=kOutput, calls=%fused_computation.11 | convolution fusion | flops 63701036 | bytes 14155776 | tf_op jit(solution)/shard_map/jit(fft)/dot.10 | solution.py:30
  1135.8 20.5 %fusion.4 = f32[12,128,6,64,3]{1,4,3,2,0:T(4,128)} fusion(f32[12,128,6,64,3]{1,3,4,2,0:T(8,128)S(1)} %get-tuple-element.31), kind=kOutput, calls=%fused_computation.9 | convolution fusion | flops 63701036 | bytes 14155776 | tf_op jit(solution)/shard_map/jit(fft)/dot.11 | solution.py:30
  1156.3 29.3 %multiply_bitcast_fusion = f32[12,128,6,3,64]{1,3,4,2,0:T(4,128)S(1)} fusion(f32[12,128,6,64,3]{1,4,3,2,0:T(4,128)} %fusion.4, f32[12,128,6,64,3]{1,4,3,2,0:T(4,128)S(1)} %fusion.6, f32[12,128,6,64,3]{1,3,4,2,0:T(8,128)} %get-tuple-element.29), kind=kOutput, calls=%fused_computation.33 | convolution fusion | flops 72548384 | bytes 28311552 | tf_op jit(solution)/shard_map/jit(fft)/dot.9 | solution.py:30
  1223.8 22.0 %copy.260 = f32[96,128,128,2]{2,3,1,0:T(2,128)} copy(f32[96,128,128,2]{2,1,0,3:T(8,128)} %pad_maximum_fusion.1) | data formatting | bytes 25165824
  (153 shorter events, 450.8 us)
Async XLA Ops:
  7.2 28.4 %copy-start.17 = (f32[64,3]{0,1:T(4,128)}, f32[64,3]{0,1:T(4,128)S(1)}, u32[]{:S(2)}) copy-start(f32[64,3]{0,1:T(4,128)S(1)} %get-tuple-element.59) | copy-start | bytes 2308
  7.2 28.3 %copy-start.19 = (f32[64,3]{0,1:T(4,128)}, f32[64,3]{0,1:T(4,128)S(1)}, u32[]{:S(2)}) copy-start(f32[64,3]{0,1:T(4,128)S(1)} %get-tuple-element.60) | copy-start | bytes 2308
  53.0 24.1 %copy-start.6 = (f32[12,128,6,64,3]{1,3,4,2,0:T(8,128)S(1)}, f32[12,128,6,64,3]{1,3,4,2,0:T(8,128)}, u32[]{:S(2)}) copy-start(f32[12,128,6,64,3]{1,3,4,2,0:T(8,128)} %get-tuple-element.40) | copy-start | bytes 21233668
  53.0 45.1 %slice-start.8 = ((s8[7077888]{0:T(1024)(128)(4,1)}), s8[4194304]{0:T(1024)(128)(4,1)S(1)}, s32[]{:S(2)}) async-start(s8[7077888]{0:T(1024)(128)(4,1)} %bitcast.394), calls=%async_computation.13 | async-start | bytes 8388608
  77.1 21.0 %slice-start.9 = ((s8[7077888]{0:T(1024)(128)(4,1)}), s8[2883584]{0:T(1024)(128)(4,1)S(1)}, s32[]{:S(2)}) async-start(s8[7077888]{0:T(1024)(128)(4,1)} %bitcast.394), calls=%async_computation.14 | async-start | bytes 5767168
  98.1 26.4 %slice-start.10 = ((s8[9437184]{0:T(1024)(128)(4,1)}), s8[1048576]{0:T(1024)(128)(4,1)S(1)}, s32[]{:S(2)}) async-start(s8[9437184]{0:T(1024)(128)(4,1)} %bitcast.396), calls=%async_computation.15 | async-start | bytes 2097152
  98.1 26.4 %slice-start.11 = ((s8[9437184]{0:T(1024)(128)(4,1)}), s8[4194304]{0:T(1024)(128)(4,1)S(1)}, s32[]{:S(2)}) async-start(s8[9437184]{0:T(1024)(128)(4,1)} %bitcast.396), calls=%async_computation.16 | async-start | bytes 8388608
  137.3 89.6 %all-to-all-start = ((bf16[12,128,6,2,96]{1,3,2,0,4:T(2,128)(2,1)}), bf16[12,128,6,2,96]{1,3,2,0,4:T(2,128)(2,1)S(1)}, u32[]{:S(2)}, u32[]{:S(2)}) async-start(bf16[12,128,6,2,96]{1,3,2,0,4:T(2,128)(2,1)} %copy.206), calls=%async_computation | async-start | bytes 7077888 | tf_op jit(solution)/shard_map/all_to_all | solution.py:48
  232.0 13.4 %copy-start.3 = (bf16[12,128,96,2,6,1]{1,2,3,0,4,5:T(8,128)(2,1)}, bf16[12,128,96,2,6,1]{1,2,3,0,4,5:T(8,128)(2,1)S(1)}, u32[]{:S(2)}) copy-start(bf16[12,128,96,2,6,1]{1,2,3,0,4,5:T(8,128)(2,1)S(1)} %convert_bitcast_fusion.3) | copy-start | bytes 10616836
  232.0 13.4 %copy-start.11 = (bf16[6,96,96]{1,2,0:T(8,128)(2,1)S(1)}, bf16[6,96,96]{1,2,0:T(8,128)(2,1)}, u32[]{:S(2)}) copy-start(bf16[6,96,96]{1,2,0:T(8,128)(2,1)} %copy.316) | copy-start | bytes 331780
  254.7 86.5 %all-to-all-start.1 = ((bf16[12,128,96,2,6]{1,3,0,4,2:T(2,128)(2,1)}), bf16[12,128,96,2,6]{1,3,0,4,2:T(2,128)(2,1)S(1)}, u32[]{:S(2)}, u32[]{:S(2)}) async-start(bf16[12,128,96,2,6]{1,3,0,4,2:T(2,128)(2,1)} %copy.216), calls=%async_computation.1 | async-start | bytes 7077888 | tf_op jit(solution)/shard_map/all_to_all | solution.py:52
  263.4 235.5 %copy-start.13 = (f32[64,3]{0,1:T(4,128)}, f32[64,3]{0,1:T(4,128)S(1)}, u32[]{:S(2)}) copy-start(f32[64,3]{0,1:T(4,128)S(1)} %get-tuple-element.61) | copy-start | bytes 2308
  263.4 235.5 %copy-start.15 = (f32[64,3]{0,1:T(4,128)}, f32[64,3]{0,1:T(4,128)S(1)}, u32[]{:S(2)}) copy-start(f32[64,3]{0,1:T(4,128)S(1)} %get-tuple-element.62) | copy-start | bytes 2308
  466.6 12.7 %copy-start.1 = (f32[12,128,6,64,3]{1,4,3,2,0:T(4,128)S(1)}, f32[12,128,6,64,3]{1,4,3,2,0:T(4,128)}, u32[]{:S(2)}) copy-start(f32[12,128,6,64,3]{1,4,3,2,0:T(4,128)} %reshape.95) | copy-start | bytes 21233668
  466.6 23.5 %slice-start = ((s8[9437184]{0:T(1024)(128)(4,1)}), s8[4194304]{0:T(1024)(128)(4,1)S(1)}, s32[]{:S(2)}) async-start(s8[9437184]{0:T(1024)(128)(4,1)} %bitcast.386), calls=%async_computation.5 | async-start | bytes 8388608
  639.3 43.7 %slice-start.6 = ((s8[7077888]{0:T(1024)(128)(4,1)}), s8[4194304]{0:T(1024)(128)(4,1)S(1)}, s32[]{:S(2)}) async-start(s8[7077888]{0:T(1024)(128)(4,1)} %bitcast.392), calls=%async_computation.11 | async-start | bytes 8388608
  658.3 24.7 %slice-start.7 = ((s8[7077888]{0:T(1024)(128)(4,1)}), s8[2883584]{0:T(1024)(128)(4,1)S(1)}, s32[]{:S(2)}) async-start(s8[7077888]{0:T(1024)(128)(4,1)} %bitcast.392), calls=%async_computation.12 | async-start | bytes 5767168
  720.1 92.3 %copy-start.12 = (bf16[6,96,96]{1,2,0:T(8,128)(2,1)S(1)}, bf16[6,96,96]{1,2,0:T(8,128)(2,1)}, u32[]{:S(2)}) copy-start(bf16[6,96,96]{1,2,0:T(8,128)(2,1)} %copy.316) | copy-start | bytes 331780
  813.6 14.2 %copy-start.5 = (bf16[12,128,96,2,6,1]{1,2,3,0,4,5:T(8,128)(2,1)}, bf16[12,128,96,2,6,1]{1,2,3,0,4,5:T(8,128)(2,1)S(1)}, u32[]{:S(2)}) copy-start(bf16[12,128,96,2,6,1]{1,2,3,0,4,5:T(8,128)(2,1)S(1)} %convert_bitcast_fusion.1) | copy-start | bytes 10616836
  839.4 95.5 %all-to-all-start.3 = ((bf16[12,128,96,2,6]{1,3,0,4,2:T(2,128)(2,1)}), bf16[12,128,96,2,6]{1,3,0,4,2:T(2,128)(2,1)}, u32[]{:S(2)}, u32[]{:S(2)}) async-start(bf16[12,128,96,2,6]{1,3,0,4,2:T(2,128)(2,1)} %copy.244), calls=%async_computation.3 | async-start | bytes 7077888 | tf_op jit(solution)/shard_map/all_to_all | solution.py:62
  844.0 355.6 %all-reduce.7.cloned.1.call-start = ((), (), s32[]{:S(2)}) async-start(), calls=%async_computation.4 | async-start | bytes 50331648 | tf_op jit(solution)/shard_map/psum | solution.py:59
  1063.3 13.8 %copy-start.2 = (f32[12,128,6,64,3]{1,4,3,2,0:T(4,128)S(1)}, f32[12,128,6,64,3]{1,4,3,2,0:T(4,128)}, u32[]{:S(2)}) copy-start(f32[12,128,6,64,3]{1,4,3,2,0:T(4,128)} %reshape.101) | copy-start | bytes 21233668
  1063.3 22.7 %slice-start.3 = ((s8[9437184]{0:T(1024)(128)(4,1)}), s8[4194304]{0:T(1024)(128)(4,1)S(1)}, s32[]{:S(2)}) async-start(s8[9437184]{0:T(1024)(128)(4,1)} %bitcast.388), calls=%async_computation.8 | async-start | bytes 8388608
  1063.3 22.7 %slice-start.4 = ((s8[9437184]{0:T(1024)(128)(4,1)}), s8[4194304]{0:T(1024)(128)(4,1)S(1)}, s32[]{:S(2)}) async-start(s8[9437184]{0:T(1024)(128)(4,1)} %bitcast.388), calls=%async_computation.9 | async-start | bytes 8388608
  (16 other events, 120.2 us)
Sparse Core Ops, SparseCore 0:
  862.1 328.6 all-reduce.6
where the time goes:
time: 1280 us; the launch traced here: 1250 us
  matrix products  475 us (37%)
  local copies, waits for them, and re-layouts  338 us (26%)
  waiting for transfers between devices  204 us (16%)
  other arithmetic  107 us (8%)
  blocking collectives  89.3 us (7%)
  starting transfers between devices  24.2 us (2%)
  between operations  15.2 us (1%)
    another operation x12, matrix products, synthesis(): return jnp.fft.irfft(jnp.pad(complex_spec, pad_width), n=lon_count, axis=-1)  221 us
    another operation x14, local copies, waits for them, and re-layouts, synthesis(): return jnp.fft.irfft(jnp.pad(complex_spec, pad_width), n=lon_count, axis=-1)  201 us
    another operation x11, matrix products, analysis(): spectrum = jnp.fft.rfft(values, axis=-1)[..., :mode_count] * mode_gains  195 us
    all_to_all x1, blocking collectives, local_step(): grad_back_own = lax.all_to_all(grad_back_lat, 'lat', 4, 2, tiled=True)  89.3 us
    all_to_all x1, waiting for transfers between devices, local_step(): back_lat = lax.all_to_all(back_own, 'lat', 2, 4, tiled=True)  77.7 us
    all_to_all x1, waiting for transfers between devices, local_step(): grad_four_lat = lax.all_to_all(grad_four_own, 'lat', 2, 4, tiled=True)  72.9 us
    all_to_all x1, waiting for transfers between devices, local_step(): four_own = lax.all_to_all(four_lat, 'lat', 4, 2, tiled=True)  53.3 us
    another operation x7, other arithmetic, synthesis(): return jnp.fft.irfft(jnp.pad(complex_spec, pad_width), n=lon_count, axis=-1)  37 us
  transfers between devices with their start and end apart: 4, of which 3 were waited for; matrix products, arithmetic and copies ran while one was open for 24% of the time, Pallas kernels for 0%

commit v1 on v0

v1 whole, which is shorter than its diff:
```python
import functools
import math

import jax
import jax.numpy as jnp
import numpy as np
from jax import lax
from jax.experimental import pallas as pl
from jax.experimental.pallas import tpu as pltpu
from jax.sharding import PartitionSpec as P

F32 = jnp.float32
BF16 = jnp.bfloat16
SEND_SLOTS = 4


def split_const(matrix):
    head = matrix.astype(BF16)
    tail = (matrix - head.astype(np.float64)).astype(BF16)
    return [head, tail]


def fourier_tables(modes, lons):
    angle = 2.0 * np.pi * (np.outer(np.arange(modes), np.arange(lons)) % lons) / lons
    forward = np.stack([np.cos(angle), -np.sin(angle)], axis=1).reshape(2 * modes, lons) / math.sqrt(lons)
    gains = np.repeat(np.where(np.arange(modes) == 0, 1.0, 2.0), 2)[:, None]
    doubled = forward * gains
    tables = split_const(forward) + split_const(doubled) + split_const(doubled.T) + split_const(forward.T)
    return [jnp.asarray(t) for t in tables]


def gelu_grad(values):
    cumulative = 0.5 * (1.0 + lax.erf(values * math.sqrt(0.5)))
    density = jnp.exp(-0.5 * values * values) / math.sqrt(2.0 * math.pi)
    return cumulative + values * density


def dot(a, b, dims=((1,), (0,))):
    return lax.dot_general(a, b, (dims, ((), ())), preferred_element_type=F32)


def layer_kernel(
    axis, n, nb,
    f_hbm, dg_hbm, w_hbm, pw_ref, pi_ref, pwt_ref, pit_ref,
    fwd_h, fwd_l, dbl_h, dbl_l, syn_h, syn_l, adj_h, adj_l,
    df_hbm, dw_hbm,
    recv, send, t1, t2, xb, coef, dq, vmix, wbuf, inbuf, outbuf, gather, dwbuf,
    send_sem, recv_sem, in_sem, out_sem, w_sem,
):
    me = lax.axis_index(axis)
    batch, tl, lons, chans = f_hbm.shape
    ml, degs, lats = pw_ref.shape
    chunks = batch // nb
    tile = 2 * nb
    rows = ml * tile
    pitch = rows + 1
    modes2 = 2 * n * ml
    units = chunks * tl

    barrier = pltpu.get_barrier_semaphore()

    def announce(k, _):
        pl.semaphore_signal(barrier, inc=1, device_id={axis: lax.rem(me + k, n)}, device_id_type=pl.DeviceIdType.MESH)
        return 0

    lax.fori_loop(1, n, announce, 0)

    def unit_in(src, unit):
        ch, t = lax.div(unit, tl), lax.rem(unit, tl)
        slot = lax.rem(unit, 2)
        return pltpu.make_async_copy(src.at[pl.ds(ch * nb, nb), t], inbuf.at[slot], in_sem.at[slot])

    def unit_out(unit):
        ch, t = lax.div(unit, tl), lax.rem(unit, tl)
        slot = lax.rem(unit, 2)
        return pltpu.make_async_copy(outbuf.at[slot], df_hbm.at[pl.ds(ch * nb, nb), t], out_sem.at[slot])

    def step_in(src, unit):
        @pl.when(unit + 1 < units)
        def _():
            unit_in(src, unit + 1).start()
        unit_in(src, unit).wait()

    def ship(stage, ch):
        index = stage * chunks + ch
        slot = lax.rem(index, SEND_SLOTS)

        def one(k, _):
            peer = lax.rem(me + k, n)
            pltpu.make_async_remote_copy(
                src_ref=send.at[slot, peer], dst_ref=recv.at[stage, ch, me],
                send_sem=send_sem.at[index], recv_sem=recv_sem.at[index],
                device_id={axis: peer}, device_id_type=pl.DeviceIdType.MESH,
            ).start()
            return 0

        lax.fori_loop(1, n, one, 0)
        recv[stage, ch, me] = send[slot, me]

    def arrived(stage, ch):
        others = recv.at[stage, ch, pl.ds(0, n - 1)]
        pltpu.make_async_copy(others, others, recv_sem.at[stage * chunks + ch]).wait()

    def wait_sent(index):
        others = send.at[lax.rem(index, SEND_SLOTS), pl.ds(0, n - 1)]
        pltpu.make_async_copy(others, others, send_sem.at[index]).wait()

    def free_slot(stage, ch):
        index = stage * chunks + ch

        @pl.when(index >= SEND_SLOTS)
        def _():
            wait_sent(index - SEND_SLOTS)

        return lax.rem(index, SEND_SLOTS)

    def put_rows(slot, t):
        send[slot, :, t] = gather[...].reshape(n, rows, chans).astype(BF16)

    def transform(values, head, tail):
        high = values.astype(BF16)
        low = (values - high.astype(F32)).astype(BF16)
        return dot(head[...], high) + (dot(tail[...], high) + dot(head[...], low))

    unit_in(f_hbm, 0).start()

    def step1_chunk(ch, _):
        slot = free_slot(0, ch)

        def row(t, _):
            unit = ch * tl + t
            step_in(f_hbm, unit)
            buf = lax.rem(unit, 2)
            for b in range(0, nb, 2):
                pair = jnp.concatenate([inbuf[buf, b], inbuf[buf, b + 1]], axis=1)
                spec = transform(pair, fwd_h, fwd_l)
                gather[pl.ds(b, modes2, stride=nb), :] = spec[:, :chans]
                gather[pl.ds(b + 1, modes2, stride=nb), :] = spec[:, chans:]
            put_rows(slot, t)
            return 0

        lax.fori_loop(0, tl, row, 0)

        @pl.when(ch == 0)
        def _():
            pl.semaphore_wait(barrier, n - 1)

        ship(0, ch)
        return 0

    lax.fori_loop(0, chunks, step1_chunk, 0)
    unit_in(dg_hbm, 0).start()

    per = wbuf.shape[1] // (2 * chans)
    parts = degs // per

    def w_in(k):
        slot = lax.rem(k, 2)
        return pltpu.make_async_copy(w_hbm.at[pl.ds(k * per * 2 * chans, per * 2 * chans)], wbuf.at[slot], w_sem.at[slot])

    w_in(0).start()

    def load_w(k, _):
        @pl.when(k + 1 < parts)
        def _():
            w_in(k + 1).start()
        w_in(k).wait()
        slot = lax.rem(k, 2)
        for j in range(per):
            for part in range(2):
                vmix[k * per + j, pl.ds(part * chans, chans)] = wbuf[
                    slot, pl.ds(j * 2 * chans + part, chans, stride=2), :].astype(BF16)
        return 0

    lax.fori_loop(0, parts, load_w, 0)

    sign = jnp.where(lax.broadcasted_iota(jnp.int32, (tile, chans), 0) < nb, -1.0, 1.0).astype(F32)

    def turn(values):
        groups = values.reshape(ml, tile, chans)
        return (pltpu.roll(groups, nb, 1) * sign[None]).reshape(rows, chans)

    def legendre(src, dst, mats):
        def mode(m, _):
            for k in range(tile):
                xb[:, k * chans:(k + 1) * chans] = src[pl.ds(m * tile + k, lats, stride=pitch), :].astype(BF16)
            out = dot(mats[m], xb[...])
            for k in range(tile):
                dst[pl.ds(m * tile + k, degs, stride=pitch), :] = out[:, k * chans:(k + 1) * chans]
            return 0

        lax.fori_loop(0, ml, mode, 0)

    def unload(stage, ch):
        def body(src, _):
            for t in range(tl):
                t1[pl.ds((src * tl + t) * pitch, rows), :] = recv[stage, ch, src, t].astype(F32)
            return 0

        lax.fori_loop(0, n, body, 0)

    def load(slot):
        def body(dev, _):
            for t in range(tl):
                send[slot, dev, t] = t2[pl.ds((dev * tl + t) * pitch, rows), :].astype(BF16)
            return 0

        lax.fori_loop(0, n, body, 0)

    def spectral(stage, ch, into, outof, kept, mix):
        arrived(stage - 1, ch)
        unload(stage - 1, ch)
        legendre(t1, t2, into)

        def degree(l, _):
            x = t2[pl.ds(l * pitch, rows), :].astype(BF16)
            kept[l, ch] = x
            t1[pl.ds(l * pitch, rows), :] = mix(l, x)
            return 0

        lax.fori_loop(0, degs, degree, 0, unroll=2)
        legendre(t1, t2, outof)
        load(free_slot(stage, ch))
        ship(stage, ch)

    def mix_forward(l, x):
        both = dot(x, vmix[l], ((1,), (1,)))
        return both[:, :chans] + turn(both[:, chans:])

    def mix_adjoint(l, x):
        real = dot(x, vmix[l, pl.ds(0, chans)])
        imag = dot(x, vmix[l, pl.ds(chans, chans)])
        return real - turn(imag)

    def step2_chunk(ch, _):
        spectral(1, ch, pw_ref, pit_ref, coef, mix_forward)
        return 0

    lax.fori_loop(0, chunks, step2_chunk, 0)

    def fetch_rows(stage, ch, t):
        for src in range(n):
            gather[pl.ds(src * rows, rows), :] = recv[stage, ch, src, t].astype(F32)

    def fetch_pair(b):
        return jnp.concatenate(
            [gather[pl.ds(b, modes2, stride=nb), :], gather[pl.ds(b + 1, modes2, stride=nb), :]], axis=1).astype(BF16)

    def step3_chunk(ch, _):
        slot = free_slot(2, ch)
        arrived(1, ch)

        def row(t, _):
            unit = ch * tl + t
            step_in(dg_hbm, unit)
            buf = lax.rem(unit, 2)
            fetch_rows(1, ch, t)
            for b in range(0, nb, 2):
                g = fetch_pair(b)
                hidden = dot(syn_h[...], g) + dot(syn_l[...], g)
                pair = jnp.concatenate([inbuf[buf, b], inbuf[buf, b + 1]], axis=1)
                spec = transform(pair * gelu_grad(hidden), dbl_h, dbl_l)
                gather[pl.ds(b, modes2, stride=nb), :] = spec[:, :chans]
                gather[pl.ds(b + 1, modes2, stride=nb), :] = spec[:, chans:]
            put_rows(slot, t)
            return 0

        lax.fori_loop(0, tl, row, 0)
        ship(2, ch)
        return 0

    lax.fori_loop(0, chunks, step3_chunk, 0)
    unit_in(dg_hbm, 0).start()

    def step4_chunk(ch, _):
        spectral(3, ch, pi_ref, pwt_ref, dq, mix_adjoint)
        return 0

    lax.fori_loop(0, chunks, step4_chunk, 0)

    def dw_out(l):
        slot = lax.rem(l, 2)
        return pltpu.make_async_copy(dwbuf.at[slot], dw_hbm.at[pl.ds(l * 2 * chans, 2 * chans)], w_sem.at[slot])

    def weight_grad(l, _):
        @pl.when(l >= 2)
        def _():
            dw_out(l - 2).wait()
        slot = lax.rem(l, 2)
        real = jnp.zeros((chans, chans), F32)
        imag = jnp.zeros((chans, chans), F32)
        for ch in range(chunks):
            y = dq[l, ch]
            x = coef[l, ch]
            real += dot(y, x, ((0,), (0,)))
            imag -= dot(turn(y.astype(F32)).astype(BF16), x, ((0,), (0,)))
        dwbuf[slot, pl.ds(0, chans, stride=2), :] = real
        dwbuf[slot, pl.ds(1, chans, stride=2), :] = imag
        dw_out(l).start()
        return 0

    lax.fori_loop(0, degs, weight_grad, 0)
    dw_out(degs - 2).wait()
    dw_out(degs - 1).wait()

    def step5_chunk(ch, _):
        arrived(3, ch)

        def row(t, _):
            unit = ch * tl + t
            step_in(dg_hbm, unit)
            buf = lax.rem(unit, 2)

            @pl.when(unit >= 2)
            def _():
                unit_out(unit - 2).wait()

            fetch_rows(3, ch, t)
            for b in range(0, nb, 2):
                g = fetch_pair(b)
                change = dot(adj_h[...], g) + dot(adj_l[...], g)
                outbuf[buf, b] = inbuf[buf, b] + change[:, :chans]
                outbuf[buf, b + 1] = inbuf[buf, b + 1] + change[:, chans:]
            unit_out(unit).start()
            return 0

        lax.fori_loop(0, tl, row, 0)
        return 0

    lax.fori_loop(0, chunks, step5_chunk, 0)
    unit_out(units - 2).wait()
    unit_out(units - 1).wait()
    for index in range(4 * chunks - SEND_SLOTS, 4 * chunks):
        wait_sent(index)


def solution(mesh):
    n = mesh.shape['lat']
    field_spec = P('member', None, 'lat', None)

    def local_step(field_loc, grad_loc, p_fwd, p_inv, w_mix):
        batch, chans, tl, lons = field_loc.shape
        degs, lats = p_fwd.shape[1:]
        ml = p_fwd.shape[0] // n
        nb = 4
        chunks = batch // nb
        rows = ml * 2 * nb
        pitch = rows + 1
        m_start = lax.axis_index('lat') * ml
        pw = lax.dynamic_slice_in_dim(p_fwd, m_start, ml, axis=0).astype(BF16)
        pi = lax.dynamic_slice_in_dim(p_inv, m_start, ml, axis=0).astype(BF16)
        tables = fourier_tables(n * ml, lons)
        anywhere = pl.BlockSpec(memory_space=pl.ANY)
        vmem = pl.BlockSpec(memory_space=pltpu.VMEM)
        grad_field, grad_w = pl.pallas_call(
            functools.partial(layer_kernel, 'lat', n, nb),
            name='layer',
            out_shape=(
                jax.ShapeDtypeStruct((batch, tl, lons, chans), F32),
                jax.ShapeDtypeStruct((degs * 2 * chans, chans), F32),
            ),
            in_specs=[anywhere] * 3 + [vmem] * (4 + len(tables)),
            out_specs=(anywhere, anywhere),
            scratch_shapes=[
                pltpu.VMEM((4, chunks, n, tl, rows, chans), BF16),
                pltpu.VMEM((SEND_SLOTS, n, tl, rows, chans), BF16),
                pltpu.VMEM((lats * pitch, chans), F32),
                pltpu.VMEM((lats * pitch, chans), F32),
                pltpu.VMEM((lats, 2 * nb * chans), BF16),
                pltpu.VMEM((degs, chunks, rows, chans), BF16),
                pltpu.VMEM((degs, chunks, rows, chans), BF16),
                pltpu.VMEM((degs, 2 * chans, chans), BF16),
                pltpu.VMEM((2, 8 * 2 * chans, chans), F32),
                pltpu.VMEM((2, nb, lons, chans), F32),
                pltpu.VMEM((2, nb, lons, chans), F32),
                pltpu.VMEM((n * rows, chans), F32),
                pltpu.VMEM((2, 2 * chans, chans), F32),
                pltpu.SemaphoreType.DMA((4 * chunks,)),
                pltpu.SemaphoreType.DMA((4 * chunks,)),
                pltpu.SemaphoreType.DMA((2,)),
                pltpu.SemaphoreType.DMA((2,)),
                pltpu.SemaphoreType.DMA((2,)),
            ],
            compiler_params=pltpu.CompilerParams(
                collective_id=0, has_side_effects=True, vmem_limit_bytes=60 * 1024 * 1024),
        )(
            field_loc.transpose(0, 2, 3, 1), grad_loc.transpose(0, 2, 3, 1),
            w_mix.transpose(0, 1, 3, 2).reshape(degs * 2 * chans, chans),
            pw, pi, pw.transpose(0, 2, 1), pi.transpose(0, 2, 1), *tables)
        total = lax.psum(grad_w, 'lat')
        return grad_field.transpose(0, 3, 1, 2), total.reshape(degs, chans, 2, chans).transpose(0, 1, 3, 2)

    return jax.shard_map(
        local_step, mesh=mesh, in_specs=(field_spec, field_spec, P(), P(), P()),
        out_specs=(field_spec, P('member', None, None, None)), check_vma=False)
```

time: 1280 us -> 509 us (0.40); the launches traced: 1250 us -> 508 us
  matrix products: 475 us -> 0 us
  Pallas kernels: 0 us -> 331 us
  local copies, waits for them, and re-layouts: 338 us -> 16.9 us
  other arithmetic: 107 us -> 0 us
  blocking collectives: 89.3 us -> 0 us
  waiting for transfers between devices: 204 us -> 146 us
  starting transfers between devices: 24.2 us -> 0.06 us
    another operation x23 -> x0, matrix products: 415 us -> none  [the longest x12 221 us: synthesis(): return jnp.fft.irfft(jnp.pad(complex_spec, pad_width), n=lon_count, axis=-1)]
    pallas_call x0 -> x1, Pallas kernels: none -> 331 us  [local_step(): pl.pallas_call(functools.partial(layer_kernel, 'lat', n, nb), name='layer...]
    another operation x20 -> x0, local copies, waits for them, and re-layouts: 228 us -> none  [the longest x14 201 us: synthesis(): return jnp.fft.irfft(jnp.pad(complex_spec, pad_width), n=lon_count, axis=-1)]
    all_to_all x3 -> x0, waiting for transfers between devices: 204 us -> none  [the longest x1 77.7 us: local_step(): back_lat = lax.all_to_all(back_own, 'lat', 2, 4, tiled=True)]
    psum x1, waiting for transfers between devices: 0.01 us -> 146 us  [local_step(): total = lax.psum(grad_w, 'lat')]
    all_to_all x1 -> x0, blocking collectives: 89.3 us -> none  [local_step(): grad_back_own = lax.all_to_all(grad_back_lat, 'lat', 4, 2, tiled=True)]
    dot_general x7 -> x0, matrix products: 60.1 us -> none  [the longest x1 17.6 us: local_step(): jnp.einsum('bolsm,bilrm->losir', grad_mixed, coeffs, preferred_element_ty...]
    another operation x17 -> x0, other arithmetic: 59.7 us -> none  [the longest x7 37 us: synthesis(): return jnp.fft.irfft(jnp.pad(complex_spec, pad_width), n=lon_count, axis=-1)]
  transfers between devices with their start and end apart: 4 -> 1, of which waited for: 3 -> 1; matrix products, arithmetic and copies ran while one was open for 24% -> 0% of each run, Pallas kernels for 0% -> 0%
where the time goes in v1:
time: 509 us; the launch traced here: 508 us
  Pallas kernels  331 us (65%)
  waiting for transfers between devices  146 us (29%)
  local copies, waits for them, and re-layouts  16.9 us (3%)
  between operations  14.1 us (3%)
    pallas_call x1, Pallas kernels, local_step(): pl.pallas_call(functools.partial(layer_kernel, 'lat', n, nb), name='layer...  331 us
    psum x1, waiting for transfers between devices, local_step(): total = lax.psum(grad_w, 'lat')  146 us
    unnamed x10, local copies, waits for them, and re-layouts  14.2 us
  transfers between devices with their start and end apart: 1, of which 1 were waited for; matrix products, arithmetic and copies ran while one was open for 0% of the time, Pallas kernels for 0%

profile of v1, /device:TPU:21, one launch (start us, length us, event | category | flops | bytes accessed | tf_op | source)
XLA Modules:
  0.0 508.0 jit_solution(4301689570933099595)
XLA Ops:
  7.2 0.1 all-reduce.2.cloned.1.call-start
  7.2 1.1 constant_dynamic-slice_fusion
  8.3 0.2 copy.20
  8.5 0.0 copy-start.1
  8.5 0.2 copy.19
  8.7 0.0 copy-start.2
  8.7 0.8 copy.17.pw_ref
  9.5 0.8 copy.18.pi_ref
  10.3 0.0 copy-done.1
  10.3 0.0 copy-done.2
  10.3 331.2 %layer.1 = (f32[12,6,192,128]{3,2,1,0:T(8,128)}, f32[24576,128]{1,0:T(8,128)}) custom-call(f32[12,6,192,128]{3,2,1,0:T(8,128)} %bitcast.14, f32[12,6,192,128]{3,2,1,0:T(8,128)} %bitcast.15, f32[24576,128]{1,0:T(8,128)} %bitcast.11, bf16[6,96,96]{2,1,0:T(8,128)(2,1)} %copy.17.pw_ref, bf16[6,96,96]{2,1,0:T(8,128)(2,1)} %copy.18.pi_ref, ...), custom_call_target="tpu_custom_call" | custom-call | tf_op jit(solution)/shard_map/layer/pallas_call | solution.py:355
  341.5 0.1 all-reduce.2.cloned.1.call-update
  341.5 145.7 %all-reduce.2.cloned.1.call-done = f32[96,128,128,2]{2,3,1,0:T(2,128)} async-done(((f32[96,128,128,2]{2,3,1,0:T(2,128)}), f32[96,128,128,2]{2,3,1,0:T(2,128)}) %all-reduce.2.cloned.1.call-update) | async-done | bytes 12582928 | tf_op jit(solution)/shard_map/psum | solution.py:390
  487.2 0.0 copy-start
  487.2 7.6 %copy.24 = f32[12,128,6,192]{1,3,2,0:T(8,128)} copy(f32[12,128,6,192]{1,3,2,0:T(8,128)} %bitcast.13) | data formatting | bytes 14155776
  494.8 1.5 copy-done
  496.4 4.8 copy.25
Async XLA Ops:
  7.2 480.0 %all-reduce.2.cloned.1.call-start = ((), (), s32[]{:S(2)}) async-start(), calls=%async_computation | async-start | bytes 25165824 | tf_op jit(solution)/shard_map/psum | solution.py:390
  8.5 1.8 copy-start.1
  8.7 1.6 copy-start.2
  487.2 9.1 %copy-start = (f32[96,128,128,2]{2,3,1,0:T(2,128)S(1)}, f32[96,128,128,2]{2,3,1,0:T(2,128)}, u32[]{:S(2)}) copy-start(f32[96,128,128,2]{2,3,1,0:T(2,128)} %all-reduce.2.cloned.1.call-done) | copy-start | bytes 37748740
Sparse Core Ops, SparseCore 0:
  341.7 145.5 all-reduce.1

commit v2 on v1

v2 whole, which is shorter than its diff:
```python
import functools
import math

import jax
import jax.numpy as jnp
import numpy as np
from jax import lax
from jax.experimental import pallas as pl
from jax.experimental.pallas import tpu as pltpu
from jax.sharding import PartitionSpec as P

F32 = jnp.float32
BF16 = jnp.bfloat16
SEND_SLOTS = 4


def split_const(matrix):
    head = matrix.astype(BF16)
    tail = (matrix - head.astype(np.float64)).astype(BF16)
    return [head, tail]


def fourier_tables(n, ml, lons):
    modes = n * ml
    order = np.arange(modes).reshape(ml, n).T.reshape(-1)
    angle = 2.0 * np.pi * (np.outer(order, np.arange(lons)) % lons) / lons
    forward = np.stack([np.cos(angle), -np.sin(angle)], axis=1).reshape(2 * modes, lons) / math.sqrt(lons)
    gains = np.repeat(np.where(order == 0, 1.0, 2.0), 2)[:, None]
    doubled = forward * gains
    tables = split_const(forward) + split_const(doubled) + split_const(doubled.T) + split_const(forward.T)
    return [jnp.asarray(t) for t in tables]


def gelu_grad(values):
    cumulative = 0.5 * (1.0 + lax.erf(values * math.sqrt(0.5)))
    density = jnp.exp(-0.5 * values * values) / math.sqrt(2.0 * math.pi)
    return cumulative + values * density


def dot(a, b, dims=((1,), (0,))):
    return lax.dot_general(a, b, (dims, ((), ())), preferred_element_type=F32)


def layer_kernel(
    axis, n, nb, pieces,
    f_hbm, dg_hbm, w_hbm, pf_hbm, pv_hbm,
    fwd_h, fwd_l, dbl_h, dbl_l, syn_h, syn_l, adj_h, adj_l,
    df_hbm, dw_hbm,
    recv, send, t1, t2, xb, coef, dq, vmix, wbuf, inbuf, outbuf, gather, pbuf, pmat, mine, theirs, ring,
    send_sem, recv_sem, in_sem, out_sem, w_sem, p_sem, pair_send, pair_recv, rs_send, rs_recv, ag_send, ag_recv, dw_sem,
):
    me = lax.axis_index(axis)
    batch, tl, lons, chans = f_hbm.shape
    ml, degs, lats = pmat.shape[1:]
    chunks = batch // nb
    tile = 2 * nb
    rows = ml * tile
    pitch = rows + 1
    modes2 = 2 * n * ml
    units = chunks * tl

    barrier = pltpu.get_barrier_semaphore()

    def announce(k, _):
        pl.semaphore_signal(barrier, inc=1, device_id={axis: lax.rem(me + k, n)}, device_id_type=pl.DeviceIdType.MESH)
        return 0

    lax.fori_loop(1, n, announce, 0)

    def unit_of(unit):
        return lax.div(unit, tl), lax.rem(unit, tl)

    def unit_in(src, unit):
        ch, t = unit_of(unit)
        slot = lax.rem(unit, 2)
        return pltpu.make_async_copy(src.at[pl.ds(ch * nb, nb), t], inbuf.at[slot], in_sem.at[slot])

    def unit_out(unit):
        ch, t = unit_of(unit)
        slot = lax.rem(unit, 2)
        return pltpu.make_async_copy(outbuf.at[slot], df_hbm.at[pl.ds(ch * nb, nb), t], out_sem.at[slot])

    def step_in(src, unit):
        @pl.when(unit + 1 < units)
        def _():
            unit_in(src, unit + 1).start()
        unit_in(src, unit).wait()

    def ship(stage, ch, t0, nt):
        index = stage * chunks + ch
        slot = lax.rem(index, SEND_SLOTS)
        part = pl.ds(t0, nt)

        def one(k, _):
            peer = lax.rem(me + k, n)
            pltpu.make_async_remote_copy(
                src_ref=send.at[slot, peer, part], dst_ref=recv.at[stage % 2, ch, me, part],
                send_sem=send_sem.at[index], recv_sem=recv_sem.at[index],
                device_id={axis: peer}, device_id_type=pl.DeviceIdType.MESH,
            ).start()
            return 0

        lax.fori_loop(1, n, one, 0)
        recv[stage % 2, ch, me, part] = send[slot, me, part]

    def arrived(stage, ch):
        others = recv.at[stage % 2, ch, pl.ds(0, n - 1)]
        pltpu.make_async_copy(others, others, recv_sem.at[stage * chunks + ch]).wait()

    def wait_sent(index):
        others = send.at[lax.rem(index, SEND_SLOTS), pl.ds(0, n - 1)]
        pltpu.make_async_copy(others, others, send_sem.at[index]).wait()

    def free_slot(stage, ch):
        index = stage * chunks + ch

        @pl.when(index >= SEND_SLOTS)
        def _():
            wait_sent(index - SEND_SLOTS)

        return lax.rem(index, SEND_SLOTS)

    def put_rows(slot, t):
        send[slot, :, t] = gather[...].reshape(n, rows, chans).astype(BF16)

    def transform(values, head, tail):
        high = values.astype(BF16)
        low = (values - high.astype(F32)).astype(BF16)
        return dot(head[...], high) + (dot(tail[...], high) + dot(head[...], low))

    unit_in(f_hbm, 0).start()
    for which, source in enumerate((pf_hbm, pv_hbm)):
        for k in range(ml):
            pltpu.make_async_copy(source.at[me + n * k], pbuf.at[which, k], p_sem.at[which]).start()

    group = 2 if tl % 2 == 0 else 1

    def by_rows(stage, ch, row):
        slot = free_slot(stage, ch)

        def part(p, _):
            def one(j, _):
                row(slot, p * group + j)
                return 0

            lax.fori_loop(0, group, one, 0)
            if stage == 0:
                @pl.when(ch + p == 0)
                def _():
                    pl.semaphore_wait(barrier, n - 1)
            ship(stage, ch, p * group, group)
            return 0

        lax.fori_loop(0, tl // group, part, 0)

    def step1_chunk(ch, _):
        def row(slot, t):
            unit = ch * tl + t
            step_in(f_hbm, unit)
            buf = lax.rem(unit, 2)
            for b in range(0, nb, 2):
                pair = jnp.concatenate([inbuf[buf, b], inbuf[buf, b + 1]], axis=1)
                spec = transform(pair, fwd_h, fwd_l)
                gather[pl.ds(b, modes2, stride=nb), :] = spec[:, :chans]
                gather[pl.ds(b + 1, modes2, stride=nb), :] = spec[:, chans:]
            put_rows(slot, t)

        by_rows(0, ch, row)
        return 0

    lax.fori_loop(0, chunks, step1_chunk, 0)
    unit_in(dg_hbm, 0).start()
    for which in range(2):
        pltpu.make_async_copy(pbuf.at[which], pbuf.at[which], p_sem.at[which]).wait()
    pmat[...] = pbuf[...].astype(BF16)

    per = wbuf.shape[1] // (2 * chans)
    parts = degs // per

    def w_in(k):
        slot = lax.rem(k, 2)
        return pltpu.make_async_copy(w_hbm.at[pl.ds(k * per * 2 * chans, per * 2 * chans)], wbuf.at[slot], w_sem.at[slot])

    w_in(0).start()

    def load_w(k, _):
        @pl.when(k + 1 < parts)
        def _():
            w_in(k + 1).start()
        w_in(k).wait()
        slot = lax.rem(k, 2)
        for j in range(per):
            for part in range(2):
                vmix[k * per + j, pl.ds(part * chans, chans)] = wbuf[
                    slot, pl.ds(j * 2 * chans + part, chans, stride=2), :].astype(BF16)
        return 0

    lax.fori_loop(0, parts, load_w, 0)

    sign = jnp.where(lax.broadcasted_iota(jnp.int32, (tile, chans), 0) < nb, -1.0, 1.0).astype(F32)

    def turn(values):
        groups = values.reshape(ml, tile, chans)
        return (pltpu.roll(groups, nb, 1) * sign[None]).reshape(rows, chans)

    def legendre(src, dst, which, over):
        def mode(m, _):
            for k in range(tile):
                xb[:, k * chans:(k + 1) * chans] = src[pl.ds(m * tile + k, lats, stride=pitch), :].astype(BF16)
            out = dot(pmat[which, m], xb[...], ((over,), (0,)))
            for k in range(tile):
                dst[pl.ds(m * tile + k, degs, stride=pitch), :] = out[:, k * chans:(k + 1) * chans]
            return 0

        lax.fori_loop(0, ml, mode, 0)

    def unload(stage, ch):
        def body(src, _):
            for t in range(tl):
                t1[pl.ds((src * tl + t) * pitch, rows), :] = recv[stage % 2, ch, src, t].astype(F32)
            return 0

        lax.fori_loop(0, n, body, 0)

    def load(slot):
        def body(dev, _):
            for t in range(tl):
                send[slot, dev, t] = t2[pl.ds((dev * tl + t) * pitch, rows), :].astype(BF16)
            return 0

        lax.fori_loop(0, n, body, 0)

    def spectral(stage, ch, into, kept, mix):
        arrived(stage - 1, ch)
        unload(stage - 1, ch)
        legendre(t1, t2, into, 1)

        def degree(l, _):
            x = t2[pl.ds(l * pitch, rows), :].astype(BF16)
            kept[l, ch] = x
            t1[pl.ds(l * pitch, rows), :] = mix(l, x)
            return 0

        lax.fori_loop(0, degs, degree, 0, unroll=2)
        legendre(t1, t2, 1 - into, 0)
        load(free_slot(stage, ch))
        ship(stage, ch, 0, tl)

    def mix_forward(l, x):
        both = dot(x, vmix[l], ((1,), (1,)))
        return both[:, :chans] + turn(both[:, chans:])

    def mix_adjoint(l, x):
        real = dot(x, vmix[l, pl.ds(0, chans)])
        imag = dot(x, vmix[l, pl.ds(chans, chans)])
        return real - turn(imag)

    def step2_chunk(ch, _):
        spectral(1, ch, 0, coef, mix_forward)
        return 0

    lax.fori_loop(0, chunks, step2_chunk, 0)

    def fetch_rows(stage, ch, t):
        for src in range(n):
            gather[pl.ds(src * rows, rows), :] = recv[stage % 2, ch, src, t].astype(F32)

    def fetch_pair(b):
        return jnp.concatenate(
            [gather[pl.ds(b, modes2, stride=nb), :], gather[pl.ds(b + 1, modes2, stride=nb), :]], axis=1).astype(BF16)

    def step3_chunk(ch, _):
        arrived(1, ch)

        def row(slot, t):
            unit = ch * tl + t
            step_in(dg_hbm, unit)
            buf = lax.rem(unit, 2)
            fetch_rows(1, ch, t)
            for b in range(0, nb, 2):
                g = fetch_pair(b)
                hidden = dot(syn_h[...], g) + dot(syn_l[...], g)
                pair = jnp.concatenate([inbuf[buf, b], inbuf[buf, b + 1]], axis=1)
                spec = transform(pair * gelu_grad(hidden), dbl_h, dbl_l)
                gather[pl.ds(b, modes2, stride=nb), :] = spec[:, :chans]
                gather[pl.ds(b + 1, modes2, stride=nb), :] = spec[:, chans:]
            put_rows(slot, t)

        by_rows(2, ch, row)
        return 0

    lax.fori_loop(0, chunks, step3_chunk, 0)
    unit_in(dg_hbm, 0).start()

    def step4_chunk(ch, _):
        spectral(3, ch, 1, dq, mix_adjoint)
        return 0

    lax.fori_loop(0, chunks, step4_chunk, 0)

    chip, core = lax.div(me, 2), lax.rem(me, 2)
    chips = n // 2
    way = 1 - 2 * core
    sibling = me + way
    onward = 2 * lax.rem(chip + way + chips, chips) + core
    half = degs // n
    piece = half // pieces * 2 * chans
    wide = 2 * chans

    def block_at(k, direction):
        return lax.rem(chip - direction * (1 + k) + 2 * chips, chips)

    def to(device, src, dst, sent, got):
        return pltpu.make_async_remote_copy(
            src_ref=src, dst_ref=dst, send_sem=sent, recv_sem=got,
            device_id={axis: device}, device_id_type=pl.DeviceIdType.MESH)

    def weight_grad(dst, degree, count):
        def one(j, _):
            real = jnp.zeros((chans, chans), F32)
            imag = jnp.zeros((chans, chans), F32)
            for ch in range(chunks):
                y = dq[degree + j, ch]
                x = coef[degree + j, ch]
                real += dot(y, x, ((0,), (0,)))
                imag -= dot(turn(y.astype(F32)).astype(BF16), x, ((0,), (0,)))
            dst[pl.ds(j * wide, chans, stride=2), :] = real
            dst[pl.ds(j * wide + 1, chans, stride=2), :] = imag
            return 0

        lax.fori_loop(0, count, one, 0)

    def pair_copy(k):
        slot = lax.rem(k, 2)
        return to(sibling, wbuf.at[slot, pl.ds(0, half * wide)], theirs.at[block_at(k, -way)],
                  pair_send.at[slot], pair_recv.at[k])

    def weight_block(k, _):
        @pl.when(k >= 2)
        def _():
            pair_copy(k - 2).wait_send()
        weight_grad(wbuf.at[lax.rem(k, 2)], (2 * block_at(k, -way) + 1 - core) * half, half)
        pair_copy(k).start()
        block = block_at(k, way)
        weight_grad(mine.at[block], (2 * block + core) * half, half)
        return 0

    lax.fori_loop(0, chips, weight_block, 0)
    pair_copy(chips - 2).wait_send()
    pair_copy(chips - 1).wait_send()

    def final_rows(unit):
        ch, t = unit_of(unit)

        @pl.when(t == 0)
        def _():
            arrived(3, ch)

        step_in(dg_hbm, unit)
        buf = lax.rem(unit, 2)

        @pl.when(unit >= 2)
        def _():
            unit_out(unit - 2).wait()

        fetch_rows(3, ch, t)
        for b in range(0, nb, 2):
            g = fetch_pair(b)
            change = dot(adj_h[...], g) + dot(adj_l[...], g)
            outbuf[buf, b] = inbuf[buf, b] + change[:, :chans]
            outbuf[buf, b + 1] = inbuf[buf, b + 1] + change[:, chans:]
        unit_out(unit).start()

    hops = (chips - 1) * pieces

    def add_up(i):
        k, part = lax.div(i, pieces), pl.ds(lax.rem(i, pieces) * piece, piece)
        block = block_at(k, way)

        @pl.when(lax.rem(i, pieces) == 0)
        def _():
            pair_copy(k).wait_recv()

        mine[block, part] += theirs[block, part]

        @pl.when(k > 0)
        def _():
            rs_copy(i - pieces).wait_recv()
            mine[block, part] += ring[block, part]

        return block, part

    def rs_copy(i):
        k, part = lax.div(i, pieces), pl.ds(lax.rem(i, pieces) * piece, piece)
        block = block_at(k, way)
        return to(onward, mine.at[block, part], ring.at[block, part], rs_send, rs_recv.at[i])

    def rs_step(i, _):
        add_up(i)
        rs_copy(i).start()

        @pl.when(i < units)
        def _():
            final_rows(i)

        return 0

    lax.fori_loop(0, hops, rs_step, 0)

    def publish(source, block, i):
        rows_out = pl.ds(((2 * block + core) * half) * wide + lax.rem(i, pieces) * piece, piece)
        pltpu.make_async_copy(source, dw_hbm.at[rows_out], dw_sem.at[0]).start()
        to(sibling, source, dw_hbm.at[rows_out], dw_sem.at[1], dw_sem.at[2]).start()

    def own_piece(s, _):
        block, part = add_up(hops + s)
        to(onward, mine.at[block, part], ring.at[block, part], ag_send, ag_recv.at[s]).start()
        publish(mine.at[block, part], block, s)
        return 0

    lax.fori_loop(0, pieces, own_piece, 0)

    def ag_step(i, _):
        part = pl.ds(lax.rem(i, pieces) * piece, piece)
        block = block_at(lax.div(i, pieces), way)
        held = ring.at[block, part]
        to(onward, held, held, ag_send, ag_recv.at[i]).wait_recv()

        @pl.when(i + pieces < hops)
        def _():
            to(onward, held, held, ag_send, ag_recv.at[i + pieces]).start()

        publish(held, block, i)
        return 0

    lax.fori_loop(0, hops, ag_step, 0)

    def rest(unit, _):
        final_rows(unit)
        return 0

    lax.fori_loop(min(hops, units), units, rest, 0)

    unit_out(units - 2).wait()
    unit_out(units - 1).wait()
    for index in range(4 * chunks - SEND_SLOTS, 4 * chunks):
        wait_sent(index)
    sent = ring.at[pl.ds(0, chips - 1)]
    pltpu.make_async_copy(sent, sent, rs_send).wait()
    pltpu.make_async_copy(sent, sent, ag_send).wait()
    shared = dw_hbm.at[pl.ds(0, degs // 2 * wide)]
    for which in range(3):
        pltpu.make_async_copy(shared, shared, dw_sem.at[which]).wait()


def solution(mesh):
    n = mesh.shape['lat']
    field_spec = P('member', None, 'lat', None)

    def local_step(field_loc, grad_loc, p_fwd, p_inv, w_mix):
        batch, chans, tl, lons = field_loc.shape
        degs, lats = p_fwd.shape[1:]
        ml = p_fwd.shape[0] // n
        nb = 4
        chunks = batch // nb
        rows = ml * 2 * nb
        pitch = rows + 1
        half = degs // n
        pieces = 3 if half % 3 == 0 else 1
        hops = (n // 2 - 1) * pieces
        ringed = pltpu.VMEM((n // 2, half * 2 * chans, chans), F32)
        tables = fourier_tables(n, ml, lons)
        anywhere = pl.BlockSpec(memory_space=pl.ANY)
        vmem = pl.BlockSpec(memory_space=pltpu.VMEM)
        grad_field, grad_w = pl.pallas_call(
            functools.partial(layer_kernel, 'lat', n, nb, pieces),
            name='layer',
            out_shape=(
                jax.ShapeDtypeStruct((batch, tl, lons, chans), F32),
                jax.ShapeDtypeStruct((degs * 2 * chans, chans), F32),
            ),
            in_specs=[anywhere] * 5 + [vmem] * len(tables),
            out_specs=(anywhere, anywhere),
            scratch_shapes=[
                pltpu.VMEM((2, chunks, n, tl, rows, chans), BF16),
                pltpu.VMEM((SEND_SLOTS, n, tl, rows, chans), BF16),
                pltpu.VMEM((lats * pitch, chans), F32),
                pltpu.VMEM((lats * pitch, chans), F32),
                pltpu.VMEM((lats, 2 * nb * chans), BF16),
                pltpu.VMEM((degs, chunks, rows, chans), BF16),
                pltpu.VMEM((degs, chunks, rows, chans), BF16),
                pltpu.VMEM((degs, 2 * chans, chans), BF16),
                pltpu.VMEM((2, 8 * 2 * chans, chans), F32),
                pltpu.VMEM((2, nb, lons, chans), F32),
                pltpu.VMEM((2, nb, lons, chans), F32),
                pltpu.VMEM((n * rows, chans), F32),
                pltpu.VMEM((2, ml, degs, lats), F32),
                pltpu.VMEM((2, ml, degs, lats), BF16),
                ringed, ringed, ringed,
                pltpu.SemaphoreType.DMA((4 * chunks,)),
                pltpu.SemaphoreType.DMA((4 * chunks,)),
                pltpu.SemaphoreType.DMA((2,)),
                pltpu.SemaphoreType.DMA((2,)),
                pltpu.SemaphoreType.DMA((2,)),
                pltpu.SemaphoreType.DMA((2,)),
                pltpu.SemaphoreType.DMA((2,)),
                pltpu.SemaphoreType.DMA((n // 2,)),
                pltpu.SemaphoreType.DMA,
                pltpu.SemaphoreType.DMA((hops,)),
                pltpu.SemaphoreType.DMA,
                pltpu.SemaphoreType.DMA((hops,)),
                pltpu.SemaphoreType.DMA((3,)),
            ],
            compiler_params=pltpu.CompilerParams(
                collective_id=0, has_side_effects=True, vmem_limit_bytes=62 * 1024 * 1024),
        )(
            field_loc.transpose(0, 2, 3, 1), grad_loc.transpose(0, 2, 3, 1),
            w_mix.transpose(0, 1, 3, 2).reshape(degs * 2 * chans, chans),
            p_fwd, p_inv, *tables)
        return grad_field.transpose(0, 3, 1, 2), grad_w.reshape(degs, chans, 2, chans).transpose(0, 1, 3, 2)

    return jax.shard_map(
        local_step, mesh=mesh, in_specs=(field_spec, field_spec, P(), P(), P()),
        out_specs=(field_spec, P('member', None, None, None)), check_vma=False)
```

time: 509 us -> 453 us (0.89)
  waiting for transfers between devices: 146 us -> 0 us
  Pallas kernels: 331 us -> 434 us
  between operations: 14.1 us -> 0.65 us
    psum x1 -> x0, waiting for transfers between devices: 146 us -> none  [local_step(): total = lax.psum(grad_w, 'lat')]
    pallas_call x1, Pallas kernels: 331 us -> 434 us  [local_step(): pl.pallas_call(functools.partial(layer_kernel, 'lat', n, nb, pieces), nam...]
    unnamed x10 -> x4, local copies, waits for them, and re-layouts: 14.2 us -> 13.9 us
  transfers between devices with their start and end apart: 1 -> 0, of which waited for: 1 -> 0; matrix products, arithmetic and copies ran while one was open for 0% -> 0% of each run, Pallas kernels for 0% -> 0%
where the time goes in v2:
time: 453 us; the launch traced here: 449 us
  Pallas kernels  434 us (96%)
  local copies, waits for them, and re-layouts  13.9 us (3%)
    pallas_call x1, Pallas kernels, local_step(): pl.pallas_call(functools.partial(layer_kernel, 'lat', n, nb, pieces), nam...  434 us
    unnamed x4, local copies, waits for them, and re-layouts  13.9 us

profile of v2, /device:TPU:21, one launch (start us, length us, event | category | flops | bytes accessed | tf_op | source)
XLA Modules:
  0.0 448.8 jit_solution(14509124823565300330)
XLA Ops:
  0.6 434.3 %layer.1 = (f32[12,6,192,128]{3,2,1,0:T(8,128)}, f32[24576,128]{1,0:T(8,128)}) custom-call(f32[12,6,192,128]{3,2,1,0:T(8,128)} %bitcast.12, f32[12,6,192,128]{3,2,1,0:T(8,128)} %bitcast.13, f32[24576,128]{1,0:T(8,128)} %bitcast.10, f32[96,96,96]{2,1,0:T(8,128)} %pf_hbm.1, f32[96,96,96]{2,1,0:T(8,128)} %pv_hbm.1, bf16[192,192]{1,0:T(8,128)(2,1)} %constant.16.clone.fwd_h, ...), custom_call_target="tpu_custom_call" | custom-call | tf_op jit(solution)/shard_map/layer/pallas_call | solution.py:475
  434.9 0.0 copy-start
  434.9 7.6 %copy.17 = f32[12,128,6,192]{1,3,2,0:T(8,128)} copy(f32[12,128,6,192]{1,3,2,0:T(8,128)} %bitcast.11) | data formatting | bytes 14155776
  442.5 1.5 copy-done
  444.1 4.8 %copy.18 = f32[96,128,128,2]{2,3,1,0:T(2,128)} copy(f32[96,128,128,2]{2,3,1,0:T(2,128)S(1)} %bitcast.9) | data formatting | bytes 25165824
Async XLA Ops:
  434.9 9.1 %copy-start = (f32[24576,128]{1,0:T(8,128)S(1)}, f32[24576,128]{1,0:T(8,128)}, u32[]{:S(2)}) copy-start(f32[24576,128]{1,0:T(8,128)} %get-tuple-element.5) | copy-start | bytes 37748740

commit v3 on v2

--- a/solution.py
+++ b/solution.py
@@ -45,9 +45,10 @@
     axis, n, nb, pieces,
     f_hbm, dg_hbm, w_hbm, pf_hbm, pv_hbm,
     fwd_h, fwd_l, dbl_h, dbl_l, syn_h, syn_l, adj_h, adj_l,
-    df_hbm, dw_hbm,
-    recv, send, t1, t2, xb, coef, dq, vmix, wbuf, inbuf, outbuf, gather, pbuf, pmat, mine, theirs, ring,
-    send_sem, recv_sem, in_sem, out_sem, w_sem, p_sem, pair_send, pair_recv, rs_send, rs_recv, ag_send, ag_recv, dw_sem,
+    df_out, dw_out,
+    recv, send, t1, t2, xb, coef, dq, vmix, wbuf, inbuf, gather, pbuf, pmat, mine, low,
+    send_sem, recv_sem, in_sem, w_sem, p_sem, pair_send, pair_recv, rs_send, rs_recv, ag_send, ag_recv,
+    low_send, low_recv, free_sem, pub_send, pub_recv,
 ):
     me = lax.axis_index(axis)
     batch, tl, lons, chans = f_hbm.shape
@@ -74,11 +75,6 @@
         ch, t = unit_of(unit)
         slot = lax.rem(unit, 2)
         return pltpu.make_async_copy(src.at[pl.ds(ch * nb, nb), t], inbuf.at[slot], in_sem.at[slot])
-
-    def unit_out(unit):
-        ch, t = unit_of(unit)
-        slot = lax.rem(unit, 2)
-        return pltpu.make_async_copy(outbuf.at[slot], df_hbm.at[pl.ds(ch * nb, nb), t], out_sem.at[slot])
 
     def step_in(src, unit):
         @pl.when(unit + 1 < units)
@@ -200,8 +196,8 @@
     sign = jnp.where(lax.broadcasted_iota(jnp.int32, (tile, chans), 0) < nb, -1.0, 1.0).astype(F32)
 
     def turn(values):
-        groups = values.reshape(ml, tile, chans)
-        return (pltpu.roll(groups, nb, 1) * sign[None]).reshape(rows, chans)
+        groups = values.reshape(-1, tile, chans)
+        return (pltpu.roll(groups, nb, 1) * sign[None]).reshape(values.shape)
 
     def legendre(src, dst, which, over):
         def mode(m, _):
@@ -260,6 +256,21 @@
         return 0
 
     lax.fori_loop(0, chunks, step2_chunk, 0)
+
+    def send_low(which, kept):
+        def one(k, _):
+            peer = lax.rem(me + k, n)
+            pltpu.make_async_remote_copy(
+                src_ref=kept.at[peer, :, pl.ds(0, tile)], dst_ref=low.at[which, me],
+                send_sem=low_send.at[which], recv_sem=low_recv.at[which],
+                device_id={axis: peer}, device_id_type=pl.DeviceIdType.MESH,
+            ).start()
+            return 0
+
+        lax.fori_loop(1, n, one, 0)
+        low[which, me] = kept[me, :, pl.ds(0, tile)]
+
+    send_low(0, coef)
 
     def fetch_rows(stage, ch, t):
         for src in range(n):
@@ -297,15 +308,17 @@
         return 0
 
     lax.fori_loop(0, chunks, step4_chunk, 0)
+    send_low(1, dq)
 
     chip, core = lax.div(me, 2), lax.rem(me, 2)
     chips = n // 2
     way = 1 - 2 * core
     sibling = me + way
     onward = 2 * lax.rem(chip + way + chips, chips) + core
-    half = degs // n
-    piece = half // pieces * 2 * chans
+    half = degs // n - 1
     wide = 2 * chans
+    piece = half * wide // pieces
+    hops = (chips - 1) * pieces
 
     def block_at(k, direction):
         return lax.rem(chip - direction * (1 + k) + 2 * chips, chips)
@@ -315,34 +328,39 @@
             src_ref=src, dst_ref=dst, send_sem=sent, recv_sem=got,
             device_id={axis: device}, device_id_type=pl.DeviceIdType.MESH)
 
-    def weight_grad(dst, degree, count):
+    def outer(dst, row, pairs):
+        real = jnp.zeros((chans, chans), F32)
+        imag = jnp.zeros((chans, chans), F32)
+        for y, x in pairs:
+            real += dot(y, x, ((0,), (0,)))
+            imag -= dot(turn(y.astype(F32)).astype(BF16), x, ((0,), (0,)))
+        dst[pl.ds(row, chans, stride=2), :] = real
+        dst[pl.ds(row + 1, chans, stride=2), :] = imag
+
+    def first_degree(block, of_core):
+        return n + (2 * block + of_core) * half
+
+    def weight_grad(dst, degree):
         def one(j, _):
-            real = jnp.zeros((chans, chans), F32)
-            imag = jnp.zeros((chans, chans), F32)
-            for ch in range(chunks):
-                y = dq[degree + j, ch]
-                x = coef[degree + j, ch]
-                real += dot(y, x, ((0,), (0,)))
-                imag -= dot(turn(y.astype(F32)).astype(BF16), x, ((0,), (0,)))
-            dst[pl.ds(j * wide, chans, stride=2), :] = real
-            dst[pl.ds(j * wide + 1, chans, stride=2), :] = imag
-            return 0
-
-        lax.fori_loop(0, count, one, 0)
+            outer(dst, j * wide, [(dq[degree + j, ch], coef[degree + j, ch]) for ch in range(chunks)])
+            return 0
+
+        lax.fori_loop(0, half, one, 0)
 
     def pair_copy(k):
         slot = lax.rem(k, 2)
-        return to(sibling, wbuf.at[slot, pl.ds(0, half * wide)], theirs.at[block_at(k, -way)],
+        rows_there = pl.ds(first_degree(block_at(k, -way), core) * wide, half * wide)
+        return to(sibling, wbuf.at[slot, pl.ds(0, half * wide)], dw_out.at[rows_there],
                   pair_send.at[slot], pair_recv.at[k])
 
     def weight_block(k, _):
         @pl.when(k >= 2)
         def _():
             pair_copy(k - 2).wait_send()
-        weight_grad(wbuf.at[lax.rem(k, 2)], (2 * block_at(k, -way) + 1 - core) * half, half)
+        weight_grad(wbuf.at[lax.rem(k, 2)], first_degree(block_at(k, -way), 1 - core))
         pair_copy(k).start()
         block = block_at(k, way)
-        weight_grad(mine.at[block], (2 * block + core) * half, half)
+        weight_grad(mine.at[block], first_degree(block, core))
         return 0
 
     lax.fori_loop(0, chips, weight_block, 0)
@@ -358,45 +376,42 @@
 
         step_in(dg_hbm, unit)
         buf = lax.rem(unit, 2)
-
-        @pl.when(unit >= 2)
-        def _():
-            unit_out(unit - 2).wait()
 
         fetch_rows(3, ch, t)
         for b in range(0, nb, 2):
             g = fetch_pair(b)
             change = dot(adj_h[...], g) + dot(adj_l[...], g)
-            outbuf[buf, b] = inbuf[buf, b] + change[:, :chans]
-            outbuf[buf, b + 1] = inbuf[buf, b + 1] + change[:, chans:]
-        unit_out(unit).start()
-
-    hops = (chips - 1) * pieces
-
-    def add_up(i):
-        k, part = lax.div(i, pieces), pl.ds(lax.rem(i, pieces) * piece, piece)
-        block = block_at(k, way)
+            df_out[ch * nb + b, t] = inbuf[buf, b] + change[:, :chans]
+            df_out[ch * nb + b + 1, t] = inbuf[buf, b + 1] + change[:, chans:]
+
+    def place(i, of_core):
+        block = block_at(lax.div(i, pieces), way)
+        start = lax.rem(i, pieces) * piece
+        return block, pl.ds(start, piece), pl.ds(first_degree(block, of_core) * wide + start, piece)
+
+    def rs_copy(i):
+        block, part, there = place(i, core)
+        return to(onward, mine.at[block, part], dw_out.at[there], rs_send, rs_recv.at[i])
+
+    def add_pair(i):
+        block, part, _ = place(i, core)
+        _, _, passed = place(i, 1 - core)
 
         @pl.when(lax.rem(i, pieces) == 0)
         def _():
-            pair_copy(k).wait_recv()
-
-        mine[block, part] += theirs[block, part]
-
-        @pl.when(k > 0)
+            pair_copy(lax.div(i, pieces)).wait_recv()
+
+        mine[block, part] += dw_out[passed]
+
+    def rs_step(i, _):
+        add_pair(i)
+
+        @pl.when(i >= pieces)
         def _():
             rs_copy(i - pieces).wait_recv()
-            mine[block, part] += ring[block, part]
-
-        return block, part
-
-    def rs_copy(i):
-        k, part = lax.div(i, pieces), pl.ds(lax.rem(i, pieces) * piece, piece)
-        block = block_at(k, way)
-        return to(onward, mine.at[block, part], ring.at[block, part], rs_send, rs_recv.at[i])
-
-    def rs_step(i, _):
-        add_up(i)
+            block, part, there = place(i, core)
+            mine[block, part] += dw_out[there]
+
         rs_copy(i).start()
 
         @pl.when(i < units)
@@ -407,30 +422,69 @@
 
     lax.fori_loop(0, hops, rs_step, 0)
 
-    def publish(source, block, i):
-        rows_out = pl.ds(((2 * block + core) * half) * wide + lax.rem(i, pieces) * piece, piece)
-        pltpu.make_async_copy(source, dw_hbm.at[rows_out], dw_sem.at[0]).start()
-        to(sibling, source, dw_hbm.at[rows_out], dw_sem.at[1], dw_sem.at[2]).start()
+    def own_sum(s, _):
+        i = hops + s
+        add_pair(i)
+        rs_copy(i - pieces).wait_recv()
+        block, part, there = place(i, core)
+        dw_out[there] += mine[block, part]
+        return 0
+
+    lax.fori_loop(0, pieces, own_sum, 0)
+    pl.semaphore_signal(free_sem, inc=1, device_id={axis: sibling}, device_id_type=pl.DeviceIdType.MESH)
+
+    for which in range(2):
+        others = low.at[which, pl.ds(0, n - 1)]
+        pltpu.make_async_copy(others, others, low_recv.at[which]).wait()
+    outer(wbuf.at[0], 0, [(low[1].reshape(-1, chans), low[0].reshape(-1, chans))])
+    dw_out[pl.ds(me * wide, wide)] = wbuf[0, pl.ds(0, wide)]
+
+    def spot(i):
+        return pl.ds(first_degree(block_at(lax.div(i, pieces), way), core) * wide + lax.rem(i, pieces) * piece, piece)
+
+    def low_spot(k):
+        return pl.ds((2 * block_at(k, way) + core) * wide, wide)
+
+    def ag_copy(rows_out, got):
+        return to(onward, dw_out.at[rows_out], dw_out.at[rows_out], ag_send, got)
+
+    def publish(rows_out):
+        to(sibling, dw_out.at[rows_out], dw_out.at[rows_out], pub_send, pub_recv).start()
+
+    pl.semaphore_wait(free_sem, 1)
 
     def own_piece(s, _):
-        block, part = add_up(hops + s)
-        to(onward, mine.at[block, part], ring.at[block, part], ag_send, ag_recv.at[s]).start()
-        publish(mine.at[block, part], block, s)
+        rows_out = spot(hops + s)
+        ag_copy(rows_out, ag_recv.at[s]).start()
+        publish(rows_out)
         return 0
 
     lax.fori_loop(0, pieces, own_piece, 0)
+    ag_copy(low_spot(chips - 1), ag_recv.at[hops]).start()
+    publish(low_spot(chips - 1))
 
     def ag_step(i, _):
-        part = pl.ds(lax.rem(i, pieces) * piece, piece)
-        block = block_at(lax.div(i, pieces), way)
-        held = ring.at[block, part]
-        to(onward, held, held, ag_send, ag_recv.at[i]).wait_recv()
+        rows_out = spot(i)
+        ag_copy(rows_out, ag_recv.at[i]).wait_recv()
 
         @pl.when(i + pieces < hops)
         def _():
-            to(onward, held, held, ag_send, ag_recv.at[i + pieces]).start()
-
-        publish(held, block, i)
+            ag_copy(rows_out, ag_recv.at[i + pieces]).start()
+
+        publish(rows_out)
+
+        @pl.when(lax.rem(i, pieces) == pieces - 1)
+        def _():
+            k = lax.div(i, pieces)
+            low_out = low_spot(k)
+            ag_copy(low_out, ag_recv.at[hops + k]).wait_recv()
+
+            @pl.when(k < chips - 2)
+            def _():
+                ag_copy(low_out, ag_recv.at[hops + k + 1]).start()
+
+            publish(low_out)
+
         return 0
 
     lax.fori_loop(0, hops, ag_step, 0)
@@ -441,16 +495,18 @@
 
     lax.fori_loop(min(hops, units), units, rest, 0)
 
-    unit_out(units - 2).wait()
-    unit_out(units - 1).wait()
     for index in range(4 * chunks - SEND_SLOTS, 4 * chunks):
         wait_sent(index)
-    sent = ring.at[pl.ds(0, chips - 1)]
+    sent = mine.at[pl.ds(0, chips - 1)]
     pltpu.make_async_copy(sent, sent, rs_send).wait()
+    sent = dw_out.at[pl.ds(0, (chips - 1) * (half + 1) * wide)]
     pltpu.make_async_copy(sent, sent, ag_send).wait()
-    shared = dw_hbm.at[pl.ds(0, degs // 2 * wide)]
-    for which in range(3):
-        pltpu.make_async_copy(shared, shared, dw_sem.at[which]).wait()
+    for which in range(2):
+        others = low.at[which, pl.ds(0, n - 1)]
+        pltpu.make_async_copy(others, others, low_send.at[which]).wait()
+    shared = dw_out.at[pl.ds(0, degs // 2 * wide)]
+    pltpu.make_async_copy(shared, shared, pub_send).wait()
+    pltpu.make_async_copy(shared, shared, pub_recv).wait()
 
 
 def solution(mesh):
@@ -465,10 +521,9 @@
         chunks = batch // nb
         rows = ml * 2 * nb
         pitch = rows + 1
-        half = degs // n
-        pieces = 3 if half % 3 == 0 else 1
+        half = degs // n - 1
+        pieces = 4 if half * 2 * chans % 32 == 0 else 1
         hops = (n // 2 - 1) * pieces
-        ringed = pltpu.VMEM((n // 2, half * 2 * chans, chans), F32)
         tables = fourier_tables(n, ml, lons)
         anywhere = pl.BlockSpec(memory_space=pl.ANY)
         vmem = pl.BlockSpec(memory_space=pltpu.VMEM)
@@ -476,11 +531,11 @@
             functools.partial(layer_kernel, 'lat', n, nb, pieces),
             name='layer',
             out_shape=(
-                jax.ShapeDtypeStruct((batch, tl, lons, chans), F32),
-                jax.ShapeDtypeStruct((degs * 2 * chans, chans), F32),
+                pltpu.VMEM((batch, tl, lons, chans), F32),
+                pltpu.VMEM((degs * 2 * chans, chans), F32),
             ),
             in_specs=[anywhere] * 5 + [vmem] * len(tables),
-            out_specs=(anywhere, anywhere),
+            out_specs=(vmem, vmem),
             scratch_shapes=[
                 pltpu.VMEM((2, chunks, n, tl, rows, chans), BF16),
                 pltpu.VMEM((SEND_SLOTS, n, tl, rows, chans), BF16),
@@ -492,14 +547,13 @@
                 pltpu.VMEM((degs, 2 * chans, chans), BF16),
                 pltpu.VMEM((2, 8 * 2 * chans, chans), F32),
                 pltpu.VMEM((2, nb, lons, chans), F32),
-                pltpu.VMEM((2, nb, lons, chans), F32),
                 pltpu.VMEM((n * rows, chans), F32),
                 pltpu.VMEM((2, ml, degs, lats), F32),
                 pltpu.VMEM((2, ml, degs, lats), BF16),
-                ringed, ringed, ringed,
+                pltpu.VMEM((n // 2, half * 2 * chans, chans), F32),
+                pltpu.VMEM((2, n, chunks, 2 * nb, chans), BF16),
                 pltpu.SemaphoreType.DMA((4 * chunks,)),
                 pltpu.SemaphoreType.DMA((4 * chunks,)),
-                pltpu.SemaphoreType.DMA((2,)),
                 pltpu.SemaphoreType.DMA((2,)),
                 pltpu.SemaphoreType.DMA((2,)),
                 pltpu.SemaphoreType.DMA((2,)),
@@ -508,11 +562,15 @@
                 pltpu.SemaphoreType.DMA,
                 pltpu.SemaphoreType.DMA((hops,)),
                 pltpu.SemaphoreType.DMA,
-                pltpu.SemaphoreType.DMA((hops,)),
-                pltpu.SemaphoreType.DMA((3,)),
+                pltpu.SemaphoreType.DMA((hops + n // 2 - 1,)),
+                pltpu.SemaphoreType.DMA((2,)),
+                pltpu.SemaphoreType.DMA((2,)),
+                pltpu.SemaphoreType.REGULAR,
+                pltpu.SemaphoreType.DMA,
+                pltpu.SemaphoreType.DMA,
             ],
             compiler_params=pltpu.CompilerParams(
-                collective_id=0, has_side_effects=True, vmem_limit_bytes=62 * 1024 * 1024),
+                collective_id=0, has_side_effects=True, vmem_limit_bytes=42 * 1024 * 1024),
         )(
             field_loc.transpose(0, 2, 3, 1), grad_loc.transpose(0, 2, 3, 1),
             w_mix.transpose(0, 1, 3, 2).reshape(degs * 2 * chans, chans),

time: 453 us -> 447 us (0.987)
  local copies, waits for them, and re-layouts: 13.9 us -> 7.74 us
    unnamed x4 -> x2, local copies, waits for them, and re-layouts: 13.9 us -> 7.74 us
where the time goes in v3:
time: 447 us; the launch traced here: 446 us
  Pallas kernels  437 us (98%)
  local copies, waits for them, and re-layouts  7.74 us (2%)
    pallas_call x1, Pallas kernels, local_step(): pl.pallas_call(functools.partial(layer_kernel, 'lat', n, nb, pieces), nam...  437 us

profile of v3, /device:TPU:21, one launch (start us, length us, event | category | flops | bytes accessed | tf_op | source)
XLA Modules:
  0.0 445.8 jit_solution(12767385219171796975)
XLA Ops:
  0.6 437.4 %layer.1 = (f32[12,6,192,128]{3,2,1,0:T(8,128)S(1)}, f32[24576,128]{1,0:T(8,128)S(1)}) custom-call(f32[12,6,192,128]{3,2,1,0:T(8,128)} %bitcast.12, f32[12,6,192,128]{3,2,1,0:T(8,128)} %bitcast.13, f32[24576,128]{1,0:T(8,128)} %bitcast.11, f32[96,96,96]{2,1,0:T(8,128)} %pf_hbm.1, f32[96,96,96]{2,1,0:T(8,128)} %pv_hbm.1, ...), custom_call_target="tpu_custom_call" | custom-call | tf_op jit(solution)/shard_map/layer/pallas_call | solution.py:530
  438.0 3.0 copy.17
  441.0 4.8 %copy.18 = f32[96,128,128,2]{2,3,1,0:T(2,128)} copy(f32[96,128,128,2]{2,3,1,0:T(2,128)S(1)} %bitcast.9) | data formatting | bytes 25165824

commit v4 on v3

--- a/solution.py
+++ b/solution.py
@@ -22,7 +22,9 @@
 
 def fourier_tables(n, ml, lons):
     modes = n * ml
-    order = np.arange(modes).reshape(ml, n).T.reshape(-1)
+    device = np.arange(n)
+    first = np.where(device % 2 == 0, device // 2, n - 1 - device // 2)
+    order = (first[:, None] + n * np.arange(ml)[None, :]).reshape(-1)
     angle = 2.0 * np.pi * (np.outer(order, np.arange(lons)) % lons) / lons
     forward = np.stack([np.cos(angle), -np.sin(angle)], axis=1).reshape(2 * modes, lons) / math.sqrt(lons)
     gains = np.repeat(np.where(order == 0, 1.0, 2.0), 2)[:, None]
@@ -42,13 +44,13 @@
 
 
 def layer_kernel(
-    axis, n, nb, pieces,
+    axis, n, nb, pieces, per,
     f_hbm, dg_hbm, w_hbm, pf_hbm, pv_hbm,
     fwd_h, fwd_l, dbl_h, dbl_l, syn_h, syn_l, adj_h, adj_l,
     df_out, dw_out,
-    recv, send, t1, t2, xb, coef, dq, vmix, wbuf, inbuf, gather, pbuf, pmat, mine, low,
-    send_sem, recv_sem, in_sem, w_sem, p_sem, pair_send, pair_recv, rs_send, rs_recv, ag_send, ag_recv,
-    low_send, low_recv, free_sem, pub_send, pub_recv,
+    recv, send, work, xb, coef, dq, vmix, wbuf, inbuf, gather, pbuf, pmat, band, cmat, qs, own, other, packs, lowx,
+    send_sem, recv_sem, in_sem, w_sem, p_sem, band_sem, pair_send, pair_recv, rs_send, rs_recv, ag_send, ag_recv,
+    free_sem, pub_send, pub_recv, own_send, own_recv, pack_send, pack_recv, share_send, share_recv,
 ):
     me = lax.axis_index(axis)
     batch, tl, lons, chans = f_hbm.shape
@@ -59,6 +61,23 @@
     pitch = rows + 1
     modes2 = 2 * n * ml
     units = chunks * tl
+    area = lats * pitch
+    top = n * (ml - 1)
+    held = n // 2 + 1
+    chip, core = lax.div(me, 2), lax.rem(me, 2)
+    chips = n // 2
+    way = 1 - 2 * core
+    sibling = me + way
+    onward = 2 * lax.rem(chip + way + chips, chips) + core
+
+    def first_mode(device):
+        z = lax.div(device, 2)
+        return jnp.where(lax.rem(device, 2) == 0, z, n - 1 - z)
+
+    def to(device, src, dst, sent, got):
+        return pltpu.make_async_remote_copy(
+            src_ref=src, dst_ref=dst, send_sem=sent, recv_sem=got,
+            device_id={axis: device}, device_id_type=pl.DeviceIdType.MESH)
 
     barrier = pltpu.get_barrier_semaphore()
 
@@ -82,29 +101,29 @@
             unit_in(src, unit + 1).start()
         unit_in(src, unit).wait()
 
+    def sent_rows(stage):
+        return pl.ds(0, rows - tile if stage == 3 else rows)
+
     def ship(stage, ch, t0, nt):
         index = stage * chunks + ch
         slot = lax.rem(index, SEND_SLOTS)
-        part = pl.ds(t0, nt)
+        part, span = pl.ds(t0, nt), sent_rows(stage)
 
         def one(k, _):
             peer = lax.rem(me + k, n)
-            pltpu.make_async_remote_copy(
-                src_ref=send.at[slot, peer, part], dst_ref=recv.at[stage % 2, ch, me, part],
-                send_sem=send_sem.at[index], recv_sem=recv_sem.at[index],
-                device_id={axis: peer}, device_id_type=pl.DeviceIdType.MESH,
-            ).start()
+            to(peer, send.at[slot, peer, part, span], recv.at[stage % 2, ch, me, part, span],
+               send_sem.at[index], recv_sem.at[index]).start()
             return 0
 
         lax.fori_loop(1, n, one, 0)
-        recv[stage % 2, ch, me, part] = send[slot, me, part]
+        recv[stage % 2, ch, me, part, span] = send[slot, me, part, span]
 
     def arrived(stage, ch):
-        others = recv.at[stage % 2, ch, pl.ds(0, n - 1)]
+        others = recv.at[stage % 2, ch, pl.ds(0, n - 1), :, sent_rows(stage)]
         pltpu.make_async_copy(others, others, recv_sem.at[stage * chunks + ch]).wait()
 
-    def wait_sent(index):
-        others = send.at[lax.rem(index, SEND_SLOTS), pl.ds(0, n - 1)]
+    def wait_sent(index, stage=0):
+        others = send.at[lax.rem(index, SEND_SLOTS), pl.ds(0, n - 1), :, sent_rows(stage)]
         pltpu.make_async_copy(others, others, send_sem.at[index]).wait()
 
     def free_slot(stage, ch):
@@ -127,7 +146,13 @@
     unit_in(f_hbm, 0).start()
     for which, source in enumerate((pf_hbm, pv_hbm)):
         for k in range(ml):
-            pltpu.make_async_copy(source.at[me + n * k], pbuf.at[which, k], p_sem.at[which]).start()
+            pltpu.make_async_copy(source.at[first_mode(me) + n * k], pbuf.at[which, k], p_sem.at[which]).start()
+
+    def band_in(d, _):
+        pltpu.make_async_copy(pf_hbm.at[top + first_mode(d), pl.ds(top, n)], band.at[d], band_sem).start()
+        return 0
+
+    lax.fori_loop(0, n, band_in, 0)
 
     group = 2 if tl % 2 == 0 else 1
 
@@ -170,12 +195,11 @@
         pltpu.make_async_copy(pbuf.at[which], pbuf.at[which], p_sem.at[which]).wait()
     pmat[...] = pbuf[...].astype(BF16)
 
-    per = wbuf.shape[1] // (2 * chans)
     parts = degs // per
 
     def w_in(k):
         slot = lax.rem(k, 2)
-        return pltpu.make_async_copy(w_hbm.at[pl.ds(k * per * 2 * chans, per * 2 * chans)], wbuf.at[slot], w_sem.at[slot])
+        return pltpu.make_async_copy(w_hbm.at[pl.ds(k * per * 2 * chans, per * 2 * chans)], wbuf.at[slot, pl.ds(0, per * 2 * chans)], w_sem.at[slot])
 
     w_in(0).start()
 
@@ -202,10 +226,11 @@
     def legendre(src, dst, which, over):
         def mode(m, _):
             for k in range(tile):
-                xb[:, k * chans:(k + 1) * chans] = src[pl.ds(m * tile + k, lats, stride=pitch), :].astype(BF16)
+                xb[:, k * chans:(k + 1) * chans] = work[
+                    pl.ds(src + m * tile + k, lats, stride=pitch), :].astype(BF16)
             out = dot(pmat[which, m], xb[...], ((over,), (0,)))
             for k in range(tile):
-                dst[pl.ds(m * tile + k, degs, stride=pitch), :] = out[:, k * chans:(k + 1) * chans]
+                work[pl.ds(dst + m * tile + k, degs, stride=pitch), :] = out[:, k * chans:(k + 1) * chans]
             return 0
 
         lax.fori_loop(0, ml, mode, 0)
@@ -213,7 +238,7 @@
     def unload(stage, ch):
         def body(src, _):
             for t in range(tl):
-                t1[pl.ds((src * tl + t) * pitch, rows), :] = recv[stage % 2, ch, src, t].astype(F32)
+                work[pl.ds((src * tl + t) * pitch, rows), :] = recv[stage % 2, ch, src, t].astype(F32)
             return 0
 
         lax.fori_loop(0, n, body, 0)
@@ -221,24 +246,43 @@
     def load(slot):
         def body(dev, _):
             for t in range(tl):
-                send[slot, dev, t] = t2[pl.ds((dev * tl + t) * pitch, rows), :].astype(BF16)
+                send[slot, dev, t] = work[pl.ds(area + (dev * tl + t) * pitch, rows), :].astype(BF16)
             return 0
 
         lax.fori_loop(0, n, body, 0)
+
+    def pack(store):
+        def one(index, _):
+            half_at, row = lax.div(index, held), lax.rem(index, held)
+            p = half_at * (held - 1) + row
+            degree = jnp.where(core == 0, jnp.minimum(chip + p, n - 1), jnp.maximum(p - 1, 0))
+            store(half_at, row, degree, (p < n - chip) == (core == 0))
+            return 0
+
+        lax.fori_loop(0, 2 * held, one, 0)
+
+    def only(ours, values):
+        values = values.astype(F32)
+        return jnp.where(ours, values, jnp.zeros_like(values)).astype(BF16)
 
     def spectral(stage, ch, into, kept, mix):
         arrived(stage - 1, ch)
         unload(stage - 1, ch)
-        legendre(t1, t2, into, 1)
+        legendre(0, area, into, 1)
 
         def degree(l, _):
-            x = t2[pl.ds(l * pitch, rows), :].astype(BF16)
+            x = work[pl.ds(area + l * pitch, rows), :].astype(BF16)
             kept[l, ch] = x
-            t1[pl.ds(l * pitch, rows), :] = mix(l, x)
+            work[pl.ds(l * pitch, rows), :] = mix(l, x)
             return 0
 
         lax.fori_loop(0, degs, degree, 0, unroll=2)
-        legendre(t1, t2, 1 - into, 0)
+        if stage == 3:
+            def keep_top(half_at, row, degree, ours):
+                own[half_at, 2, ch, row] = only(ours, work[pl.ds((top + degree) * pitch + rows - tile, tile), :])
+
+            pack(keep_top)
+        legendre(0, area, 1 - into, 0)
         load(free_slot(stage, ch))
         ship(stage, ch, 0, tl)
 
@@ -256,21 +300,6 @@
         return 0
 
     lax.fori_loop(0, chunks, step2_chunk, 0)
-
-    def send_low(which, kept):
-        def one(k, _):
-            peer = lax.rem(me + k, n)
-            pltpu.make_async_remote_copy(
-                src_ref=kept.at[peer, :, pl.ds(0, tile)], dst_ref=low.at[which, me],
-                send_sem=low_send.at[which], recv_sem=low_recv.at[which],
-                device_id={axis: peer}, device_id_type=pl.DeviceIdType.MESH,
-            ).start()
-            return 0
-
-        lax.fori_loop(1, n, one, 0)
-        low[which, me] = kept[me, :, pl.ds(0, tile)]
-
-    send_low(0, coef)
 
     def fetch_rows(stage, ch, t):
         for src in range(n):
@@ -308,25 +337,32 @@
         return 0
 
     lax.fori_loop(0, chunks, step4_chunk, 0)
-    send_low(1, dq)
-
-    chip, core = lax.div(me, 2), lax.rem(me, 2)
-    chips = n // 2
-    way = 1 - 2 * core
-    sibling = me + way
-    onward = 2 * lax.rem(chip + way + chips, chips) + core
+
+    for which, kept in enumerate((coef, dq)):
+        def keep_low(half_at, row, degree, ours):
+            own[half_at, which, :, row] = only(ours, kept[degree, :, pl.ds(0, tile)])
+
+        pack(keep_low)
+    own_copy = to(sibling, own.at[1 - core], other, own_send, own_recv)
+    own_copy.start()
+
+    def pack_block(k):
+        return packs.at[core, lax.rem(chip - way * k + chips, chips)]
+
+    def pack_copy(k):
+        return to(onward, pack_block(k), pack_block(k), pack_send, pack_recv.at[k])
+
+    def share(k):
+        to(sibling, pack_block(k), pack_block(k), share_send, share_recv).start()
+
     half = degs // n - 1
     wide = 2 * chans
-    piece = half * wide // pieces
+    block_rows = half * wide
+    piece = block_rows // pieces
     hops = (chips - 1) * pieces
 
     def block_at(k, direction):
         return lax.rem(chip - direction * (1 + k) + 2 * chips, chips)
-
-    def to(device, src, dst, sent, got):
-        return pltpu.make_async_remote_copy(
-            src_ref=src, dst_ref=dst, send_sem=sent, recv_sem=got,
-            device_id={axis: device}, device_id_type=pl.DeviceIdType.MESH)
 
     def outer(dst, row, pairs):
         real = jnp.zeros((chans, chans), F32)
@@ -349,8 +385,8 @@
 
     def pair_copy(k):
         slot = lax.rem(k, 2)
-        rows_there = pl.ds(first_degree(block_at(k, -way), core) * wide, half * wide)
-        return to(sibling, wbuf.at[slot, pl.ds(0, half * wide)], dw_out.at[rows_there],
+        rows_there = pl.ds(first_degree(block_at(k, -way), core) * wide, block_rows)
+        return to(sibling, wbuf.at[slot, pl.ds(0, block_rows)], dw_out.at[rows_there],
                   pair_send.at[slot], pair_recv.at[k])
 
     def weight_block(k, _):
@@ -360,19 +396,64 @@
         weight_grad(wbuf.at[lax.rem(k, 2)], first_degree(block_at(k, -way), 1 - core))
         pair_copy(k).start()
         block = block_at(k, way)
-        weight_grad(mine.at[block], first_degree(block, core))
+        weight_grad(work.at[pl.ds(block * block_rows, block_rows)], first_degree(block, core))
         return 0
 
     lax.fori_loop(0, chips, weight_block, 0)
     pair_copy(chips - 2).wait_send()
     pair_copy(chips - 1).wait_send()
+    own_copy.wait()
+    packs[core, chip] = (own[core].astype(F32) + other[...].astype(F32)).astype(BF16)
+
+    pltpu.make_async_copy(band, band, band_sem).wait()
+    qs[...] = jnp.zeros_like(qs)
+    span = cmat.shape[2]
+    mine_t = (lax.broadcasted_iota(jnp.int32, (8, lats), 1) == me * tl + lax.broadcasted_iota(jnp.int32, (8, lats), 0))
+    mine_t &= lax.broadcasted_iota(jnp.int32, (8, lats), 0) < tl
+    mine_t = jnp.where(mine_t, 1.0, 0.0).astype(BF16)
+
+    def tabulate(d, _):
+        z, of_core = lax.div(d, 2), lax.rem(d, 2)
+        row = lax.broadcasted_iota(jnp.int32, (n, span), 0)
+        p = jnp.where(of_core == 0, row - z, row + 1)
+        target = jnp.where(p > held - 1, p + 1, p)
+        moved = jnp.where(target == lax.broadcasted_iota(jnp.int32, (n, span), 1), 1.0, 0.0).astype(BF16)
+        picked = dot(mine_t, band[d].astype(BF16), ((1,), (1,))).astype(BF16)
+        cmat[z, pl.ds(pl.multiple_of(of_core * 8, 8), 8), :] = dot(picked, moved)
+        return 0
+
+    lax.fori_loop(0, n, tabulate, 0)
+
+    def apply_top(ch, z):
+        for h in range(2):
+            qs[pl.ds(h * held * tile, held * tile), :] = packs[h, z, 2, ch].reshape(held * tile, chans).astype(F32)
+        for k in range(tile):
+            xb[0:span, k * chans:(k + 1) * chans] = qs[pl.ds(k, span, stride=tile), :].astype(BF16)
+        out = dot(cmat[z].astype(BF16), xb[0:span, :])
+        for k in range(tile):
+            gather[pl.ds(k, 16, stride=tile), :] = out[:, k * chans:(k + 1) * chans]
+        for c in range(2):
+            for t in range(tl):
+                recv[1, ch, 2 * z + c, t, pl.ds(rows - tile, tile)] = gather[
+                    pl.ds((8 * c + t) * tile, tile), :].astype(BF16)
+
+    def low_degree(l):
+        def one(z, _):
+            for c in range(2):
+                p = l - z if c == 0 else l + 1
+                ours = p >= 0 if c == 0 else p >= n - z
+                p = jnp.maximum(p, 0)
+                h = jnp.where(p > held - 1, 1, 0)
+                for which in range(2):
+                    lowx[which, 2 * z + c] = only(ours, packs[h, z, which, :, p - h * (held - 1)])
+            return 0
+
+        lax.fori_loop(0, chips, one, 0)
+        outer(wbuf.at[0], 0, [(lowx[1].reshape(-1, chans), lowx[0].reshape(-1, chans))])
+        dw_out[pl.ds(l * wide, wide)] = wbuf[0, pl.ds(0, wide)]
 
     def final_rows(unit):
         ch, t = unit_of(unit)
-
-        @pl.when(t == 0)
-        def _():
-            arrived(3, ch)
 
         step_in(dg_hbm, unit)
         buf = lax.rem(unit, 2)
@@ -387,21 +468,20 @@
     def place(i, of_core):
         block = block_at(lax.div(i, pieces), way)
         start = lax.rem(i, pieces) * piece
-        return block, pl.ds(start, piece), pl.ds(first_degree(block, of_core) * wide + start, piece)
+        return pl.ds(block * block_rows + start, piece), pl.ds(first_degree(block, of_core) * wide + start, piece)
 
     def rs_copy(i):
-        block, part, there = place(i, core)
-        return to(onward, mine.at[block, part], dw_out.at[there], rs_send, rs_recv.at[i])
+        here, there = place(i, core)
+        return to(onward, work.at[here], dw_out.at[there], rs_send, rs_recv.at[i])
 
     def add_pair(i):
-        block, part, _ = place(i, core)
-        _, _, passed = place(i, 1 - core)
+        here, passed = place(i, 1 - core)
 
         @pl.when(lax.rem(i, pieces) == 0)
         def _():
             pair_copy(lax.div(i, pieces)).wait_recv()
 
-        mine[block, part] += dw_out[passed]
+        work[here] += dw_out[passed]
 
     def rs_step(i, _):
         add_pair(i)
@@ -409,102 +489,104 @@
         @pl.when(i >= pieces)
         def _():
             rs_copy(i - pieces).wait_recv()
-            block, part, there = place(i, core)
-            mine[block, part] += dw_out[there]
+            here, there = place(i, core)
+            work[here] += dw_out[there]
 
         rs_copy(i).start()
 
-        @pl.when(i < units)
-        def _():
-            final_rows(i)
+        @pl.when(lax.rem(i, pieces) == 0)
+        def _():
+            k = lax.div(i, pieces)
+
+            @pl.when(k > 0)
+            def _():
+                pack_copy(k - 1).wait_recv()
+
+            pack_copy(k).start()
+            share(k)
 
         return 0
 
     lax.fori_loop(0, hops, rs_step, 0)
+    pack_copy(chips - 2).wait_recv()
+    share(chips - 1)
 
     def own_sum(s, _):
         i = hops + s
         add_pair(i)
         rs_copy(i - pieces).wait_recv()
-        block, part, there = place(i, core)
-        dw_out[there] += mine[block, part]
+        here, there = place(i, core)
+        dw_out[there] += work[here]
         return 0
 
     lax.fori_loop(0, pieces, own_sum, 0)
     pl.semaphore_signal(free_sem, inc=1, device_id={axis: sibling}, device_id_type=pl.DeviceIdType.MESH)
 
-    for which in range(2):
-        others = low.at[which, pl.ds(0, n - 1)]
-        pltpu.make_async_copy(others, others, low_recv.at[which]).wait()
-    outer(wbuf.at[0], 0, [(low[1].reshape(-1, chans), low[0].reshape(-1, chans))])
-    dw_out[pl.ds(me * wide, wide)] = wbuf[0, pl.ds(0, wide)]
-
-    def spot(i):
-        return pl.ds(first_degree(block_at(lax.div(i, pieces), way), core) * wide + lax.rem(i, pieces) * piece, piece)
-
-    def low_spot(k):
-        return pl.ds((2 * block_at(k, way) + core) * wide, wide)
-
-    def ag_copy(rows_out, got):
-        return to(onward, dw_out.at[rows_out], dw_out.at[rows_out], ag_send, got)
-
-    def publish(rows_out):
-        to(sibling, dw_out.at[rows_out], dw_out.at[rows_out], pub_send, pub_recv).start()
+    def ag_copy(i, got):
+        _, there = place(i, core)
+        return to(onward, dw_out.at[there], dw_out.at[there], ag_send, ag_recv.at[got])
+
+    def publish(i):
+        _, there = place(i, core)
+        to(sibling, dw_out.at[there], dw_out.at[there], pub_send, pub_recv).start()
 
     pl.semaphore_wait(free_sem, 1)
 
     def own_piece(s, _):
-        rows_out = spot(hops + s)
-        ag_copy(rows_out, ag_recv.at[s]).start()
-        publish(rows_out)
+        ag_copy(hops + s, s).start()
+        publish(hops + s)
         return 0
 
     lax.fori_loop(0, pieces, own_piece, 0)
-    ag_copy(low_spot(chips - 1), ag_recv.at[hops]).start()
-    publish(low_spot(chips - 1))
+    gathered = packs.at[1 - core]
+    pltpu.make_async_copy(gathered, gathered, share_recv).wait()
+
+    def task(i):
+        @pl.when(i < chips)
+        def _():
+            for ch in range(chunks):
+                @pl.when(i == 0)
+                def _():
+                    arrived(3, ch)
+                apply_top(ch, i)
+
+        @pl.when((i >= chips) & (i < chips + units))
+        def _():
+            final_rows(i - chips)
+
+        @pl.when(i < n)
+        def _():
+            low_degree(i)
 
     def ag_step(i, _):
-        rows_out = spot(i)
-        ag_copy(rows_out, ag_recv.at[i]).wait_recv()
+        ag_copy(i, i).wait_recv()
 
         @pl.when(i + pieces < hops)
         def _():
-            ag_copy(rows_out, ag_recv.at[i + pieces]).start()
-
-        publish(rows_out)
-
-        @pl.when(lax.rem(i, pieces) == pieces - 1)
-        def _():
-            k = lax.div(i, pieces)
-            low_out = low_spot(k)
-            ag_copy(low_out, ag_recv.at[hops + k]).wait_recv()
-
-            @pl.when(k < chips - 2)
-            def _():
-                ag_copy(low_out, ag_recv.at[hops + k + 1]).start()
-
-            publish(low_out)
-
+            ag_copy(i, i + pieces).start()
+
+        publish(i)
+        task(i)
         return 0
 
     lax.fori_loop(0, hops, ag_step, 0)
 
-    def rest(unit, _):
-        final_rows(unit)
-        return 0
-
-    lax.fori_loop(min(hops, units), units, rest, 0)
-
-    for index in range(4 * chunks - SEND_SLOTS, 4 * chunks):
-        wait_sent(index)
-    sent = mine.at[pl.ds(0, chips - 1)]
+    def rest(i, _):
+        task(i)
+        return 0
+
+    lax.fori_loop(hops, max(hops, chips + units, n), rest, 0)
+
+    wait_sent(3 * chunks - 1)
+    for ch in range(chunks):
+        wait_sent(3 * chunks + ch, 3)
+    sent = work.at[pl.ds(0, (chips - 1) * block_rows)]
     pltpu.make_async_copy(sent, sent, rs_send).wait()
-    sent = dw_out.at[pl.ds(0, (chips - 1) * (half + 1) * wide)]
     pltpu.make_async_copy(sent, sent, ag_send).wait()
-    for which in range(2):
-        others = low.at[which, pl.ds(0, n - 1)]
-        pltpu.make_async_copy(others, others, low_send.at[which]).wait()
-    shared = dw_out.at[pl.ds(0, degs // 2 * wide)]
+    sent = packs.at[0, pl.ds(0, chips - 1)]
+    pltpu.make_async_copy(sent, sent, pack_send).wait()
+    pltpu.make_async_copy(packs.at[0], packs.at[0], share_send).wait()
+    shared = dw_out.at[pl.ds(0, chips * block_rows)]
     pltpu.make_async_copy(shared, shared, pub_send).wait()
     pltpu.make_async_copy(shared, shared, pub_recv).wait()
 
@@ -524,11 +606,14 @@
         half = degs // n - 1
         pieces = 4 if half * 2 * chans % 32 == 0 else 1
         hops = (n // 2 - 1) * pieces
+        per = 4
+        held = n // 2 + 1
+        packed = (3, chunks, held, 2 * nb, chans)
         tables = fourier_tables(n, ml, lons)
         anywhere = pl.BlockSpec(memory_space=pl.ANY)
         vmem = pl.BlockSpec(memory_space=pltpu.VMEM)
         grad_field, grad_w = pl.pallas_call(
-            functools.partial(layer_kernel, 'lat', n, nb, pieces),
+            functools.partial(layer_kernel, 'lat', n, nb, pieces, per),
             name='layer',
             out_shape=(
                 pltpu.VMEM((batch, tl, lons, chans), F32),
@@ -539,33 +624,42 @@
             scratch_shapes=[
                 pltpu.VMEM((2, chunks, n, tl, rows, chans), BF16),
                 pltpu.VMEM((SEND_SLOTS, n, tl, rows, chans), BF16),
-                pltpu.VMEM((lats * pitch, chans), F32),
-                pltpu.VMEM((lats * pitch, chans), F32),
+                pltpu.VMEM((max(2 * lats * pitch, n // 2 * half * 2 * chans), chans), F32),
                 pltpu.VMEM((lats, 2 * nb * chans), BF16),
                 pltpu.VMEM((degs, chunks, rows, chans), BF16),
                 pltpu.VMEM((degs, chunks, rows, chans), BF16),
                 pltpu.VMEM((degs, 2 * chans, chans), BF16),
-                pltpu.VMEM((2, 8 * 2 * chans, chans), F32),
+                pltpu.VMEM((2, max(per, half) * 2 * chans, chans), F32),
                 pltpu.VMEM((2, nb, lons, chans), F32),
                 pltpu.VMEM((n * rows, chans), F32),
                 pltpu.VMEM((2, ml, degs, lats), F32),
                 pltpu.VMEM((2, ml, degs, lats), BF16),
-                pltpu.VMEM((n // 2, half * 2 * chans, chans), F32),
+                pltpu.VMEM((n, n, lats), F32),
+                pltpu.VMEM((n // 2, 16, 32), F32),
+                pltpu.VMEM((32 * 2 * nb, chans), F32),
+                pltpu.VMEM((2,) + packed, BF16),
+                pltpu.VMEM(packed, BF16),
+                pltpu.VMEM((2, n // 2) + packed, BF16),
                 pltpu.VMEM((2, n, chunks, 2 * nb, chans), BF16),
                 pltpu.SemaphoreType.DMA((4 * chunks,)),
                 pltpu.SemaphoreType.DMA((4 * chunks,)),
                 pltpu.SemaphoreType.DMA((2,)),
                 pltpu.SemaphoreType.DMA((2,)),
                 pltpu.SemaphoreType.DMA((2,)),
+                pltpu.SemaphoreType.DMA,
                 pltpu.SemaphoreType.DMA((2,)),
                 pltpu.SemaphoreType.DMA((n // 2,)),
                 pltpu.SemaphoreType.DMA,
                 pltpu.SemaphoreType.DMA((hops,)),
                 pltpu.SemaphoreType.DMA,
-                pltpu.SemaphoreType.DMA((hops + n // 2 - 1,)),
-                pltpu.SemaphoreType.DMA((2,)),
-                pltpu.SemaphoreType.DMA((2,)),
+                pltpu.SemaphoreType.DMA((hops,)),
                 pltpu.SemaphoreType.REGULAR,
+                pltpu.SemaphoreType.DMA,
+                pltpu.SemaphoreType.DMA,
+                pltpu.SemaphoreType.DMA,
+                pltpu.SemaphoreType.DMA,
+                pltpu.SemaphoreType.DMA,
+                pltpu.SemaphoreType.DMA((n // 2 - 1,)),
                 pltpu.SemaphoreType.DMA,
                 pltpu.SemaphoreType.DMA,
             ],

time: 447 us -> 430 us (0.962)
  Pallas kernels: 437 us -> 421 us
    pallas_call x1, Pallas kernels: 437 us -> 421 us  [local_step(): pl.pallas_call(functools.partial(layer_kernel, 'lat', n, nb, pieces, per)...]
where the time goes in v4:
time: 430 us; the launch traced here: 429 us
  Pallas kernels  421 us (98%)
  local copies, waits for them, and re-layouts  7.74 us (2%)
    pallas_call x1, Pallas kernels, local_step(): pl.pallas_call(functools.partial(layer_kernel, 'lat', n, nb, pieces, per)...  421 us

profile of v4, /device:TPU:21, one launch (start us, length us, event | category | flops | bytes accessed | tf_op | source)
XLA Modules:
  0.0 429.4 jit_solution(15935222487933689605)
XLA Ops:
  0.6 421.0 %layer.1 = (f32[12,6,192,128]{3,2,1,0:T(8,128)S(1)}, f32[24576,128]{1,0:T(8,128)S(1)}) custom-call(f32[12,6,192,128]{3,2,1,0:T(8,128)} %bitcast.12, f32[12,6,192,128]{3,2,1,0:T(8,128)} %bitcast.13, f32[24576,128]{1,0:T(8,128)} %bitcast.11, f32[96,96,96]{2,1,0:T(8,128)} %pf_hbm.1, f32[96,96,96]{2,1,0:T(8,128)} %pv_hbm.1, ...), custom_call_target="tpu_custom_call" | custom-call | tf_op jit(solution)/shard_map/layer/pallas_call | solution.py:615
  421.7 3.0 copy.17
  424.6 4.8 %copy.18 = f32[96,128,128,2]{2,3,1,0:T(2,128)} copy(f32[96,128,128,2]{2,3,1,0:T(2,128)S(1)} %bitcast.9) | data formatting | bytes 25165824

commit v5 on v4

--- a/solution.py
+++ b/solution.py
@@ -517,10 +517,8 @@
         rs_copy(i - pieces).wait_recv()
         here, there = place(i, core)
         dw_out[there] += work[here]
-        return 0
-
-    lax.fori_loop(0, pieces, own_sum, 0)
-    pl.semaphore_signal(free_sem, inc=1, device_id={axis: sibling}, device_id_type=pl.DeviceIdType.MESH)
+        ag_copy(i, s).start()
+        return 0
 
     def ag_copy(i, got):
         _, there = place(i, core)
@@ -530,10 +528,12 @@
         _, there = place(i, core)
         to(sibling, dw_out.at[there], dw_out.at[there], pub_send, pub_recv).start()
 
+    lax.fori_loop(0, pieces, own_sum, 0)
+
+    pl.semaphore_signal(free_sem, inc=1, device_id={axis: sibling}, device_id_type=pl.DeviceIdType.MESH)
     pl.semaphore_wait(free_sem, 1)
 
     def own_piece(s, _):
-        ag_copy(hops + s, s).start()
         publish(hops + s)
         return 0
 
@@ -589,6 +589,19 @@
     shared = dw_out.at[pl.ds(0, chips * block_rows)]
     pltpu.make_async_copy(shared, shared, pub_send).wait()
     pltpu.make_async_copy(shared, shared, pub_recv).wait()
+
+
+def put_kernel(df_ref, dw_ref, df_hbm, dw_hbm, sems):
+    copies = []
+    for source, target, parts in ((df_ref, df_hbm, 3), (dw_ref, dw_hbm, 4)):
+        size = source.shape[0] // parts
+        for k in range(parts):
+            part = pl.ds(k * size, size)
+            copies.append(pltpu.make_async_copy(source.at[part], target.at[part], sems.at[len(copies)]))
+    for copy in copies:
+        copy.start()
+    for copy in copies:
+        copy.wait()
 
 
 def solution(mesh):
@@ -669,6 +682,18 @@
             field_loc.transpose(0, 2, 3, 1), grad_loc.transpose(0, 2, 3, 1),
             w_mix.transpose(0, 1, 3, 2).reshape(degs * 2 * chans, chans),
             p_fwd, p_inv, *tables)
+        grad_field, grad_w = pl.pallas_call(
+            put_kernel,
+            name='put',
+            out_shape=(
+                jax.ShapeDtypeStruct(grad_field.shape, F32),
+                jax.ShapeDtypeStruct(grad_w.shape, F32),
+            ),
+            in_specs=[vmem] * 2,
+            out_specs=(anywhere, anywhere),
+            scratch_shapes=[pltpu.SemaphoreType.DMA((7,))],
+            compiler_params=pltpu.CompilerParams(vmem_limit_bytes=1024 * 1024),
+        )(grad_field, grad_w)
         return grad_field.transpose(0, 3, 1, 2), grad_w.reshape(degs, chans, 2, chans).transpose(0, 1, 3, 2)
 
     return jax.shard_map(

time: 430 us -> 426 us (level)
  local copies, waits for them, and re-layouts: 7.74 us -> 0 us
    unnamed x2 -> x0, local copies, waits for them, and re-layouts: 7.74 us -> none
    pallas_call x1, Pallas kernels: 421 us -> 414 us  [local_step(): pl.pallas_call(functools.partial(layer_kernel, 'lat', n, nb, pieces, per)...]
    pallas_call x0 -> x1, Pallas kernels: none -> 6.83 us  [local_step(): pl.pallas_call(put_kernel, name='put', out_shape=(jax.ShapeDtypeStruct(gr...]
where the time goes in v5:
time: 426 us; the launch traced here: 421 us
  Pallas kernels  421 us (99%)
    pallas_call x1, Pallas kernels, local_step(): pl.pallas_call(functools.partial(layer_kernel, 'lat', n, nb, pieces, per)...  414 us

profile of v5, /device:TPU:21, one launch (start us, length us, event | category | flops | bytes accessed | tf_op | source)
XLA Modules:
  0.0 421.5 jit_solution(16536429713425942865)
XLA Ops:
  0.6 414.0 %layer.1 = (f32[12,6,192,128]{3,2,1,0:T(8,128)S(1)}, f32[24576,128]{1,0:T(8,128)S(1)}) custom-call(f32[12,6,192,128]{3,2,1,0:T(8,128)} %bitcast.10, f32[12,6,192,128]{3,2,1,0:T(8,128)} %bitcast.11, f32[24576,128]{1,0:T(8,128)} %bitcast.9, f32[96,96,96]{2,1,0:T(8,128)} %pf_hbm.1, f32[96,96,96]{2,1,0:T(8,128)} %pv_hbm.1, ...), custom_call_target="tpu_custom_call" | custom-call | tf_op jit(solution)/shard_map/layer/pallas_call | solution.py:628
  414.7 6.8 %put.1 = (f32[12,6,192,128]{3,2,1,0:T(8,128)}, f32[24576,128]{1,0:T(8,128)}) custom-call(f32[12,6,192,128]{3,2,1,0:T(8,128)S(1)} %get-tuple-element.6.df_ref, f32[24576,128]{1,0:T(8,128)S(1)} %get-tuple-element.7.dw_ref), custom_call_target="tpu_custom_call" | custom-call | tf_op jit(solution)/shard_map/put/pallas_call | solution.py:685

commit v6 on v5

--- a/solution.py
+++ b/solution.py
@@ -11,7 +11,6 @@
 
 F32 = jnp.float32
 BF16 = jnp.bfloat16
-SEND_SLOTS = 4
 
 
 def split_const(matrix):
@@ -30,7 +29,7 @@
     gains = np.repeat(np.where(order == 0, 1.0, 2.0), 2)[:, None]
     doubled = forward * gains
     tables = split_const(forward) + split_const(doubled) + split_const(doubled.T) + split_const(forward.T)
-    return [jnp.asarray(t) for t in tables]
+    return jnp.stack([jnp.asarray(t) for t in tables])
 
 
 def gelu_grad(values):
@@ -45,12 +44,12 @@
 
 def layer_kernel(
     axis, n, nb, pieces, per,
-    f_hbm, dg_hbm, w_hbm, pf_hbm, pv_hbm,
-    fwd_h, fwd_l, dbl_h, dbl_l, syn_h, syn_l, adj_h, adj_l,
+    f_hbm, dg_hbm, w_hbm, pf_hbm, pv_hbm, tab_hbm,
     df_out, dw_out,
-    recv, send, work, xb, coef, dq, vmix, wbuf, inbuf, gather, pbuf, pmat, band, cmat, qs, own, other, packs, lowx,
+    recv, send, work, xb, coef, dq, vmix, wbuf, inbuf, gather, pbuf, pmat, band, cmat, qs, own, other, packs, lowx, tab,
     send_sem, recv_sem, in_sem, w_sem, p_sem, band_sem, pair_send, pair_recv, rs_send, rs_recv, ag_send, ag_recv,
     free_sem, pub_send, pub_recv, own_send, own_recv, pack_send, pack_recv, share_send, share_recv,
+    tab_sem, top_send, near_recv, far_recv, swap_send, swap_recv,
 ):
     me = lax.axis_index(axis)
     batch, tl, lons, chans = f_hbm.shape
@@ -61,6 +60,8 @@
     pitch = rows + 1
     modes2 = 2 * n * ml
     units = chunks * tl
+    slots = chunks + 1
+    fwd_h, fwd_l, dbl_h, dbl_l, syn_h, syn_l, adj_h, adj_l = (tab.at[k] for k in range(8))
     area = lats * pitch
     top = n * (ml - 1)
     held = n // 2 + 1
@@ -79,14 +80,6 @@
             src_ref=src, dst_ref=dst, send_sem=sent, recv_sem=got,
             device_id={axis: device}, device_id_type=pl.DeviceIdType.MESH)
 
-    barrier = pltpu.get_barrier_semaphore()
-
-    def announce(k, _):
-        pl.semaphore_signal(barrier, inc=1, device_id={axis: lax.rem(me + k, n)}, device_id_type=pl.DeviceIdType.MESH)
-        return 0
-
-    lax.fori_loop(1, n, announce, 0)
-
     def unit_of(unit):
         return lax.div(unit, tl), lax.rem(unit, tl)
 
@@ -102,11 +95,11 @@
         unit_in(src, unit).wait()
 
     def sent_rows(stage):
-        return pl.ds(0, rows - tile if stage == 3 else rows)
+        return pl.ds(0, rows - tile if stage % 2 else rows)
 
     def ship(stage, ch, t0, nt):
         index = stage * chunks + ch
-        slot = lax.rem(index, SEND_SLOTS)
+        slot = lax.rem(index, slots)
         part, span = pl.ds(t0, nt), sent_rows(stage)
 
         def one(k, _):
@@ -122,18 +115,21 @@
         others = recv.at[stage % 2, ch, pl.ds(0, n - 1), :, sent_rows(stage)]
         pltpu.make_async_copy(others, others, recv_sem.at[stage * chunks + ch]).wait()
 
-    def wait_sent(index, stage=0):
-        others = send.at[lax.rem(index, SEND_SLOTS), pl.ds(0, n - 1), :, sent_rows(stage)]
+    def wait_sent(index, stage):
+        others = send.at[lax.rem(index, slots), pl.ds(0, n - 1), :, sent_rows(stage)]
         pltpu.make_async_copy(others, others, send_sem.at[index]).wait()
 
     def free_slot(stage, ch):
         index = stage * chunks + ch
-
-        @pl.when(index >= SEND_SLOTS)
-        def _():
-            wait_sent(index - SEND_SLOTS)
-
-        return lax.rem(index, SEND_SLOTS)
+        if stage >= 1:
+            @pl.when(ch >= 1)
+            def _():
+                wait_sent(index - slots, stage - 1)
+        if stage >= 2:
+            @pl.when(ch == 0)
+            def _():
+                wait_sent(index - slots, stage - 2)
+        return lax.rem(index, slots)
 
     def put_rows(slot, t):
         send[slot, :, t] = gather[...].reshape(n, rows, chans).astype(BF16)
@@ -144,15 +140,31 @@
         return dot(head[...], high) + (dot(tail[...], high) + dot(head[...], low))
 
     unit_in(f_hbm, 0).start()
+    first_tables = pltpu.make_async_copy(tab_hbm.at[pl.ds(0, 2)], tab.at[pl.ds(0, 2)], tab_sem.at[0])
+    other_tables = pltpu.make_async_copy(tab_hbm.at[pl.ds(2, 6)], tab.at[pl.ds(2, 6)], tab_sem.at[1])
+    first_tables.start()
+    barrier = pltpu.get_barrier_semaphore()
+
+    def announce(k, _):
+        pl.semaphore_signal(barrier, inc=1, device_id={axis: lax.rem(me + k, n)}, device_id_type=pl.DeviceIdType.MESH)
+        return 0
+
+    lax.fori_loop(1, n, announce, 0)
+
     for which, source in enumerate((pf_hbm, pv_hbm)):
         for k in range(ml):
             pltpu.make_async_copy(source.at[first_mode(me) + n * k], pbuf.at[which, k], p_sem.at[which]).start()
 
+    other_tables.start()
+
     def band_in(d, _):
-        pltpu.make_async_copy(pf_hbm.at[top + first_mode(d), pl.ds(top, n)], band.at[d], band_sem).start()
+        for which, source in enumerate((pf_hbm, pv_hbm)):
+            pltpu.make_async_copy(
+                source.at[top + first_mode(d), pl.ds(top, n)], band.at[which, d], band_sem.at[which]).start()
         return 0
 
     lax.fori_loop(0, n, band_in, 0)
+    first_tables.wait()
 
     group = 2 if tl % 2 == 0 else 1
 
@@ -173,6 +185,15 @@
             return 0
 
         lax.fori_loop(0, tl // group, part, 0)
+
+    parts = degs // per
+    depth = min(parts, work.shape[0] // (per * 2 * chans))
+
+    def w_in(k):
+        slot = lax.rem(k, depth)
+        return pltpu.make_async_copy(
+            w_hbm.at[pl.ds(k * per * 2 * chans, per * 2 * chans)],
+            work.at[pl.ds(slot * per * 2 * chans, per * 2 * chans)], w_sem.at[slot])
 
     def step1_chunk(ch, _):
         def row(slot, t):
@@ -187,6 +208,12 @@
             put_rows(slot, t)
 
         by_rows(0, ch, row)
+
+        @pl.when(ch == 0)
+        def _():
+            for k in range(depth):
+                w_in(k).start()
+
         return 0
 
     lax.fori_loop(0, chunks, step1_chunk, 0)
@@ -194,28 +221,44 @@
     for which in range(2):
         pltpu.make_async_copy(pbuf.at[which], pbuf.at[which], p_sem.at[which]).wait()
     pmat[...] = pbuf[...].astype(BF16)
-
-    parts = degs // per
-
-    def w_in(k):
-        slot = lax.rem(k, 2)
-        return pltpu.make_async_copy(w_hbm.at[pl.ds(k * per * 2 * chans, per * 2 * chans)], wbuf.at[slot, pl.ds(0, per * 2 * chans)], w_sem.at[slot])
-
-    w_in(0).start()
+    other_tables.wait()
 
     def load_w(k, _):
-        @pl.when(k + 1 < parts)
-        def _():
-            w_in(k + 1).start()
         w_in(k).wait()
-        slot = lax.rem(k, 2)
+        base = lax.rem(k, depth) * per * 2 * chans
         for j in range(per):
             for part in range(2):
-                vmix[k * per + j, pl.ds(part * chans, chans)] = wbuf[
-                    slot, pl.ds(j * 2 * chans + part, chans, stride=2), :].astype(BF16)
+                vmix[k * per + j, pl.ds(part * chans, chans)] = work[
+                    pl.ds(base + j * 2 * chans + part, chans, stride=2), :].astype(BF16)
+
+        @pl.when(k + depth < parts)
+        def _():
+            w_in(k + depth).start()
+
         return 0
 
     lax.fori_loop(0, parts, load_w, 0)
+
+    for which in range(2):
+        pltpu.make_async_copy(band.at[which], band.at[which], band_sem.at[which]).wait()
+    qs[...] = jnp.zeros_like(qs)
+    span = cmat.shape[3]
+    mine_t = (lax.broadcasted_iota(jnp.int32, (8, lats), 1) == me * tl + lax.broadcasted_iota(jnp.int32, (8, lats), 0))
+    mine_t &= lax.broadcasted_iota(jnp.int32, (8, lats), 0) < tl
+    mine_t = jnp.where(mine_t, 1.0, 0.0).astype(BF16)
+
+    def tabulate(d, _):
+        z, of_core = lax.div(d, 2), lax.rem(d, 2)
+        row = lax.broadcasted_iota(jnp.int32, (n, span), 0)
+        p = jnp.where(of_core == 0, row - z, row + 1)
+        target = jnp.where(p > held - 1, p + 1, p)
+        moved = jnp.where(target == lax.broadcasted_iota(jnp.int32, (n, span), 1), 1.0, 0.0).astype(BF16)
+        for which in range(2):
+            picked = dot(mine_t, band[which, d].astype(BF16), ((1,), (1,))).astype(BF16)
+            cmat[which, z, pl.ds(pl.multiple_of(of_core * 8, 8), 8), :] = dot(picked, moved)
+        return 0
+
+    lax.fori_loop(0, n, tabulate, 0)
 
     sign = jnp.where(lax.broadcasted_iota(jnp.int32, (tile, chans), 0) < nb, -1.0, 1.0).astype(F32)
 
@@ -277,14 +320,54 @@
             return 0
 
         lax.fori_loop(0, degs, degree, 0, unroll=2)
-        if stage == 3:
-            def keep_top(half_at, row, degree, ours):
-                own[half_at, 2, ch, row] = only(ours, work[pl.ds((top + degree) * pitch + rows - tile, tile), :])
-
-            pack(keep_top)
+
+        def keep_top(half_at, row, degree, ours):
+            own[half_at, 2, ch, row] = only(ours, work[pl.ds((top + degree) * pitch + rows - tile, tile), :])
+
+        pack(keep_top)
+        if stage == 1:
+            swap = to(sibling, own.at[1 - core, 2, ch], other.at[2, ch], swap_send.at[ch], swap_recv.at[ch])
+            swap.start()
         legendre(0, area, 1 - into, 0)
         load(free_slot(stage, ch))
+        if stage == 1:
+            swap.wait()
+            packs[core, chip, 2, ch] = (own[core, 2, ch].astype(F32) + other[2, ch].astype(F32)).astype(BF16)
+
+            @pl.when(ch >= 2)
+            def _():
+                relay_top(ch - 2)
+
+            for away in (2, -2):
+                top_copy(0, away, ch, near_recv).start()
         ship(stage, ch, 0, tl)
+
+    def top_copy(source, away, ch, got):
+        block = packs.at[core, lax.rem(chip + source + chips, chips), 2, ch]
+        return to(2 * lax.rem(chip + away + chips, chips) + core, block, block, top_send, got.at[ch])
+
+    def top_blocks(count, ch):
+        return packs.at[core, pl.ds(0, count), 2, ch]
+
+    def relay_top(ch):
+        pltpu.make_async_copy(top_blocks(2, ch), top_blocks(2, ch), near_recv.at[ch]).wait()
+        for source in (2, -2):
+            for away in (1, -1):
+                top_copy(source, away, ch, far_recv).start()
+        top_copy(-2 * way, 2 * way, ch, far_recv).start()
+
+    def apply_top(which, ch, z):
+        for h in range(2):
+            qs[pl.ds(h * held * tile, held * tile), :] = packs[h, z, 2, ch].reshape(held * tile, chans).astype(F32)
+        for k in range(tile):
+            xb[0:span, k * chans:(k + 1) * chans] = qs[pl.ds(k, span, stride=tile), :].astype(BF16)
+        out = dot(cmat[which, z].astype(BF16), xb[0:span, :])
+        for k in range(tile):
+            gather[pl.ds(k, 16, stride=tile), :] = out[:, k * chans:(k + 1) * chans]
+        for c in range(2):
+            for t in range(tl):
+                recv[1, ch, 2 * z + c, t, pl.ds(rows - tile, tile)] = gather[
+                    pl.ds((8 * c + t) * tile, tile), :].astype(BF16)
 
     def mix_forward(l, x):
         both = dot(x, vmix[l], ((1,), (1,)))
@@ -300,6 +383,7 @@
         return 0
 
     lax.fori_loop(0, chunks, step2_chunk, 0)
+    relay_top(chunks - 2)
 
     def fetch_rows(stage, ch, t):
         for src in range(n):
@@ -311,6 +395,26 @@
 
     def step3_chunk(ch, _):
         arrived(1, ch)
+        pltpu.make_async_copy(top_blocks(5, ch), top_blocks(5, ch), far_recv.at[ch]).wait()
+        swap = to(sibling, top_blocks(chips, ch), top_blocks(chips, ch), swap_send.at[ch], swap_recv.at[ch])
+        swap.start()
+
+        @pl.when(ch == 0)
+        def _():
+            relay_top(chunks - 1)
+
+        swap.wait()
+
+        @pl.when(ch == chunks - 1)
+        def _():
+            all_sent = packs.at[0, pl.ds(0, 7), 2]
+            pltpu.make_async_copy(all_sent, all_sent, top_send).wait()
+
+        def apply(z, _):
+            apply_top(1, ch, z)
+            return 0
+
+        lax.fori_loop(0, chips, apply, 0)
 
         def row(slot, t):
             unit = ch * tl + t
@@ -405,38 +509,6 @@
     own_copy.wait()
     packs[core, chip] = (own[core].astype(F32) + other[...].astype(F32)).astype(BF16)
 
-    pltpu.make_async_copy(band, band, band_sem).wait()
-    qs[...] = jnp.zeros_like(qs)
-    span = cmat.shape[2]
-    mine_t = (lax.broadcasted_iota(jnp.int32, (8, lats), 1) == me * tl + lax.broadcasted_iota(jnp.int32, (8, lats), 0))
-    mine_t &= lax.broadcasted_iota(jnp.int32, (8, lats), 0) < tl
-    mine_t = jnp.where(mine_t, 1.0, 0.0).astype(BF16)
-
-    def tabulate(d, _):
-        z, of_core = lax.div(d, 2), lax.rem(d, 2)
-        row = lax.broadcasted_iota(jnp.int32, (n, span), 0)
-        p = jnp.where(of_core == 0, row - z, row + 1)
-        target = jnp.where(p > held - 1, p + 1, p)
-        moved = jnp.where(target == lax.broadcasted_iota(jnp.int32, (n, span), 1), 1.0, 0.0).astype(BF16)
-        picked = dot(mine_t, band[d].astype(BF16), ((1,), (1,))).astype(BF16)
-        cmat[z, pl.ds(pl.multiple_of(of_core * 8, 8), 8), :] = dot(picked, moved)
-        return 0
-
-    lax.fori_loop(0, n, tabulate, 0)
-
-    def apply_top(ch, z):
-        for h in range(2):
-            qs[pl.ds(h * held * tile, held * tile), :] = packs[h, z, 2, ch].reshape(held * tile, chans).astype(F32)
-        for k in range(tile):
-            xb[0:span, k * chans:(k + 1) * chans] = qs[pl.ds(k, span, stride=tile), :].astype(BF16)
-        out = dot(cmat[z].astype(BF16), xb[0:span, :])
-        for k in range(tile):
-            gather[pl.ds(k, 16, stride=tile), :] = out[:, k * chans:(k + 1) * chans]
-        for c in range(2):
-            for t in range(tl):
-                recv[1, ch, 2 * z + c, t, pl.ds(rows - tile, tile)] = gather[
-                    pl.ds((8 * c + t) * tile, tile), :].astype(BF16)
-
     def low_degree(l):
         def one(z, _):
             for c in range(2):
@@ -548,7 +620,7 @@
                 @pl.when(i == 0)
                 def _():
                     arrived(3, ch)
-                apply_top(ch, i)
+                apply_top(0, ch, i)
 
         @pl.when((i >= chips) & (i < chips + units))
         def _():
@@ -577,7 +649,7 @@
 
     lax.fori_loop(hops, max(hops, chips + units, n), rest, 0)
 
-    wait_sent(3 * chunks - 1)
+    wait_sent(3 * chunks - 1, 2)
     for ch in range(chunks):
         wait_sent(3 * chunks + ch, 3)
     sent = work.at[pl.ds(0, (chips - 1) * block_rows)]
@@ -632,11 +704,11 @@
                 pltpu.VMEM((batch, tl, lons, chans), F32),
                 pltpu.VMEM((degs * 2 * chans, chans), F32),
             ),
-            in_specs=[anywhere] * 5 + [vmem] * len(tables),
+            in_specs=[anywhere] * 6,
             out_specs=(vmem, vmem),
             scratch_shapes=[
                 pltpu.VMEM((2, chunks, n, tl, rows, chans), BF16),
-                pltpu.VMEM((SEND_SLOTS, n, tl, rows, chans), BF16),
+                pltpu.VMEM((chunks + 1, n, tl, rows, chans), BF16),
                 pltpu.VMEM((max(2 * lats * pitch, n // 2 * half * 2 * chans), chans), F32),
                 pltpu.VMEM((lats, 2 * nb * chans), BF16),
                 pltpu.VMEM((degs, chunks, rows, chans), BF16),
@@ -647,19 +719,20 @@
                 pltpu.VMEM((n * rows, chans), F32),
                 pltpu.VMEM((2, ml, degs, lats), F32),
                 pltpu.VMEM((2, ml, degs, lats), BF16),
-                pltpu.VMEM((n, n, lats), F32),
-                pltpu.VMEM((n // 2, 16, 32), F32),
+                pltpu.VMEM((2, n, n, lats), F32),
+                pltpu.VMEM((2, n // 2, 16, 32), F32),
                 pltpu.VMEM((32 * 2 * nb, chans), F32),
                 pltpu.VMEM((2,) + packed, BF16),
                 pltpu.VMEM(packed, BF16),
                 pltpu.VMEM((2, n // 2) + packed, BF16),
                 pltpu.VMEM((2, n, chunks, 2 * nb, chans), BF16),
+                pltpu.VMEM(tables.shape, BF16),
                 pltpu.SemaphoreType.DMA((4 * chunks,)),
                 pltpu.SemaphoreType.DMA((4 * chunks,)),
                 pltpu.SemaphoreType.DMA((2,)),
+                pltpu.SemaphoreType.DMA((degs // per,)),
                 pltpu.SemaphoreType.DMA((2,)),
                 pltpu.SemaphoreType.DMA((2,)),
-                pltpu.SemaphoreType.DMA,
                 pltpu.SemaphoreType.DMA((2,)),
                 pltpu.SemaphoreType.DMA((n // 2,)),
                 pltpu.SemaphoreType.DMA,
@@ -675,13 +748,19 @@
                 pltpu.SemaphoreType.DMA((n // 2 - 1,)),
                 pltpu.SemaphoreType.DMA,
                 pltpu.SemaphoreType.DMA,
+                pltpu.SemaphoreType.DMA((2,)),
+                pltpu.SemaphoreType.DMA,
+                pltpu.SemaphoreType.DMA((chunks,)),
+                pltpu.SemaphoreType.DMA((chunks,)),
+                pltpu.SemaphoreType.DMA((chunks,)),
+                pltpu.SemaphoreType.DMA((chunks,)),
             ],
             compiler_params=pltpu.CompilerParams(
                 collective_id=0, has_side_effects=True, vmem_limit_bytes=42 * 1024 * 1024),
         )(
             field_loc.transpose(0, 2, 3, 1), grad_loc.transpose(0, 2, 3, 1),
             w_mix.transpose(0, 1, 3, 2).reshape(degs * 2 * chans, chans),
-            p_fwd, p_inv, *tables)
+            p_fwd, p_inv, tables)
         grad_field, grad_w = pl.pallas_call(
             put_kernel,
             name='put',

time: 426 us -> 419 us (0.984); the launches traced: 421 us -> 419 us
  no operation moved by 1% of the time
where the time goes in v6:
time: 419 us
  Pallas kernels  418 us (100%)
    pallas_call x1, Pallas kernels, local_step(): pl.pallas_call(functools.partial(layer_kernel, 'lat', n, nb, pieces, per)...  411 us

profile of v6, /device:TPU:21, one launch (start us, length us, event | category | flops | bytes accessed | tf_op | source)
XLA Modules:
  0.0 418.9 jit_solution(7516855475332309000)
XLA Ops:
  0.6 411.5 %layer.1 = (f32[12,6,192,128]{3,2,1,0:T(8,128)S(1)}, f32[24576,128]{1,0:T(8,128)S(1)}) custom-call(f32[12,6,192,128]{3,2,1,0:T(8,128)} %bitcast.10, f32[12,6,192,128]{3,2,1,0:T(8,128)} %bitcast.11, f32[24576,128]{1,0:T(8,128)} %bitcast.9, f32[96,96,96]{2,1,0:T(8,128)} %pf_hbm.1, f32[96,96,96]{2,1,0:T(8,128)} %pv_hbm.1, bf16[8,192,192]{2,1,0:T(8,128)(2,1)} %constant.34.tab_hbm), custom_call_target="tpu_custom_call" | custom-call | tf_op jit(solution)/shard_map/layer/pallas_call | solution.py:700
  412.1 6.8 %put.1 = (f32[12,6,192,128]{3,2,1,0:T(8,128)}, f32[24576,128]{1,0:T(8,128)}) custom-call(f32[12,6,192,128]{3,2,1,0:T(8,128)S(1)} %get-tuple-element.6.df_ref, f32[24576,128]{1,0:T(8,128)S(1)} %get-tuple-element.7.dw_ref), custom_call_target="tpu_custom_call" | custom-call | tf_op jit(solution)/shard_map/put/pallas_call | solution.py:764

commit v7 on v6

--- a/solution.py
+++ b/solution.py
@@ -38,6 +38,18 @@
     return cumulative + values * density
 
 
+def loop(stop, step, start=0, unroll=None):
+    def one(i, carry):
+        step(i)
+        return carry
+
+    lax.fori_loop(start, stop, one, 0, unroll=unroll)
+
+
+def head(size):
+    return pl.ds(0, size)
+
+
 def dot(a, b, dims=((1,), (0,))):
     return lax.dot_general(a, b, (dims, ((), ())), preferred_element_type=F32)
 
@@ -47,9 +59,11 @@
     f_hbm, dg_hbm, w_hbm, pf_hbm, pv_hbm, tab_hbm,
     df_out, dw_out,
     recv, send, work, xb, coef, dq, vmix, wbuf, inbuf, gather, pbuf, pmat, band, cmat, qs, own, other, packs, lowx, tab,
+    topin, partial, mid, sums, sumin, joined,
     send_sem, recv_sem, in_sem, w_sem, p_sem, band_sem, pair_send, pair_recv, rs_send, rs_recv, ag_send, ag_recv,
     free_sem, pub_send, pub_recv, own_send, own_recv, pack_send, pack_recv, share_send, share_recv,
     tab_sem, top_send, near_recv, far_recv, swap_send, swap_recv,
+    row_send, row_recv, mid_send, mid_recv, sum_send, sum_recv, join_send, join_recv,
 ):
     me = lax.axis_index(axis)
     batch, tl, lons, chans = f_hbm.shape
@@ -94,30 +108,53 @@
             unit_in(src, unit + 1).start()
         unit_in(src, unit).wait()
 
-    def sent_rows(stage):
-        return pl.ds(0, rows - tile if stage % 2 else rows)
+    body, peak = head(rows - tile), pl.ds(rows - tile, tile)
 
     def ship(stage, ch, t0, nt):
         index = stage * chunks + ch
         slot = lax.rem(index, slots)
-        part, span = pl.ds(t0, nt), sent_rows(stage)
-
-        def one(k, _):
+        part = pl.ds(t0, nt)
+
+        def one(k):
             peer = lax.rem(me + k, n)
-            to(peer, send.at[slot, peer, part, span], recv.at[stage % 2, ch, me, part, span],
+            to(peer, send.at[slot, peer, part, body], recv.at[stage % 2, ch, me, part, body],
                send_sem.at[index], recv_sem.at[index]).start()
-            return 0
-
-        lax.fori_loop(1, n, one, 0)
-        recv[stage % 2, ch, me, part, span] = send[slot, me, part, span]
+
+        loop(n, one, 1)
+        recv[stage % 2, ch, me, part, body] = send[slot, me, part, body]
 
     def arrived(stage, ch):
-        others = recv.at[stage % 2, ch, pl.ds(0, n - 1), :, sent_rows(stage)]
+        others = recv.at[stage % 2, ch, head(n - 1), :, body]
         pltpu.make_async_copy(others, others, recv_sem.at[stage * chunks + ch]).wait()
 
+    def peaks(count):
+        return topin.at[0, 0, head(count)]
+
     def wait_sent(index, stage):
-        others = send.at[lax.rem(index, slots), pl.ds(0, n - 1), :, sent_rows(stage)]
+        others = send.at[lax.rem(index, slots), head(n - 1), :, body]
         pltpu.make_async_copy(others, others, send_sem.at[index]).wait()
+        if stage % 2 == 0:
+            ch = index - stage * chunks
+            pltpu.make_async_copy(peaks(n - 3), peaks(n - 3), row_send.at[ch]).wait()
+
+    def send_peak(stage, ch):
+        slot = lax.rem(stage * chunks + ch, slots)
+        far = chips // 2
+        for same in (True, False):
+            its_core = core if same else 1 - core
+            for away in range(1 - far, far + 1):
+                place = (away > 0) - (away < 0)
+                hop, target = away - place, (0, 2, 1)[place]
+                if away == far:
+                    hop = jnp.where(its_core == 0, 1 - far, far - 1)
+                    target = jnp.where(its_core == 0, 1, 2)
+                owner = 2 * lax.rem(chip + away + chips, chips) + its_core
+                source = send.at[slot, owner, :, peak]
+                if same and away in (-1, 0, 1):
+                    topin[ch, target, me] = source[...]
+                else:
+                    to(2 * lax.rem(chip + hop + chips, chips) + its_core, source, topin.at[ch, target, me],
+                       row_send.at[ch], row_recv.at[ch]).start()
 
     def free_slot(stage, ch):
         index = stage * chunks + ch
@@ -140,16 +177,20 @@
         return dot(head[...], high) + (dot(tail[...], high) + dot(head[...], low))
 
     unit_in(f_hbm, 0).start()
-    first_tables = pltpu.make_async_copy(tab_hbm.at[pl.ds(0, 2)], tab.at[pl.ds(0, 2)], tab_sem.at[0])
+    first_tables = pltpu.make_async_copy(tab_hbm.at[head(2)], tab.at[head(2)], tab_sem.at[0])
     other_tables = pltpu.make_async_copy(tab_hbm.at[pl.ds(2, 6)], tab.at[pl.ds(2, 6)], tab_sem.at[1])
     first_tables.start()
+
+    def clear(ch):
+        topin[ch] = jnp.zeros(topin.shape[1:], BF16)
+
+    loop(chunks, clear)
     barrier = pltpu.get_barrier_semaphore()
 
-    def announce(k, _):
+    def announce(k):
         pl.semaphore_signal(barrier, inc=1, device_id={axis: lax.rem(me + k, n)}, device_id_type=pl.DeviceIdType.MESH)
-        return 0
-
-    lax.fori_loop(1, n, announce, 0)
+
+    loop(n, announce, 1)
 
     for which, source in enumerate((pf_hbm, pv_hbm)):
         for k in range(ml):
@@ -157,34 +198,15 @@
 
     other_tables.start()
 
-    def band_in(d, _):
+    def band_in(d):
         for which, source in enumerate((pf_hbm, pv_hbm)):
             pltpu.make_async_copy(
                 source.at[top + first_mode(d), pl.ds(top, n)], band.at[which, d], band_sem.at[which]).start()
-        return 0
-
-    lax.fori_loop(0, n, band_in, 0)
+
+    loop(n, band_in)
     first_tables.wait()
 
-    group = 2 if tl % 2 == 0 else 1
-
-    def by_rows(stage, ch, row):
-        slot = free_slot(stage, ch)
-
-        def part(p, _):
-            def one(j, _):
-                row(slot, p * group + j)
-                return 0
-
-            lax.fori_loop(0, group, one, 0)
-            if stage == 0:
-                @pl.when(ch + p == 0)
-                def _():
-                    pl.semaphore_wait(barrier, n - 1)
-            ship(stage, ch, p * group, group)
-            return 0
-
-        lax.fori_loop(0, tl // group, part, 0)
+    group = max(1, tl // 3)
 
     parts = degs // per
     depth = min(parts, work.shape[0] // (per * 2 * chans))
@@ -195,8 +217,10 @@
             w_hbm.at[pl.ds(k * per * 2 * chans, per * 2 * chans)],
             work.at[pl.ds(slot * per * 2 * chans, per * 2 * chans)], w_sem.at[slot])
 
-    def step1_chunk(ch, _):
-        def row(slot, t):
+    def step1_chunk(ch):
+        slot = free_slot(0, ch)
+
+        def row(t):
             unit = ch * tl + t
             step_in(f_hbm, unit)
             buf = lax.rem(unit, 2)
@@ -207,23 +231,99 @@
                 gather[pl.ds(b + 1, modes2, stride=nb), :] = spec[:, chans:]
             put_rows(slot, t)
 
-        by_rows(0, ch, row)
+            @pl.when((ch == 0) & (t == group - 1))
+            def _():
+                pl.semaphore_wait(barrier, n - 1)
+                ship(0, 0, 0, group)
+
+
+        loop(tl, row)
+        send_peak(0, ch)
 
         @pl.when(ch == 0)
         def _():
+            ship(0, 0, group, tl - group)
             for k in range(depth):
                 w_in(k).start()
 
-        return 0
-
-    lax.fori_loop(0, chunks, step1_chunk, 0)
+
+    loop(chunks, step1_chunk)
     unit_in(dg_hbm, 0).start()
+    for which in range(2):
+        pltpu.make_async_copy(band.at[which], band.at[which], band_sem.at[which]).wait()
+    qs[...] = jnp.zeros_like(qs)
+
+    def pack(z, store):
+        def one(index):
+            half_at, row = lax.div(index, held), lax.rem(index, held)
+            p = half_at * (held - 1) + row
+            degree = jnp.where(core == 0, jnp.minimum(z + p, n - 1), jnp.maximum(p - 1, 0))
+            store(half_at, row, degree, (p < n - z) == (core == 0))
+
+        loop(2 * held, one)
+
+    def project(which, ch, target, device):
+        def body_of(src):
+            gather[pl.ds(src * tl * tile, tl * tile), :] = topin[ch, target, src].reshape(tl * tile, chans).astype(F32)
+
+        loop(n, body_of)
+        for k in range(tile):
+            xb[:, k * chans:(k + 1) * chans] = gather[pl.ds(k, lats, stride=tile), :].astype(BF16)
+        out = dot(band[which, device].astype(BF16), xb[...])
+        for k in range(tile):
+            qs[pl.ds(k, n, stride=tile), :] = out[:, k * chans:(k + 1) * chans]
+
+    def relay_peak(which, ch):
+        pltpu.make_async_copy(peaks(n - 3), peaks(n - 3), row_recv.at[ch]).wait()
+        targets = (lax.rem(chip - 1 + chips, chips), lax.rem(chip + 1, chips))
+        for side, z in enumerate(targets):
+            project(which, ch, side + 1, 2 * z + core)
+
+            def keep(half_at, row, degree, ours):
+                values = qs[pl.ds(pl.multiple_of(degree * tile, tile), tile), :]
+                partial[half_at, side, row] = jnp.where(ours, values, jnp.zeros_like(values))
+
+            pack(z, keep)
+        swap = to(sibling, partial.at[1 - core], mid.at[ch], mid_send.at[ch], mid_recv.at[ch])
+        swap.start()
+        if which == 1:
+            pltpu.make_async_copy(sums.at[ch], sums.at[ch], sum_send.at[ch]).wait()
+        swap.wait()
+        sums[ch] = partial[core] + mid[ch]
+        for side, z in enumerate(targets):
+            to(2 * z + core, sums.at[ch, side], sumin.at[ch, side], sum_send.at[ch], sum_recv.at[ch]).start()
+
+    def finish_peak(which, ch):
+        pltpu.make_async_copy(sumin.at[ch], sumin.at[ch], sum_recv.at[ch]).wait()
+        joined[ch, core] = sumin[ch, 0] + sumin[ch, 1]
+        swap = to(sibling, joined.at[ch, core], joined.at[ch, core], join_send.at[ch], join_recv.at[ch])
+        swap.start()
+        project(which, ch, 0, me)
+        swap.wait()
+
+        def one(degree):
+            p = jnp.where(core == 0, degree - chip, degree + 1)
+            ours = degree >= first_mode(me)
+            p = jnp.maximum(p, 0)
+            h = jnp.where(p > held - 1, 1, 0)
+            come = joined[ch, h, p - h * (held - 1)]
+            work[pl.ds(area + (top + degree) * pitch + rows - tile, tile), :] = qs[
+                pl.ds(pl.multiple_of(degree * tile, tile), tile), :] + jnp.where(ours, come, jnp.zeros_like(come))
+
+        loop(n, one)
+
+    relay_peak(0, 0)
+
+    def ship_rows(ch):
+        ship(0, ch, 0, tl)
+
+    loop(chunks - 1, ship_rows, 1)
     for which in range(2):
         pltpu.make_async_copy(pbuf.at[which], pbuf.at[which], p_sem.at[which]).wait()
     pmat[...] = pbuf[...].astype(BF16)
     other_tables.wait()
 
-    def load_w(k, _):
+    def load_w(k):
         w_in(k).wait()
         base = lax.rem(k, depth) * per * 2 * chans
         for j in range(per):
@@ -235,19 +335,15 @@
         def _():
             w_in(k + depth).start()
 
-        return 0
-
-    lax.fori_loop(0, parts, load_w, 0)
-
-    for which in range(2):
-        pltpu.make_async_copy(band.at[which], band.at[which], band_sem.at[which]).wait()
-    qs[...] = jnp.zeros_like(qs)
+
+    loop(parts, load_w)
+
     span = cmat.shape[3]
     mine_t = (lax.broadcasted_iota(jnp.int32, (8, lats), 1) == me * tl + lax.broadcasted_iota(jnp.int32, (8, lats), 0))
     mine_t &= lax.broadcasted_iota(jnp.int32, (8, lats), 0) < tl
     mine_t = jnp.where(mine_t, 1.0, 0.0).astype(BF16)
 
-    def tabulate(d, _):
+    def tabulate(d):
         z, of_core = lax.div(d, 2), lax.rem(d, 2)
         row = lax.broadcasted_iota(jnp.int32, (n, span), 0)
         p = jnp.where(of_core == 0, row - z, row + 1)
@@ -256,9 +352,19 @@
         for which in range(2):
             picked = dot(mine_t, band[which, d].astype(BF16), ((1,), (1,))).astype(BF16)
             cmat[which, z, pl.ds(pl.multiple_of(of_core * 8, 8), 8), :] = dot(picked, moved)
-        return 0
-
-    lax.fori_loop(0, n, tabulate, 0)
+
+    loop(n, tabulate)
+
+    def no_degree(l):
+        work[pl.ds(area + l * pitch + rows - tile, tile), :] = jnp.zeros((tile, chans), F32)
+
+    loop(top, no_degree)
+
+    def relay_first(ch):
+        relay_peak(0, ch)
+
+    loop(chunks, relay_first, 1)
+    ship(0, chunks - 1, 0, tl)
 
     sign = jnp.where(lax.broadcasted_iota(jnp.int32, (tile, chans), 0) < nb, -1.0, 1.0).astype(F32)
 
@@ -267,42 +373,29 @@
         return (pltpu.roll(groups, nb, 1) * sign[None]).reshape(values.shape)
 
     def legendre(src, dst, which, over):
-        def mode(m, _):
+        def mode(m):
             for k in range(tile):
                 xb[:, k * chans:(k + 1) * chans] = work[
                     pl.ds(src + m * tile + k, lats, stride=pitch), :].astype(BF16)
             out = dot(pmat[which, m], xb[...], ((over,), (0,)))
             for k in range(tile):
                 work[pl.ds(dst + m * tile + k, degs, stride=pitch), :] = out[:, k * chans:(k + 1) * chans]
-            return 0
-
-        lax.fori_loop(0, ml, mode, 0)
+
+        loop(ml - 1, mode)
 
     def unload(stage, ch):
-        def body(src, _):
+        def body(src):
             for t in range(tl):
                 work[pl.ds((src * tl + t) * pitch, rows), :] = recv[stage % 2, ch, src, t].astype(F32)
-            return 0
-
-        lax.fori_loop(0, n, body, 0)
+
+        loop(n, body)
 
     def load(slot):
-        def body(dev, _):
+        def body(dev):
             for t in range(tl):
                 send[slot, dev, t] = work[pl.ds(area + (dev * tl + t) * pitch, rows), :].astype(BF16)
-            return 0
-
-        lax.fori_loop(0, n, body, 0)
-
-    def pack(store):
-        def one(index, _):
-            half_at, row = lax.div(index, held), lax.rem(index, held)
-            p = half_at * (held - 1) + row
-            degree = jnp.where(core == 0, jnp.minimum(chip + p, n - 1), jnp.maximum(p - 1, 0))
-            store(half_at, row, degree, (p < n - chip) == (core == 0))
-            return 0
-
-        lax.fori_loop(0, 2 * held, one, 0)
+
+        loop(n, body)
 
     def only(ours, values):
         values = values.astype(F32)
@@ -312,19 +405,19 @@
         arrived(stage - 1, ch)
         unload(stage - 1, ch)
         legendre(0, area, into, 1)
-
-        def degree(l, _):
+        finish_peak(into, ch)
+
+        def degree(l):
             x = work[pl.ds(area + l * pitch, rows), :].astype(BF16)
             kept[l, ch] = x
             work[pl.ds(l * pitch, rows), :] = mix(l, x)
-            return 0
-
-        lax.fori_loop(0, degs, degree, 0, unroll=2)
+
+        loop(degs, degree, unroll=2)
 
         def keep_top(half_at, row, degree, ours):
             own[half_at, 2, ch, row] = only(ours, work[pl.ds((top + degree) * pitch + rows - tile, tile), :])
 
-        pack(keep_top)
+        pack(chip, keep_top)
         if stage == 1:
             swap = to(sibling, own.at[1 - core, 2, ch], other.at[2, ch], swap_send.at[ch], swap_recv.at[ch])
             swap.start()
@@ -340,6 +433,11 @@
 
             for away in (2, -2):
                 top_copy(0, away, ch, near_recv).start()
+        else:
+            @pl.when(ch == 0)
+            def _():
+                relay_peak(1, chunks - 1)
+
         ship(stage, ch, 0, tl)
 
     def top_copy(source, away, ch, got):
@@ -347,7 +445,7 @@
         return to(2 * lax.rem(chip + away + chips, chips) + core, block, block, top_send, got.at[ch])
 
     def top_blocks(count, ch):
-        return packs.at[core, pl.ds(0, count), 2, ch]
+        return packs.at[core, head(count), 2, ch]
 
     def relay_top(ch):
         pltpu.make_async_copy(top_blocks(2, ch), top_blocks(2, ch), near_recv.at[ch]).wait()
@@ -374,15 +472,14 @@
         return both[:, :chans] + turn(both[:, chans:])
 
     def mix_adjoint(l, x):
-        real = dot(x, vmix[l, pl.ds(0, chans)])
+        real = dot(x, vmix[l, head(chans)])
         imag = dot(x, vmix[l, pl.ds(chans, chans)])
         return real - turn(imag)
 
-    def step2_chunk(ch, _):
+    def step2_chunk(ch):
         spectral(1, ch, 0, coef, mix_forward)
-        return 0
-
-    lax.fori_loop(0, chunks, step2_chunk, 0)
+
+    loop(chunks, step2_chunk)
     relay_top(chunks - 2)
 
     def fetch_rows(stage, ch, t):
@@ -393,7 +490,7 @@
         return jnp.concatenate(
             [gather[pl.ds(b, modes2, stride=nb), :], gather[pl.ds(b + 1, modes2, stride=nb), :]], axis=1).astype(BF16)
 
-    def step3_chunk(ch, _):
+    def step3_chunk(ch):
         arrived(1, ch)
         pltpu.make_async_copy(top_blocks(5, ch), top_blocks(5, ch), far_recv.at[ch]).wait()
         swap = to(sibling, top_blocks(chips, ch), top_blocks(chips, ch), swap_send.at[ch], swap_recv.at[ch])
@@ -407,16 +504,21 @@
 
         @pl.when(ch == chunks - 1)
         def _():
-            all_sent = packs.at[0, pl.ds(0, 7), 2]
+            all_sent = packs.at[0, head(7), 2]
             pltpu.make_async_copy(all_sent, all_sent, top_send).wait()
 
-        def apply(z, _):
+        def apply(z):
             apply_top(1, ch, z)
-            return 0
-
-        lax.fori_loop(0, chips, apply, 0)
-
-        def row(slot, t):
+
+        loop(chips, apply)
+
+        @pl.when(ch == 1)
+        def _():
+            relay_peak(1, 0)
+
+        slot = free_slot(2, ch)
+
+        def row(t):
             unit = ch * tl + t
             step_in(dg_hbm, unit)
             buf = lax.rem(unit, 2)
@@ -430,23 +532,33 @@
                 gather[pl.ds(b + 1, modes2, stride=nb), :] = spec[:, chans:]
             put_rows(slot, t)
 
-        by_rows(2, ch, row)
-        return 0
-
-    lax.fori_loop(0, chunks, step3_chunk, 0)
+        loop(tl, row)
+        send_peak(2, ch)
+
+        @pl.when(ch < chunks - 1)
+        def _():
+            ship(2, ch, 0, tl)
+
+
+    loop(chunks, step3_chunk)
+
+    def relay_second(ch):
+        relay_peak(1, ch)
+
+    loop(chunks - 1, relay_second, 1)
+    ship(2, chunks - 1, 0, tl)
     unit_in(dg_hbm, 0).start()
 
-    def step4_chunk(ch, _):
+    def step4_chunk(ch):
         spectral(3, ch, 1, dq, mix_adjoint)
-        return 0
-
-    lax.fori_loop(0, chunks, step4_chunk, 0)
+
+    loop(chunks, step4_chunk)
 
     for which, kept in enumerate((coef, dq)):
         def keep_low(half_at, row, degree, ours):
-            own[half_at, which, :, row] = only(ours, kept[degree, :, pl.ds(0, tile)])
-
-        pack(keep_low)
+            own[half_at, which, :, row] = only(ours, kept[degree, :, head(tile)])
+
+        pack(chip, keep_low)
     own_copy = to(sibling, own.at[1 - core], other, own_send, own_recv)
     own_copy.start()
 
@@ -481,19 +593,18 @@
         return n + (2 * block + of_core) * half
 
     def weight_grad(dst, degree):
-        def one(j, _):
+        def one(j):
             outer(dst, j * wide, [(dq[degree + j, ch], coef[degree + j, ch]) for ch in range(chunks)])
-            return 0
-
-        lax.fori_loop(0, half, one, 0)
+
+        loop(half, one)
 
     def pair_copy(k):
         slot = lax.rem(k, 2)
         rows_there = pl.ds(first_degree(block_at(k, -way), core) * wide, block_rows)
-        return to(sibling, wbuf.at[slot, pl.ds(0, block_rows)], dw_out.at[rows_there],
+        return to(sibling, wbuf.at[slot, head(block_rows)], dw_out.at[rows_there],
                   pair_send.at[slot], pair_recv.at[k])
 
-    def weight_block(k, _):
+    def weight_block(k):
         @pl.when(k >= 2)
         def _():
             pair_copy(k - 2).wait_send()
@@ -501,16 +612,15 @@
         pair_copy(k).start()
         block = block_at(k, way)
         weight_grad(work.at[pl.ds(block * block_rows, block_rows)], first_degree(block, core))
-        return 0
-
-    lax.fori_loop(0, chips, weight_block, 0)
+
+    loop(chips, weight_block)
     pair_copy(chips - 2).wait_send()
     pair_copy(chips - 1).wait_send()
     own_copy.wait()
     packs[core, chip] = (own[core].astype(F32) + other[...].astype(F32)).astype(BF16)
 
     def low_degree(l):
-        def one(z, _):
+        def one(z):
             for c in range(2):
                 p = l - z if c == 0 else l + 1
                 ours = p >= 0 if c == 0 else p >= n - z
@@ -518,11 +628,10 @@
                 h = jnp.where(p > held - 1, 1, 0)
                 for which in range(2):
                     lowx[which, 2 * z + c] = only(ours, packs[h, z, which, :, p - h * (held - 1)])
-            return 0
-
-        lax.fori_loop(0, chips, one, 0)
+
+        loop(chips, one)
         outer(wbuf.at[0], 0, [(lowx[1].reshape(-1, chans), lowx[0].reshape(-1, chans))])
-        dw_out[pl.ds(l * wide, wide)] = wbuf[0, pl.ds(0, wide)]
+        dw_out[pl.ds(l * wide, wide)] = wbuf[0, head(wide)]
 
     def final_rows(unit):
         ch, t = unit_of(unit)
@@ -555,7 +664,7 @@
 
         work[here] += dw_out[passed]
 
-    def rs_step(i, _):
+    def rs_step(i):
         add_pair(i)
 
         @pl.when(i >= pieces)
@@ -577,20 +686,18 @@
             pack_copy(k).start()
             share(k)
 
-        return 0
-
-    lax.fori_loop(0, hops, rs_step, 0)
+
+    loop(hops, rs_step)
     pack_copy(chips - 2).wait_recv()
     share(chips - 1)
 
-    def own_sum(s, _):
+    def own_sum(s):
         i = hops + s
         add_pair(i)
         rs_copy(i - pieces).wait_recv()
         here, there = place(i, core)
         dw_out[there] += work[here]
         ag_copy(i, s).start()
-        return 0
 
     def ag_copy(i, got):
         _, there = place(i, core)
@@ -600,16 +707,15 @@
         _, there = place(i, core)
         to(sibling, dw_out.at[there], dw_out.at[there], pub_send, pub_recv).start()
 
-    lax.fori_loop(0, pieces, own_sum, 0)
+    loop(pieces, own_sum)
 
     pl.semaphore_signal(free_sem, inc=1, device_id={axis: sibling}, device_id_type=pl.DeviceIdType.MESH)
     pl.semaphore_wait(free_sem, 1)
 
-    def own_piece(s, _):
+    def own_piece(s):
         publish(hops + s)
-        return 0
-
-    lax.fori_loop(0, pieces, own_piece, 0)
+
+    loop(pieces, own_piece)
     gathered = packs.at[1 - core]
     pltpu.make_async_copy(gathered, gathered, share_recv).wait()
 
@@ -630,7 +736,7 @@
         def _():
             low_degree(i)
 
-    def ag_step(i, _):
+    def ag_step(i):
         ag_copy(i, i).wait_recv()
 
         @pl.when(i + pieces < hops)
@@ -639,26 +745,26 @@
 
         publish(i)
         task(i)
-        return 0
-
-    lax.fori_loop(0, hops, ag_step, 0)
-
-    def rest(i, _):
+
+    loop(hops, ag_step)
+
+    def rest(i):
         task(i)
-        return 0
-
-    lax.fori_loop(hops, max(hops, chips + units, n), rest, 0)
+
+    loop(max(hops, chips + units, n), rest, hops)
 
     wait_sent(3 * chunks - 1, 2)
     for ch in range(chunks):
         wait_sent(3 * chunks + ch, 3)
-    sent = work.at[pl.ds(0, (chips - 1) * block_rows)]
+    for ch in range(chunks):
+        pltpu.make_async_copy(sums.at[ch], sums.at[ch], sum_send.at[ch]).wait()
+    sent = work.at[head((chips - 1) * block_rows)]
     pltpu.make_async_copy(sent, sent, rs_send).wait()
     pltpu.make_async_copy(sent, sent, ag_send).wait()
-    sent = packs.at[0, pl.ds(0, chips - 1)]
+    sent = packs.at[0, head(chips - 1)]
     pltpu.make_async_copy(sent, sent, pack_send).wait()
     pltpu.make_async_copy(packs.at[0], packs.at[0], share_send).wait()
-    shared = dw_out.at[pl.ds(0, chips * block_rows)]
+    shared = dw_out.at[head(chips * block_rows)]
     pltpu.make_async_copy(shared, shared, pub_send).wait()
     pltpu.make_async_copy(shared, shared, pub_recv).wait()
 
@@ -727,6 +833,12 @@
                 pltpu.VMEM((2, n // 2) + packed, BF16),
                 pltpu.VMEM((2, n, chunks, 2 * nb, chans), BF16),
                 pltpu.VMEM(tables.shape, BF16),
+                pltpu.VMEM((chunks, 3, n, tl, 2 * nb, chans), BF16),
+                pltpu.VMEM((2, 2, held, 2 * nb, chans), F32),
+                pltpu.VMEM((chunks, 2, held, 2 * nb, chans), F32),
+                pltpu.VMEM((chunks, 2, held, 2 * nb, chans), F32),
+                pltpu.VMEM((chunks, 2, held, 2 * nb, chans), F32),
+                pltpu.VMEM((chunks, 2, held, 2 * nb, chans), F32),
                 pltpu.SemaphoreType.DMA((4 * chunks,)),
                 pltpu.SemaphoreType.DMA((4 * chunks,)),
                 pltpu.SemaphoreType.DMA((2,)),
@@ -754,9 +866,17 @@
                 pltpu.SemaphoreType.DMA((chunks,)),
                 pltpu.SemaphoreType.DMA((chunks,)),
                 pltpu.SemaphoreType.DMA((chunks,)),
+                pltpu.SemaphoreType.DMA((chunks,)),
+                pltpu.SemaphoreType.DMA((chunks,)),
+                pltpu.SemaphoreType.DMA((chunks,)),
+                pltpu.SemaphoreType.DMA((chunks,)),
+                pltpu.SemaphoreType.DMA((chunks,)),
+                pltpu.SemaphoreType.DMA((chunks,)),
+                pltpu.SemaphoreType.DMA((chunks,)),
+                pltpu.SemaphoreType.DMA((chunks,)),
             ],
             compiler_params=pltpu.CompilerParams(
-                collective_id=0, has_side_effects=True, vmem_limit_bytes=42 * 1024 * 1024),
+                collective_id=0, has_side_effects=True, vmem_limit_bytes=43 * 1024 * 1024),
         )(
             field_loc.transpose(0, 2, 3, 1), grad_loc.transpose(0, 2, 3, 1),
             w_mix.transpose(0, 1, 3, 2).reshape(degs * 2 * chans, chans),

time: 419 us -> 415 us (level)
  Pallas kernels: 418 us -> 413 us
    pallas_call x1, Pallas kernels: 411 us -> 406 us  [local_step(): pl.pallas_call(functools.partial(layer_kernel, 'lat', n, nb, pieces, per)...]
where the time goes in v7:
time: 415 us; the launch traced here: 414 us
  Pallas kernels  413 us (100%)
    pallas_call x1, Pallas kernels, local_step(): pl.pallas_call(functools.partial(layer_kernel, 'lat', n, nb, pieces, per)...  406 us

profile of v7, /device:TPU:21, one launch (start us, length us, event | category | flops | bytes accessed | tf_op | source)
XLA Modules:
  0.0 413.9 jit_solution(8993629604605761874)
XLA Ops:
  0.6 406.4 %layer.1 = (f32[12,6,192,128]{3,2,1,0:T(8,128)S(1)}, f32[24576,128]{1,0:T(8,128)S(1)}) custom-call(f32[12,6,192,128]{3,2,1,0:T(8,128)} %bitcast.10, f32[12,6,192,128]{3,2,1,0:T(8,128)} %bitcast.11, f32[24576,128]{1,0:T(8,128)} %bitcast.9, f32[96,96,96]{2,1,0:T(8,128)} %pf_hbm.1, f32[96,96,96]{2,1,0:T(8,128)} %pv_hbm.1, bf16[8,192,192]{2,1,0:T(8,128)(2,1)} %constant.34.tab_hbm), custom_call_target="tpu_custom_call" | custom-call | tf_op jit(solution)/shard_map/layer/pallas_call | solution.py:806
  407.0 6.8 %put.1 = (f32[12,6,192,128]{3,2,1,0:T(8,128)}, f32[24576,128]{1,0:T(8,128)}) custom-call(f32[12,6,192,128]{3,2,1,0:T(8,128)S(1)} %get-tuple-element.6.df_ref, f32[24576,128]{1,0:T(8,128)S(1)} %get-tuple-element.7.dw_ref), custom_call_target="tpu_custom_call" | custom-call | tf_op jit(solution)/shard_map/put/pallas_call | solution.py:884

commit v8 on v7

--- a/solution.py
+++ b/solution.py
@@ -59,11 +59,12 @@
     f_hbm, dg_hbm, w_hbm, pf_hbm, pv_hbm, tab_hbm,
     df_out, dw_out,
     recv, send, work, xb, coef, dq, vmix, wbuf, inbuf, gather, pbuf, pmat, band, cmat, qs, own, other, packs, lowx, tab,
-    topin, partial, mid, sums, sumin, joined,
+    topin, partial, mid, sums, sumin, joined, second,
     send_sem, recv_sem, in_sem, w_sem, p_sem, band_sem, pair_send, pair_recv, rs_send, rs_recv, ag_send, ag_recv,
     free_sem, pub_send, pub_recv, own_send, own_recv, pack_send, pack_recv, share_send, share_recv,
     tab_sem, top_send, near_recv, far_recv, swap_send, swap_recv,
     row_send, row_recv, mid_send, mid_recv, sum_send, sum_recv, join_send, join_recv,
+    always_send, always_recv, some_send, some_recv,
 ):
     me = lax.axis_index(axis)
     batch, tl, lons, chans = f_hbm.shape
@@ -74,6 +75,7 @@
     pitch = rows + 1
     modes2 = 2 * n * ml
     units = chunks * tl
+    final = chunks - 1
     slots = chunks + 1
     fwd_h, fwd_l, dbl_h, dbl_l, syn_h, syn_l, adj_h, adj_l = (tab.at[k] for k in range(8))
     area = lats * pitch
@@ -81,6 +83,7 @@
     held = n // 2 + 1
     chip, core = lax.div(me, 2), lax.rem(me, 2)
     chips = n // 2
+    last = chips - 1
     way = 1 - 2 * core
     sibling = me + way
     onward = 2 * lax.rem(chip + way + chips, chips) + core
@@ -180,11 +183,6 @@
     first_tables = pltpu.make_async_copy(tab_hbm.at[head(2)], tab.at[head(2)], tab_sem.at[0])
     other_tables = pltpu.make_async_copy(tab_hbm.at[pl.ds(2, 6)], tab.at[pl.ds(2, 6)], tab_sem.at[1])
     first_tables.start()
-
-    def clear(ch):
-        topin[ch] = jnp.zeros(topin.shape[1:], BF16)
-
-    loop(chunks, clear)
     barrier = pltpu.get_barrier_semaphore()
 
     def announce(k):
@@ -248,6 +246,21 @@
 
 
     loop(chunks, step1_chunk)
+
+    def clear(src):
+        away = lax.rem(lax.div(src, 2) - chip + chips, chips)
+        back = lax.rem(chips - away, chips)
+        reach = chips // 2 - 1
+        own_chip = away == 0
+        above = (away < reach) | ((away == reach) & (core == 0))
+        below = (back < reach) | ((back == reach) & (core == 1))
+        for target, used in enumerate((own_chip, above, below)):
+            @pl.when(jnp.logical_not(used))
+            def _():
+                for ch in range(chunks):
+                    topin[ch, target, src] = jnp.zeros(topin.shape[3:], BF16)
+
+    loop(n, clear)
     unit_in(dg_hbm, 0).start()
     for which in range(2):
         pltpu.make_async_copy(band.at[which], band.at[which], band_sem.at[which]).wait()
@@ -275,7 +288,7 @@
 
     def relay_peak(which, ch):
         pltpu.make_async_copy(peaks(n - 3), peaks(n - 3), row_recv.at[ch]).wait()
-        targets = (lax.rem(chip - 1 + chips, chips), lax.rem(chip + 1, chips))
+        targets = (lax.rem(chip + last, chips), lax.rem(chip + 1, chips))
         for side, z in enumerate(targets):
             project(which, ch, side + 1, 2 * z + core)
 
@@ -317,7 +330,7 @@
     def ship_rows(ch):
         ship(0, ch, 0, tl)
 
-    loop(chunks - 1, ship_rows, 1)
+    loop(final, ship_rows, 1)
     for which in range(2):
         pltpu.make_async_copy(pbuf.at[which], pbuf.at[which], p_sem.at[which]).wait()
     pmat[...] = pbuf[...].astype(BF16)
@@ -364,7 +377,7 @@
         relay_peak(0, ch)
 
     loop(chunks, relay_first, 1)
-    ship(0, chunks - 1, 0, tl)
+    ship(0, final, 0, tl)
 
     sign = jnp.where(lax.broadcasted_iota(jnp.int32, (tile, chans), 0) < nb, -1.0, 1.0).astype(F32)
 
@@ -436,7 +449,7 @@
         else:
             @pl.when(ch == 0)
             def _():
-                relay_peak(1, chunks - 1)
+                relay_peak(1, final)
 
         ship(stage, ch, 0, tl)
 
@@ -498,11 +511,11 @@
 
         @pl.when(ch == 0)
         def _():
-            relay_top(chunks - 1)
+            relay_top(final)
 
         swap.wait()
 
-        @pl.when(ch == chunks - 1)
+        @pl.when(ch == final)
         def _():
             all_sent = packs.at[0, head(7), 2]
             pltpu.make_async_copy(all_sent, all_sent, top_send).wait()
@@ -535,7 +548,7 @@
         loop(tl, row)
         send_peak(2, ch)
 
-        @pl.when(ch < chunks - 1)
+        @pl.when(ch < final)
         def _():
             ship(2, ch, 0, tl)
 
@@ -545,8 +558,8 @@
     def relay_second(ch):
         relay_peak(1, ch)
 
-    loop(chunks - 1, relay_second, 1)
-    ship(2, chunks - 1, 0, tl)
+    loop(final, relay_second, 1)
+    ship(2, final, 0, tl)
     unit_in(dg_hbm, 0).start()
 
     def step4_chunk(ch):
@@ -559,6 +572,33 @@
             own[half_at, which, :, row] = only(ours, kept[degree, :, head(tile)])
 
         pack(chip, keep_low)
+
+    def both_parts(peer, action):
+        degree = n + peer
+        for which, kept in enumerate((coef, dq)):
+            action(to(peer, kept.at[degree, :, head(tile)], second.at[which, me, :, head(tile)],
+                      always_send, always_recv))
+
+            @pl.when(first_mode(me) <= peer)
+            def _():
+                more = pl.ds(tile, tile)
+                action(to(peer, kept.at[degree, :, more], second.at[which, me, :, more],
+                          some_send.at[peer], some_recv.at[me]))
+
+    def send_second(k):
+        both_parts(lax.rem(me + k, n), lambda copy: copy.start())
+
+    loop(n, send_second, 1)
+    for which, kept in enumerate((coef, dq)):
+        second[which, me] = kept[n + me, :, head(2 * tile)]
+
+    def clear_second(src):
+        @pl.when(first_mode(src) > me)
+        def _():
+            for which in range(2):
+                second[which, src, :, pl.ds(tile, tile)] = jnp.zeros((chunks, tile, chans), BF16)
+
+    loop(n, clear_second)
     own_copy = to(sibling, own.at[1 - core], other, own_send, own_recv)
     own_copy.start()
 
@@ -571,11 +611,11 @@
     def share(k):
         to(sibling, pack_block(k), pack_block(k), share_send, share_recv).start()
 
-    half = degs // n - 1
+    half = degs // n - 2
     wide = 2 * chans
     block_rows = half * wide
     piece = block_rows // pieces
-    hops = (chips - 1) * pieces
+    hops = (last) * pieces
 
     def block_at(k, direction):
         return lax.rem(chip - direction * (1 + k) + 2 * chips, chips)
@@ -590,7 +630,7 @@
         dst[pl.ds(row + 1, chans, stride=2), :] = imag
 
     def first_degree(block, of_core):
-        return n + (2 * block + of_core) * half
+        return 2 * n + (2 * block + of_core) * half
 
     def weight_grad(dst, degree):
         def one(j):
@@ -615,7 +655,7 @@
 
     loop(chips, weight_block)
     pair_copy(chips - 2).wait_send()
-    pair_copy(chips - 1).wait_send()
+    pair_copy(last).wait_send()
     own_copy.wait()
     packs[core, chip] = (own[core].astype(F32) + other[...].astype(F32)).astype(BF16)
 
@@ -689,7 +729,7 @@
 
     loop(hops, rs_step)
     pack_copy(chips - 2).wait_recv()
-    share(chips - 1)
+    share(last)
 
     def own_sum(s):
         i = hops + s
@@ -699,6 +739,17 @@
         dw_out[there] += work[here]
         ag_copy(i, s).start()
 
+    def second_spot(k):
+        return pl.ds((n + 2 * block_at(k, way) + core) * wide, wide)
+
+    def second_copy(k, got):
+        spot = dw_out.at[second_spot(k)]
+        return to(onward, spot, spot, ag_send, ag_recv.at[hops + got])
+
+    def second_publish(k):
+        spot = dw_out.at[second_spot(k)]
+        to(sibling, spot, spot, pub_send, pub_recv).start()
+
     def ag_copy(i, got):
         _, there = place(i, core)
         return to(onward, dw_out.at[there], dw_out.at[there], ag_send, ag_recv.at[got])
@@ -707,7 +758,20 @@
         _, there = place(i, core)
         to(sibling, dw_out.at[there], dw_out.at[there], pub_send, pub_recv).start()
 
+    firsts = second.at[:, head(n - 1), :, head(tile)]
+    pltpu.make_async_copy(firsts, firsts, always_recv).wait()
+
+    def wait_second(src):
+        @pl.when((first_mode(src) <= me) & (src != me))
+        def _():
+            part = second.at[:, src, :, pl.ds(tile, tile)]
+            pltpu.make_async_copy(part, part, some_recv.at[src]).wait()
+
+    loop(n, wait_second)
+    outer(wbuf.at[0], 0, [(second[1].reshape(-1, chans), second[0].reshape(-1, chans))])
+    dw_out[second_spot(last)] = wbuf[0, head(wide)]
     loop(pieces, own_sum)
+    second_copy(last, 0).start()
 
     pl.semaphore_signal(free_sem, inc=1, device_id={axis: sibling}, device_id_type=pl.DeviceIdType.MESH)
     pl.semaphore_wait(free_sem, 1)
@@ -716,6 +780,7 @@
         publish(hops + s)
 
     loop(pieces, own_piece)
+    second_publish(last)
     gathered = packs.at[1 - core]
     pltpu.make_async_copy(gathered, gathered, share_recv).wait()
 
@@ -744,6 +809,18 @@
             ag_copy(i, i + pieces).start()
 
         publish(i)
+
+        @pl.when(lax.rem(i, pieces) == pieces - 1)
+        def _():
+            k = lax.div(i, pieces)
+            second_copy(k, k).wait_recv()
+
+            @pl.when(k < chips - 2)
+            def _():
+                second_copy(k, k + 1).start()
+
+            second_publish(k)
+
         task(i)
 
     loop(hops, ag_step)
@@ -753,18 +830,28 @@
 
     loop(max(hops, chips + units, n), rest, hops)
 
-    wait_sent(3 * chunks - 1, 2)
+    wait_sent(2 * chunks + final, 2)
     for ch in range(chunks):
         wait_sent(3 * chunks + ch, 3)
     for ch in range(chunks):
         pltpu.make_async_copy(sums.at[ch], sums.at[ch], sum_send.at[ch]).wait()
-    sent = work.at[head((chips - 1) * block_rows)]
+    sent = work.at[head((last) * block_rows)]
     pltpu.make_async_copy(sent, sent, rs_send).wait()
+    sent = dw_out.at[head((last) * (block_rows + wide))]
     pltpu.make_async_copy(sent, sent, ag_send).wait()
-    sent = packs.at[0, head(chips - 1)]
+    pltpu.make_async_copy(firsts, firsts, always_send).wait()
+
+    def wait_some(peer):
+        @pl.when((first_mode(me) <= peer) & (peer != me))
+        def _():
+            part = second.at[:, peer, :, pl.ds(tile, tile)]
+            pltpu.make_async_copy(part, part, some_send.at[peer]).wait()
+
+    loop(n, wait_some)
+    sent = packs.at[0, head(last)]
     pltpu.make_async_copy(sent, sent, pack_send).wait()
     pltpu.make_async_copy(packs.at[0], packs.at[0], share_send).wait()
-    shared = dw_out.at[head(chips * block_rows)]
+    shared = dw_out.at[head(chips * (block_rows + wide))]
     pltpu.make_async_copy(shared, shared, pub_send).wait()
     pltpu.make_async_copy(shared, shared, pub_recv).wait()
 
@@ -794,7 +881,7 @@
         chunks = batch // nb
         rows = ml * 2 * nb
         pitch = rows + 1
-        half = degs // n - 1
+        half = degs // n - 2
         pieces = 4 if half * 2 * chans % 32 == 0 else 1
         hops = (n // 2 - 1) * pieces
         per = 4
@@ -839,6 +926,7 @@
                 pltpu.VMEM((chunks, 2, held, 2 * nb, chans), F32),
                 pltpu.VMEM((chunks, 2, held, 2 * nb, chans), F32),
                 pltpu.VMEM((chunks, 2, held, 2 * nb, chans), F32),
+                pltpu.VMEM((2, n, chunks, 4 * nb, chans), BF16),
                 pltpu.SemaphoreType.DMA((4 * chunks,)),
                 pltpu.SemaphoreType.DMA((4 * chunks,)),
                 pltpu.SemaphoreType.DMA((2,)),
@@ -850,7 +938,7 @@
                 pltpu.SemaphoreType.DMA,
                 pltpu.SemaphoreType.DMA((hops,)),
                 pltpu.SemaphoreType.DMA,
-                pltpu.SemaphoreType.DMA((hops,)),
+                pltpu.SemaphoreType.DMA((hops + n // 2 - 1,)),
                 pltpu.SemaphoreType.REGULAR,
                 pltpu.SemaphoreType.DMA,
                 pltpu.SemaphoreType.DMA,
@@ -874,6 +962,10 @@
                 pltpu.SemaphoreType.DMA((chunks,)),
                 pltpu.SemaphoreType.DMA((chunks,)),
                 pltpu.SemaphoreType.DMA((chunks,)),
+                pltpu.SemaphoreType.DMA,
+                pltpu.SemaphoreType.DMA,
+                pltpu.SemaphoreType.DMA((n,)),
+                pltpu.SemaphoreType.DMA((n,)),
             ],
             compiler_params=pltpu.CompilerParams(
                 collective_id=0, has_side_effects=True, vmem_limit_bytes=43 * 1024 * 1024),

time: 415 us -> 409 us (0.986)
  Pallas kernels: 413 us -> 408 us
    pallas_call x1, Pallas kernels: 406 us -> 401 us  [local_step(): pl.pallas_call(functools.partial(layer_kernel, 'lat', n, nb, pieces, per)...]
where the time goes in v8:
time: 409 us; the launch traced here: 408 us
  Pallas kernels  408 us (100%)
    pallas_call x1, Pallas kernels, local_step(): pl.pallas_call(functools.partial(layer_kernel, 'lat', n, nb, pieces, per)...  401 us

profile of v8, /device:TPU:21, one launch (start us, length us, event | category | flops | bytes accessed | tf_op | source)
XLA Modules:
  0.0 408.2 jit_solution(7830261854086861980)
XLA Ops:
  0.6 400.7 %layer.1 = (f32[12,6,192,128]{3,2,1,0:T(8,128)S(1)}, f32[24576,128]{1,0:T(8,128)S(1)}) custom-call(f32[12,6,192,128]{3,2,1,0:T(8,128)} %bitcast.10, f32[12,6,192,128]{3,2,1,0:T(8,128)} %bitcast.11, f32[24576,128]{1,0:T(8,128)} %bitcast.9, f32[96,96,96]{2,1,0:T(8,128)} %pf_hbm.1, f32[96,96,96]{2,1,0:T(8,128)} %pv_hbm.1, bf16[8,192,192]{2,1,0:T(8,128)(2,1)} %constant.34.tab_hbm), custom_call_target="tpu_custom_call" | custom-call | tf_op jit(solution)/shard_map/layer/pallas_call | solution.py:893
  401.4 6.8 %put.1 = (f32[12,6,192,128]{3,2,1,0:T(8,128)}, f32[24576,128]{1,0:T(8,128)}) custom-call(f32[12,6,192,128]{3,2,1,0:T(8,128)S(1)} %get-tuple-element.6.df_ref, f32[24576,128]{1,0:T(8,128)S(1)} %get-tuple-element.7.dw_ref), custom_call_target="tpu_custom_call" | custom-call | tf_op jit(solution)/shard_map/put/pallas_call | solution.py:976

commit v9 on v8

--- a/solution.py
+++ b/solution.py
@@ -59,12 +59,12 @@
     f_hbm, dg_hbm, w_hbm, pf_hbm, pv_hbm, tab_hbm,
     df_out, dw_out,
     recv, send, work, xb, coef, dq, vmix, wbuf, inbuf, gather, pbuf, pmat, band, cmat, qs, own, other, packs, lowx, tab,
-    topin, partial, mid, sums, sumin, joined, second,
+    topin, partial, mid, sums, sumin, joined, handed, second,
     send_sem, recv_sem, in_sem, w_sem, p_sem, band_sem, pair_send, pair_recv, rs_send, rs_recv, ag_send, ag_recv,
     free_sem, pub_send, pub_recv, own_send, own_recv, pack_send, pack_recv, share_send, share_recv,
     tab_sem, top_send, near_recv, far_recv, swap_send, swap_recv,
     row_send, row_recv, mid_send, mid_recv, sum_send, sum_recv, join_send, join_recv,
-    always_send, always_recv, some_send, some_recv,
+    always_send, always_recv, some_send, some_recv, hand_recv,
 ):
     me = lax.axis_index(axis)
     batch, tl, lons, chans = f_hbm.shape
@@ -82,11 +82,19 @@
     top = n * (ml - 1)
     held = n // 2 + 1
     chip, core = lax.div(me, 2), lax.rem(me, 2)
+    other_core = 1 - core
     chips = n // 2
     last = chips - 1
     way = 1 - 2 * core
     sibling = me + way
-    onward = 2 * lax.rem(chip + way + chips, chips) + core
+
+    def chip_at(away):
+        return lax.rem(chip + away + chips, chips)
+
+    def across(away, its_core):
+        return 2 * chip_at(away) + its_core
+
+    onward = across(way, core)
 
     def first_mode(device):
         z = lax.div(device, 2)
@@ -130,33 +138,33 @@
         others = recv.at[stage % 2, ch, head(n - 1), :, body]
         pltpu.make_async_copy(others, others, recv_sem.at[stage * chunks + ch]).wait()
 
-    def peaks(count):
-        return topin.at[0, 0, head(count)]
+    def peaks():
+        return send.at[0, head(n - 5), :, peak]
 
     def wait_sent(index, stage):
         others = send.at[lax.rem(index, slots), head(n - 1), :, body]
         pltpu.make_async_copy(others, others, send_sem.at[index]).wait()
         if stage % 2 == 0:
             ch = index - stage * chunks
-            pltpu.make_async_copy(peaks(n - 3), peaks(n - 3), row_send.at[ch]).wait()
+            pltpu.make_async_copy(peaks(), peaks(), row_send.at[ch]).wait()
 
     def send_peak(stage, ch):
         slot = lax.rem(stage * chunks + ch, slots)
         far = chips // 2
         for same in (True, False):
-            its_core = core if same else 1 - core
+            its_core = core if same else other_core
             for away in range(1 - far, far + 1):
-                place = (away > 0) - (away < 0)
-                hop, target = away - place, (0, 2, 1)[place]
+                near = max(-2, min(2, away))
+                hop, target, apart = away - near, (0, 2, 4, 3, 1)[near], abs(away - near)
                 if away == far:
-                    hop = jnp.where(its_core == 0, 1 - far, far - 1)
-                    target = jnp.where(its_core == 0, 1, 2)
-                owner = 2 * lax.rem(chip + away + chips, chips) + its_core
-                source = send.at[slot, owner, :, peak]
-                if same and away in (-1, 0, 1):
-                    topin[ch, target, me] = source[...]
+                    hop = jnp.where(its_core == 0, 2 - far, far - 2)
+                    target = jnp.where(its_core == 0, 3, 4)
+                source = send.at[slot, across(away, its_core), :, peak]
+                place = topin.at[ch, target, 2 * apart + core]
+                if same and not apart:
+                    place[...] = source[...]
                 else:
-                    to(2 * lax.rem(chip + hop + chips, chips) + its_core, source, topin.at[ch, target, me],
+                    to(across(hop, its_core), source, place,
                        row_send.at[ch], row_recv.at[ch]).start()
 
     def free_slot(stage, ch):
@@ -247,20 +255,6 @@
 
     loop(chunks, step1_chunk)
 
-    def clear(src):
-        away = lax.rem(lax.div(src, 2) - chip + chips, chips)
-        back = lax.rem(chips - away, chips)
-        reach = chips // 2 - 1
-        own_chip = away == 0
-        above = (away < reach) | ((away == reach) & (core == 0))
-        below = (back < reach) | ((back == reach) & (core == 1))
-        for target, used in enumerate((own_chip, above, below)):
-            @pl.when(jnp.logical_not(used))
-            def _():
-                for ch in range(chunks):
-                    topin[ch, target, src] = jnp.zeros(topin.shape[3:], BF16)
-
-    loop(n, clear)
     unit_in(dg_hbm, 0).start()
     for which in range(2):
         pltpu.make_async_copy(band.at[which], band.at[which], band_sem.at[which]).wait()
@@ -276,35 +270,55 @@
         loop(2 * held, one)
 
     def project(which, ch, target, device):
-        def body_of(src):
-            gather[pl.ds(src * tl * tile, tl * tile), :] = topin[ch, target, src].reshape(tl * tile, chans).astype(F32)
-
-        loop(n, body_of)
+        gather[...] = jnp.zeros_like(gather)
+        side = 1 if target == 3 else -1
+
+        def place_rows(apart):
+            for c in range(2):
+                src = across(side * apart, c)
+                gather[pl.ds(pl.multiple_of(src * tl * tile, tile), tl * tile), :] = topin[
+                    ch, target, 2 * apart + c].reshape(tl * tile, chans).astype(F32)
+
+        place_rows(0)
+        if target > 2:
+            place_rows(1)
+
+            @pl.when(core == target - 3)
+            def _():
+                place_rows(2)
+
         for k in range(tile):
             xb[:, k * chans:(k + 1) * chans] = gather[pl.ds(k, lats, stride=tile), :].astype(BF16)
         out = dot(band[which, device].astype(BF16), xb[...])
         for k in range(tile):
             qs[pl.ds(k, n, stride=tile), :] = out[:, k * chans:(k + 1) * chans]
 
-    def relay_peak(which, ch):
-        pltpu.make_async_copy(peaks(n - 3), peaks(n - 3), row_recv.at[ch]).wait()
-        targets = (lax.rem(chip + last, chips), lax.rem(chip + 1, chips))
-        for side, z in enumerate(targets):
-            project(which, ch, side + 1, 2 * z + core)
+    def sum_rows(which, ch):
+        pltpu.make_async_copy(peaks(), peaks(), row_recv.at[ch]).wait()
+        for target, away in enumerate((-1, 1, -2, 2)):
+            project(which, ch, target + 1, across(away, core))
 
             def keep(half_at, row, degree, ours):
                 values = qs[pl.ds(pl.multiple_of(degree * tile, tile), tile), :]
-                partial[half_at, side, row] = jnp.where(ours, values, jnp.zeros_like(values))
-
-            pack(z, keep)
-        swap = to(sibling, partial.at[1 - core], mid.at[ch], mid_send.at[ch], mid_recv.at[ch])
+                partial[half_at, target, row] = jnp.where(ours, values, jnp.zeros_like(values))
+
+            pack(chip_at(away), keep)
+        swap = to(sibling, partial.at[other_core], mid.at[ch], mid_send.at[ch], mid_recv.at[ch])
         swap.start()
         if which == 1:
             pltpu.make_async_copy(sums.at[ch], sums.at[ch], sum_send.at[ch]).wait()
         swap.wait()
         sums[ch] = partial[core] + mid[ch]
-        for side, z in enumerate(targets):
-            to(2 * z + core, sums.at[ch, side], sumin.at[ch, side], sum_send.at[ch], sum_recv.at[ch]).start()
+        for side, away in enumerate((-1, 1)):
+            to(across(away, core), sums.at[ch, 2 + side], handed.at[ch, side],
+               sum_send.at[ch], hand_recv.at[ch]).start()
+
+    def pass_sums(ch):
+        pltpu.make_async_copy(handed.at[ch], handed.at[ch], hand_recv.at[ch]).wait()
+        for side, away in enumerate((-1, 1)):
+            sums[ch, side] += handed[ch, side]
+            to(across(away, core), sums.at[ch, side], sumin.at[ch, side],
+               sum_send.at[ch], sum_recv.at[ch]).start()
 
     def finish_peak(which, ch):
         pltpu.make_async_copy(sumin.at[ch], sumin.at[ch], sum_recv.at[ch]).wait()
@@ -325,7 +339,7 @@
 
         loop(n, one)
 
-    relay_peak(0, 0)
+    sum_rows(0, 0)
 
     def ship_rows(ch):
         ship(0, ch, 0, tl)
@@ -373,11 +387,14 @@
 
     loop(top, no_degree)
 
-    def relay_first(ch):
-        relay_peak(0, ch)
-
-    loop(chunks, relay_first, 1)
+    pass_sums(0)
+
+    def sum_first(ch):
+        sum_rows(0, ch)
+
+    loop(chunks, sum_first, 1)
     ship(0, final, 0, tl)
+    loop(chunks, pass_sums, 1)
 
     sign = jnp.where(lax.broadcasted_iota(jnp.int32, (tile, chans), 0) < nb, -1.0, 1.0).astype(F32)
 
@@ -432,7 +449,7 @@
 
         pack(chip, keep_top)
         if stage == 1:
-            swap = to(sibling, own.at[1 - core, 2, ch], other.at[2, ch], swap_send.at[ch], swap_recv.at[ch])
+            swap = to(sibling, own.at[other_core, 2, ch], other.at[2, ch], swap_send.at[ch], swap_recv.at[ch])
             swap.start()
         legendre(0, area, 1 - into, 0)
         load(free_slot(stage, ch))
@@ -449,13 +466,18 @@
         else:
             @pl.when(ch == 0)
             def _():
-                relay_peak(1, final)
+                pass_sums(final - 1)
+                sum_rows(1, final)
+
+            @pl.when(ch == 1)
+            def _():
+                pass_sums(final)
 
         ship(stage, ch, 0, tl)
 
     def top_copy(source, away, ch, got):
-        block = packs.at[core, lax.rem(chip + source + chips, chips), 2, ch]
-        return to(2 * lax.rem(chip + away + chips, chips) + core, block, block, top_send, got.at[ch])
+        block = packs.at[core, chip_at(source), 2, ch]
+        return to(across(away, core), block, block, top_send, got.at[ch])
 
     def top_blocks(count, ch):
         return packs.at[core, head(count), 2, ch]
@@ -527,7 +549,7 @@
 
         @pl.when(ch == 1)
         def _():
-            relay_peak(1, 0)
+            sum_rows(1, 0)
 
         slot = free_slot(2, ch)
 
@@ -555,10 +577,11 @@
 
     loop(chunks, step3_chunk)
 
-    def relay_second(ch):
-        relay_peak(1, ch)
-
-    loop(final, relay_second, 1)
+    def sum_second(ch):
+        pass_sums(ch - 1)
+        sum_rows(1, ch)
+
+    loop(final, sum_second, 1)
     ship(2, final, 0, tl)
     unit_in(dg_hbm, 0).start()
 
@@ -599,11 +622,11 @@
                 second[which, src, :, pl.ds(tile, tile)] = jnp.zeros((chunks, tile, chans), BF16)
 
     loop(n, clear_second)
-    own_copy = to(sibling, own.at[1 - core], other, own_send, own_recv)
+    own_copy = to(sibling, own.at[other_core], other, own_send, own_recv)
     own_copy.start()
 
     def pack_block(k):
-        return packs.at[core, lax.rem(chip - way * k + chips, chips)]
+        return packs.at[core, chip_at(-way * k)]
 
     def pack_copy(k):
         return to(onward, pack_block(k), pack_block(k), pack_send, pack_recv.at[k])
@@ -648,7 +671,7 @@
         @pl.when(k >= 2)
         def _():
             pair_copy(k - 2).wait_send()
-        weight_grad(wbuf.at[lax.rem(k, 2)], first_degree(block_at(k, -way), 1 - core))
+        weight_grad(wbuf.at[lax.rem(k, 2)], first_degree(block_at(k, -way), other_core))
         pair_copy(k).start()
         block = block_at(k, way)
         weight_grad(work.at[pl.ds(block * block_rows, block_rows)], first_degree(block, core))
@@ -696,7 +719,7 @@
         return to(onward, work.at[here], dw_out.at[there], rs_send, rs_recv.at[i])
 
     def add_pair(i):
-        here, passed = place(i, 1 - core)
+        here, passed = place(i, other_core)
 
         @pl.when(lax.rem(i, pieces) == 0)
         def _():
@@ -781,7 +804,7 @@
 
     loop(pieces, own_piece)
     second_publish(last)
-    gathered = packs.at[1 - core]
+    gathered = packs.at[other_core]
     pltpu.make_async_copy(gathered, gathered, share_recv).wait()
 
     def task(i):
@@ -858,7 +881,7 @@
 
 def put_kernel(df_ref, dw_ref, df_hbm, dw_hbm, sems):
     copies = []
-    for source, target, parts in ((df_ref, df_hbm, 3), (dw_ref, dw_hbm, 4)):
+    for source, target, parts in ((df_ref, df_hbm, 6), (dw_ref, dw_hbm, 12)):
         size = source.shape[0] // parts
         for k in range(parts):
             part = pl.ds(k * size, size)
@@ -920,9 +943,10 @@
                 pltpu.VMEM((2, n // 2) + packed, BF16),
                 pltpu.VMEM((2, n, chunks, 2 * nb, chans), BF16),
                 pltpu.VMEM(tables.shape, BF16),
-                pltpu.VMEM((chunks, 3, n, tl, 2 * nb, chans), BF16),
-                pltpu.VMEM((2, 2, held, 2 * nb, chans), F32),
-                pltpu.VMEM((chunks, 2, held, 2 * nb, chans), F32),
+                pltpu.VMEM((chunks, 5, 6, tl, 2 * nb, chans), BF16),
+                pltpu.VMEM((2, 4, held, 2 * nb, chans), F32),
+                pltpu.VMEM((chunks, 4, held, 2 * nb, chans), F32),
+                pltpu.VMEM((chunks, 4, held, 2 * nb, chans), F32),
                 pltpu.VMEM((chunks, 2, held, 2 * nb, chans), F32),
                 pltpu.VMEM((chunks, 2, held, 2 * nb, chans), F32),
                 pltpu.VMEM((chunks, 2, held, 2 * nb, chans), F32),
@@ -966,6 +990,7 @@
                 pltpu.SemaphoreType.DMA,
                 pltpu.SemaphoreType.DMA((n,)),
                 pltpu.SemaphoreType.DMA((n,)),
+                pltpu.SemaphoreType.DMA((chunks,)),
             ],
             compiler_params=pltpu.CompilerParams(
                 collective_id=0, has_side_effects=True, vmem_limit_bytes=43 * 1024 * 1024),
@@ -982,7 +1007,7 @@
             ),
             in_specs=[vmem] * 2,
             out_specs=(anywhere, anywhere),
-            scratch_shapes=[pltpu.SemaphoreType.DMA((7,))],
+            scratch_shapes=[pltpu.SemaphoreType.DMA((18,))],
             compiler_params=pltpu.CompilerParams(vmem_limit_bytes=1024 * 1024),
         )(grad_field, grad_w)
         return grad_field.transpose(0, 3, 1, 2), grad_w.reshape(degs, chans, 2, chans).transpose(0, 1, 3, 2)

time: 409 us -> 411 us (level)
  no operation moved by 1% of the time
where the time goes in v9:
time: 411 us; the launch traced here: 406 us
  Pallas kernels  405 us (99%)
    pallas_call x1, Pallas kernels, local_step(): pl.pallas_call(functools.partial(layer_kernel, 'lat', n, nb, pieces, per)...  399 us

profile of v9, /device:TPU:21, one launch (start us, length us, event | category | flops | bytes accessed | tf_op | source)
XLA Modules:
  0.0 406.1 jit_solution(9707091616866391487)
XLA Ops:
  0.6 398.6 %layer.1 = (f32[12,6,192,128]{3,2,1,0:T(8,128)S(1)}, f32[24576,128]{1,0:T(8,128)S(1)}) custom-call(f32[12,6,192,128]{3,2,1,0:T(8,128)} %bitcast.10, f32[12,6,192,128]{3,2,1,0:T(8,128)} %bitcast.11, f32[24576,128]{1,0:T(8,128)} %bitcast.9, f32[96,96,96]{2,1,0:T(8,128)} %pf_hbm.1, f32[96,96,96]{2,1,0:T(8,128)} %pv_hbm.1, bf16[8,192,192]{2,1,0:T(8,128)(2,1)} %constant.34.tab_hbm), custom_call_target="tpu_custom_call" | custom-call | tf_op jit(solution)/shard_map/layer/pallas_call | solution.py:916
  399.2 6.9 %put.1 = (f32[12,6,192,128]{3,2,1,0:T(8,128)}, f32[24576,128]{1,0:T(8,128)}) custom-call(f32[12,6,192,128]{3,2,1,0:T(8,128)S(1)} %get-tuple-element.6.df_ref, f32[24576,128]{1,0:T(8,128)S(1)} %get-tuple-element.7.dw_ref), custom_call_target="tpu_custom_call" | custom-call | tf_op jit(solution)/shard_map/put/pallas_call | solution.py:1001

commit v10 on v9

--- a/solution.py
+++ b/solution.py
@@ -442,7 +442,7 @@
             kept[l, ch] = x
             work[pl.ds(l * pitch, rows), :] = mix(l, x)
 
-        loop(degs, degree, unroll=2)
+        loop(degs, degree, unroll=8)
 
         def keep_top(half_at, row, degree, ours):
             own[half_at, 2, ch, row] = only(ours, work[pl.ds((top + degree) * pitch + rows - tile, tile), :])
@@ -507,9 +507,8 @@
         return both[:, :chans] + turn(both[:, chans:])
 
     def mix_adjoint(l, x):
-        real = dot(x, vmix[l, head(chans)])
-        imag = dot(x, vmix[l, pl.ds(chans, chans)])
-        return real - turn(imag)
+        both = dot(x, jnp.concatenate([vmix[l, head(chans)], vmix[l, pl.ds(chans, chans)]], axis=1))
+        return both[:, :chans] - turn(both[:, chans:])
 
     def step2_chunk(ch):
         spectral(1, ch, 0, coef, mix_forward)

time: 411 us -> 408 us (level)
  no operation moved by 1% of the time
where the time goes in v10:
time: 408 us; the launch traced here: 407 us
  Pallas kernels  406 us (100%)
    pallas_call x1, Pallas kernels, local_step(): pl.pallas_call(functools.partial(layer_kernel, 'lat', n, nb, pieces, per)...  399 us

profile of v10, /device:TPU:21, one launch (start us, length us, event | category | flops | bytes accessed | tf_op | source)
XLA Modules:
  0.0 407.0 jit_solution(1809463915406923722)
XLA Ops:
  0.6 399.5 %layer.1 = (f32[12,6,192,128]{3,2,1,0:T(8,128)S(1)}, f32[24576,128]{1,0:T(8,128)S(1)}) custom-call(f32[12,6,192,128]{3,2,1,0:T(8,128)} %bitcast.10, f32[12,6,192,128]{3,2,1,0:T(8,128)} %bitcast.11, f32[24576,128]{1,0:T(8,128)} %bitcast.9, f32[96,96,96]{2,1,0:T(8,128)} %pf_hbm.1, f32[96,96,96]{2,1,0:T(8,128)} %pv_hbm.1, bf16[8,192,192]{2,1,0:T(8,128)(2,1)} %constant.34.tab_hbm), custom_call_target="tpu_custom_call" | custom-call | tf_op jit(solution)/shard_map/layer/pallas_call | solution.py:915
  400.1 6.9 %put.1 = (f32[12,6,192,128]{3,2,1,0:T(8,128)}, f32[24576,128]{1,0:T(8,128)}) custom-call(f32[12,6,192,128]{3,2,1,0:T(8,128)S(1)} %get-tuple-element.6.df_ref, f32[24576,128]{1,0:T(8,128)S(1)} %get-tuple-element.7.dw_ref), custom_call_target="tpu_custom_call" | custom-call | tf_op jit(solution)/shard_map/put/pallas_call | solution.py:1000

commit v11 on v10

--- a/solution.py
+++ b/solution.py
@@ -55,7 +55,7 @@
 
 
 def layer_kernel(
-    axis, n, nb, pieces, per,
+    axis, n, nb, pieces, per, depth,
     f_hbm, dg_hbm, w_hbm, pf_hbm, pv_hbm, tab_hbm,
     df_out, dw_out,
     recv, send, work, xb, coef, dq, vmix, wbuf, inbuf, gather, pbuf, pmat, band, cmat, qs, own, other, packs, lowx, tab,
@@ -198,30 +198,22 @@
 
     loop(n, announce, 1)
 
-    for which, source in enumerate((pf_hbm, pv_hbm)):
-        for k in range(ml):
-            pltpu.make_async_copy(source.at[first_mode(me) + n * k], pbuf.at[which, k], p_sem.at[which]).start()
-
-    other_tables.start()
-
-    def band_in(d):
-        for which, source in enumerate((pf_hbm, pv_hbm)):
-            pltpu.make_async_copy(
-                source.at[top + first_mode(d), pl.ds(top, n)], band.at[which, d], band_sem.at[which]).start()
-
-    loop(n, band_in)
     first_tables.wait()
 
     group = max(1, tl // 3)
 
     parts = degs // per
-    depth = min(parts, work.shape[0] // (per * 2 * chans))
 
     def w_in(k):
         slot = lax.rem(k, depth)
         return pltpu.make_async_copy(
             w_hbm.at[pl.ds(k * per * 2 * chans, per * 2 * chans)],
             work.at[pl.ds(slot * per * 2 * chans, per * 2 * chans)], w_sem.at[slot])
+
+    def band_in(d):
+        for which, source in enumerate((pf_hbm, pv_hbm)):
+            pltpu.make_async_copy(
+                source.at[top + first_mode(d), pl.ds(top, n)], band.at[which, d], band_sem.at[which]).start()
 
     def step1_chunk(ch):
         slot = free_slot(0, ch)
@@ -249,6 +241,12 @@
         @pl.when(ch == 0)
         def _():
             ship(0, 0, group, tl - group)
+            other_tables.start()
+            for which, source in enumerate((pf_hbm, pv_hbm)):
+                for k in range(ml):
+                    pltpu.make_async_copy(
+                        source.at[first_mode(me) + n * k], pbuf.at[which, k], p_sem.at[which]).start()
+            loop(n, band_in)
             for k in range(depth):
                 w_in(k).start()
 
@@ -605,7 +603,7 @@
             def _():
                 more = pl.ds(tile, tile)
                 action(to(peer, kept.at[degree, :, more], second.at[which, me, :, more],
-                          some_send.at[peer], some_recv.at[me]))
+                          some_send, some_recv))
 
     def send_second(k):
         both_parts(lax.rem(me + k, n), lambda copy: copy.start())
@@ -783,13 +781,17 @@
     firsts = second.at[:, head(n - 1), :, head(tile)]
     pltpu.make_async_copy(firsts, firsts, always_recv).wait()
 
-    def wait_second(src):
-        @pl.when((first_mode(src) <= me) & (src != me))
-        def _():
-            part = second.at[:, src, :, pl.ds(tile, tile)]
-            pltpu.make_async_copy(part, part, some_recv.at[src]).wait()
-
-    loop(n, wait_second)
+    self_too = (first_mode(me) <= me).astype(jnp.int32)
+    comes, goes = me + 1 - self_too, n - first_mode(me) - self_too
+
+    def wait_some(count, sem):
+        for k in range(1, n):
+            @pl.when(count == k)
+            def _():
+                part = second.at[:, head(k), :, pl.ds(tile, tile)]
+                pltpu.make_async_copy(part, part, sem).wait()
+
+    wait_some(comes, some_recv)
     outer(wbuf.at[0], 0, [(second[1].reshape(-1, chans), second[0].reshape(-1, chans))])
     dw_out[second_spot(last)] = wbuf[0, head(wide)]
     loop(pieces, own_sum)
@@ -863,13 +865,7 @@
     pltpu.make_async_copy(sent, sent, ag_send).wait()
     pltpu.make_async_copy(firsts, firsts, always_send).wait()
 
-    def wait_some(peer):
-        @pl.when((first_mode(me) <= peer) & (peer != me))
-        def _():
-            part = second.at[:, peer, :, pl.ds(tile, tile)]
-            pltpu.make_async_copy(part, part, some_send.at[peer]).wait()
-
-    loop(n, wait_some)
+    wait_some(goes, some_send)
     sent = packs.at[0, head(last)]
     pltpu.make_async_copy(sent, sent, pack_send).wait()
     pltpu.make_async_copy(packs.at[0], packs.at[0], share_send).wait()
@@ -907,13 +903,15 @@
         pieces = 4 if half * 2 * chans % 32 == 0 else 1
         hops = (n // 2 - 1) * pieces
         per = 4
+        area = max(2 * lats * pitch, n // 2 * half * 2 * chans)
+        depth = min(degs // per, area // (per * 2 * chans))
         held = n // 2 + 1
         packed = (3, chunks, held, 2 * nb, chans)
         tables = fourier_tables(n, ml, lons)
         anywhere = pl.BlockSpec(memory_space=pl.ANY)
         vmem = pl.BlockSpec(memory_space=pltpu.VMEM)
         grad_field, grad_w = pl.pallas_call(
-            functools.partial(layer_kernel, 'lat', n, nb, pieces, per),
+            functools.partial(layer_kernel, 'lat', n, nb, pieces, per, depth),
             name='layer',
             out_shape=(
                 pltpu.VMEM((batch, tl, lons, chans), F32),
@@ -924,7 +922,7 @@
             scratch_shapes=[
                 pltpu.VMEM((2, chunks, n, tl, rows, chans), BF16),
                 pltpu.VMEM((chunks + 1, n, tl, rows, chans), BF16),
-                pltpu.VMEM((max(2 * lats * pitch, n // 2 * half * 2 * chans), chans), F32),
+                pltpu.VMEM((area, chans), F32),
                 pltpu.VMEM((lats, 2 * nb * chans), BF16),
                 pltpu.VMEM((degs, chunks, rows, chans), BF16),
                 pltpu.VMEM((degs, chunks, rows, chans), BF16),
@@ -953,7 +951,7 @@
                 pltpu.SemaphoreType.DMA((4 * chunks,)),
                 pltpu.SemaphoreType.DMA((4 * chunks,)),
                 pltpu.SemaphoreType.DMA((2,)),
-                pltpu.SemaphoreType.DMA((degs // per,)),
+                pltpu.SemaphoreType.DMA((depth,)),
                 pltpu.SemaphoreType.DMA((2,)),
                 pltpu.SemaphoreType.DMA((2,)),
                 pltpu.SemaphoreType.DMA((2,)),
@@ -987,8 +985,8 @@
                 pltpu.SemaphoreType.DMA((chunks,)),
                 pltpu.SemaphoreType.DMA,
                 pltpu.SemaphoreType.DMA,
-                pltpu.SemaphoreType.DMA((n,)),
-                pltpu.SemaphoreType.DMA((n,)),
+                pltpu.SemaphoreType.DMA,
+                pltpu.SemaphoreType.DMA,
                 pltpu.SemaphoreType.DMA((chunks,)),
             ],
             compiler_params=pltpu.CompilerParams(

time: 408 us -> 408 us (level)
  no operation moved by 1% of the time
where the time goes in v11:
time: 408 us; the launch traced here: 404 us
  Pallas kernels  403 us (99%)
    pallas_call x1, Pallas kernels, local_step(): pl.pallas_call(functools.partial(layer_kernel, 'lat', n, nb, pieces, per,...  396 us

profile of v11, /device:TPU:21, one launch (start us, length us, event | category | flops | bytes accessed | tf_op | source)
XLA Modules:
  0.0 403.9 jit_solution(2043065030072245657)
XLA Ops:
  0.6 396.4 %layer.1 = (f32[12,6,192,128]{3,2,1,0:T(8,128)S(1)}, f32[24576,128]{1,0:T(8,128)S(1)}) custom-call(f32[12,6,192,128]{3,2,1,0:T(8,128)} %bitcast.10, f32[12,6,192,128]{3,2,1,0:T(8,128)} %bitcast.11, f32[24576,128]{1,0:T(8,128)} %bitcast.9, f32[96,96,96]{2,1,0:T(8,128)} %pf_hbm.1, f32[96,96,96]{2,1,0:T(8,128)} %pv_hbm.1, bf16[8,192,192]{2,1,0:T(8,128)(2,1)} %constant.34.tab_hbm), custom_call_target="tpu_custom_call" | custom-call | tf_op jit(solution)/shard_map/layer/pallas_call | solution.py:913
  397.1 6.9 %put.1 = (f32[12,6,192,128]{3,2,1,0:T(8,128)}, f32[24576,128]{1,0:T(8,128)}) custom-call(f32[12,6,192,128]{3,2,1,0:T(8,128)S(1)} %get-tuple-element.6.df_ref, f32[24576,128]{1,0:T(8,128)S(1)} %get-tuple-element.7.dw_ref), custom_call_target="tpu_custom_call" | custom-call | tf_op jit(solution)/shard_map/put/pallas_call | solution.py:998

commit v12 on v11

--- a/solution.py
+++ b/solution.py
@@ -594,12 +594,12 @@
         pack(chip, keep_low)
 
     def both_parts(peer, action):
-        degree = n + peer
+        degree = n + first_mode(peer)
         for which, kept in enumerate((coef, dq)):
             action(to(peer, kept.at[degree, :, head(tile)], second.at[which, me, :, head(tile)],
                       always_send, always_recv))
 
-            @pl.when(first_mode(me) <= peer)
+            @pl.when(first_mode(me) <= first_mode(peer))
             def _():
                 more = pl.ds(tile, tile)
                 action(to(peer, kept.at[degree, :, more], second.at[which, me, :, more],
@@ -610,10 +610,10 @@
 
     loop(n, send_second, 1)
     for which, kept in enumerate((coef, dq)):
-        second[which, me] = kept[n + me, :, head(2 * tile)]
+        second[which, me] = kept[n + first_mode(me), :, head(2 * tile)]
 
     def clear_second(src):
-        @pl.when(first_mode(src) > me)
+        @pl.when(first_mode(src) > first_mode(me))
         def _():
             for which in range(2):
                 second[which, src, :, pl.ds(tile, tile)] = jnp.zeros((chunks, tile, chans), BF16)
@@ -760,7 +760,7 @@
         ag_copy(i, s).start()
 
     def second_spot(k):
-        return pl.ds((n + 2 * block_at(k, way) + core) * wide, wide)
+        return pl.ds((n + first_mode(2 * block_at(k, way) + core)) * wide, wide)
 
     def second_copy(k, got):
         spot = dw_out.at[second_spot(k)]
@@ -781,8 +781,7 @@
     firsts = second.at[:, head(n - 1), :, head(tile)]
     pltpu.make_async_copy(firsts, firsts, always_recv).wait()
 
-    self_too = (first_mode(me) <= me).astype(jnp.int32)
-    comes, goes = me + 1 - self_too, n - first_mode(me) - self_too
+    comes, goes = first_mode(me), n - 1 - first_mode(me)
 
     def wait_some(count, sem):
         for k in range(1, n):

time: 408 us -> 408 us (level)
  no operation moved by 1% of the time
where the time goes in v12:
time: 408 us; the launch traced here: 404 us
  Pallas kernels  404 us (99%)
    pallas_call x1, Pallas kernels, local_step(): pl.pallas_call(functools.partial(layer_kernel, 'lat', n, nb, pieces, per,...  397 us

profile of v12, /device:TPU:21, one launch (start us, length us, event | category | flops | bytes accessed | tf_op | source)
XLA Modules:
  0.0 404.2 jit_solution(12611569816302666806)
XLA Ops:
  0.6 396.7 %layer.1 = (f32[12,6,192,128]{3,2,1,0:T(8,128)S(1)}, f32[24576,128]{1,0:T(8,128)S(1)}) custom-call(f32[12,6,192,128]{3,2,1,0:T(8,128)} %bitcast.10, f32[12,6,192,128]{3,2,1,0:T(8,128)} %bitcast.11, f32[24576,128]{1,0:T(8,128)} %bitcast.9, f32[96,96,96]{2,1,0:T(8,128)} %pf_hbm.1, f32[96,96,96]{2,1,0:T(8,128)} %pv_hbm.1, bf16[8,192,192]{2,1,0:T(8,128)(2,1)} %constant.34.tab_hbm), custom_call_target="tpu_custom_call" | custom-call | tf_op jit(solution)/shard_map/layer/pallas_call | solution.py:912
  397.3 6.9 %put.1 = (f32[12,6,192,128]{3,2,1,0:T(8,128)}, f32[24576,128]{1,0:T(8,128)}) custom-call(f32[12,6,192,128]{3,2,1,0:T(8,128)S(1)} %get-tuple-element.6.df_ref, f32[24576,128]{1,0:T(8,128)S(1)} %get-tuple-element.7.dw_ref), custom_call_target="tpu_custom_call" | custom-call | tf_op jit(solution)/shard_map/put/pallas_call | solution.py:997

commit v13 on v12

--- a/solution.py
+++ b/solution.py
@@ -108,15 +108,24 @@
     def unit_of(unit):
         return lax.div(unit, tl), lax.rem(unit, tl)
 
+    ahead = inbuf.shape[0] - 1
+
     def unit_in(src, unit):
         ch, t = unit_of(unit)
-        slot = lax.rem(unit, 2)
+        slot = in_slot(unit)
         return pltpu.make_async_copy(src.at[pl.ds(ch * nb, nb), t], inbuf.at[slot], in_sem.at[slot])
 
+    def in_slot(unit):
+        return lax.rem(unit, ahead + 1)
+
+    def start_in(src, first=0):
+        for unit in range(first, ahead):
+            unit_in(src, unit).start()
+
     def step_in(src, unit):
-        @pl.when(unit + 1 < units)
-        def _():
-            unit_in(src, unit + 1).start()
+        @pl.when(unit + ahead < units)
+        def _():
+            unit_in(src, unit + ahead).start()
         unit_in(src, unit).wait()
 
     body, peak = head(rows - tile), pl.ds(rows - tile, tile)
@@ -191,6 +200,7 @@
     first_tables = pltpu.make_async_copy(tab_hbm.at[head(2)], tab.at[head(2)], tab_sem.at[0])
     other_tables = pltpu.make_async_copy(tab_hbm.at[pl.ds(2, 6)], tab.at[pl.ds(2, 6)], tab_sem.at[1])
     first_tables.start()
+    start_in(f_hbm, 1)
     barrier = pltpu.get_barrier_semaphore()
 
     def announce(k):
@@ -221,7 +231,7 @@
         def row(t):
             unit = ch * tl + t
             step_in(f_hbm, unit)
-            buf = lax.rem(unit, 2)
+            buf = in_slot(unit)
             for b in range(0, nb, 2):
                 pair = jnp.concatenate([inbuf[buf, b], inbuf[buf, b + 1]], axis=1)
                 spec = transform(pair, fwd_h, fwd_l)
@@ -253,7 +263,7 @@
 
     loop(chunks, step1_chunk)
 
-    unit_in(dg_hbm, 0).start()
+    start_in(dg_hbm)
     for which in range(2):
         pltpu.make_async_copy(band.at[which], band.at[which], band_sem.at[which]).wait()
     qs[...] = jnp.zeros_like(qs)
@@ -553,7 +563,7 @@
         def row(t):
             unit = ch * tl + t
             step_in(dg_hbm, unit)
-            buf = lax.rem(unit, 2)
+            buf = in_slot(unit)
             fetch_rows(1, ch, t)
             for b in range(0, nb, 2):
                 g = fetch_pair(b)
@@ -580,7 +590,7 @@
 
     loop(final, sum_second, 1)
     ship(2, final, 0, tl)
-    unit_in(dg_hbm, 0).start()
+    start_in(dg_hbm)
 
     def step4_chunk(ch):
         spectral(3, ch, 1, dq, mix_adjoint)
@@ -697,7 +707,7 @@
         ch, t = unit_of(unit)
 
         step_in(dg_hbm, unit)
-        buf = lax.rem(unit, 2)
+        buf = in_slot(unit)
 
         fetch_rows(3, ch, t)
         for b in range(0, nb, 2):
@@ -927,7 +937,7 @@
                 pltpu.VMEM((degs, chunks, rows, chans), BF16),
                 pltpu.VMEM((degs, 2 * chans, chans), BF16),
                 pltpu.VMEM((2, max(per, half) * 2 * chans, chans), F32),
-                pltpu.VMEM((2, nb, lons, chans), F32),
+                pltpu.VMEM((4, nb, lons, chans), F32),
                 pltpu.VMEM((n * rows, chans), F32),
                 pltpu.VMEM((2, ml, degs, lats), F32),
                 pltpu.VMEM((2, ml, degs, lats), BF16),
@@ -949,7 +959,7 @@
                 pltpu.VMEM((2, n, chunks, 4 * nb, chans), BF16),
                 pltpu.SemaphoreType.DMA((4 * chunks,)),
                 pltpu.SemaphoreType.DMA((4 * chunks,)),
-                pltpu.SemaphoreType.DMA((2,)),
+                pltpu.SemaphoreType.DMA((4,)),
                 pltpu.SemaphoreType.DMA((depth,)),
                 pltpu.SemaphoreType.DMA((2,)),
                 pltpu.SemaphoreType.DMA((2,)),

time: 408 us -> 408 us (level)
  no operation moved by 1% of the time
where the time goes in v13:
time: 408 us; the launch traced here: 406 us
  Pallas kernels  405 us (99%)
    pallas_call x1, Pallas kernels, local_step(): pl.pallas_call(functools.partial(layer_kernel, 'lat', n, nb, pieces, per,...  398 us

profile of v13, /device:TPU:21, one launch (start us, length us, event | category | flops | bytes accessed | tf_op | source)
XLA Modules:
  0.0 405.6 jit_solution(9819972089014306332)
XLA Ops:
  0.6 398.1 %layer.1 = (f32[12,6,192,128]{3,2,1,0:T(8,128)S(1)}, f32[24576,128]{1,0:T(8,128)S(1)}) custom-call(f32[12,6,192,128]{3,2,1,0:T(8,128)} %bitcast.10, f32[12,6,192,128]{3,2,1,0:T(8,128)} %bitcast.11, f32[24576,128]{1,0:T(8,128)} %bitcast.9, f32[96,96,96]{2,1,0:T(8,128)} %pf_hbm.1, f32[96,96,96]{2,1,0:T(8,128)} %pv_hbm.1, bf16[8,192,192]{2,1,0:T(8,128)(2,1)} %constant.34.tab_hbm), custom_call_target="tpu_custom_call" | custom-call | tf_op jit(solution)/shard_map/layer/pallas_call | solution.py:922
  398.7 6.9 %put.1 = (f32[12,6,192,128]{3,2,1,0:T(8,128)}, f32[24576,128]{1,0:T(8,128)}) custom-call(f32[12,6,192,128]{3,2,1,0:T(8,128)S(1)} %get-tuple-element.6.df_ref, f32[24576,128]{1,0:T(8,128)S(1)} %get-tuple-element.7.dw_ref), custom_call_target="tpu_custom_call" | custom-call | tf_op jit(solution)/shard_map/put/pallas_call | solution.py:1007

commit v14 on v12

--- a/solution.py
+++ b/solution.py
@@ -24,9 +24,9 @@
     device = np.arange(n)
     first = np.where(device % 2 == 0, device // 2, n - 1 - device // 2)
     order = (first[:, None] + n * np.arange(ml)[None, :]).reshape(-1)
-    angle = 2.0 * np.pi * (np.outer(order, np.arange(lons)) % lons) / lons
+    angle = math.tau * (np.outer(order, np.arange(lons)) % lons) / lons
     forward = np.stack([np.cos(angle), -np.sin(angle)], axis=1).reshape(2 * modes, lons) / math.sqrt(lons)
-    gains = np.repeat(np.where(order == 0, 1.0, 2.0), 2)[:, None]
+    gains = np.repeat(2.0 - (order == 0), 2)[:, None]
     doubled = forward * gains
     tables = split_const(forward) + split_const(doubled) + split_const(doubled.T) + split_const(forward.T)
     return jnp.stack([jnp.asarray(t) for t in tables])
@@ -34,7 +34,7 @@
 
 def gelu_grad(values):
     cumulative = 0.5 * (1.0 + lax.erf(values * math.sqrt(0.5)))
-    density = jnp.exp(-0.5 * values * values) / math.sqrt(2.0 * math.pi)
+    density = jnp.exp(-0.5 * values * values) / math.sqrt(math.tau)
     return cumulative + values * density
 
 
@@ -96,6 +96,10 @@
 
     onward = across(way, core)
 
+    def around(k):
+        far = chips // 2 - lax.div(k + 1, 2)
+        return jnp.where(lax.rem(k, 2) == 0, far, -far)
+
     def first_mode(device):
         z = lax.div(device, 2)
         return jnp.where(lax.rem(device, 2) == 0, z, n - 1 - z)
@@ -127,11 +131,15 @@
         part = pl.ds(t0, nt)
 
         def one(k):
-            peer = lax.rem(me + k, n)
-            to(peer, send.at[slot, peer, part, body], recv.at[stage % 2, ch, me, part, body],
-               send_sem.at[index], recv_sem.at[index]).start()
-
-        loop(n, one, 1)
+            away = around(k)
+            for its_core in (core, other_core):
+                peer = across(away, its_core)
+                to(peer, send.at[slot, peer, part, body], recv.at[stage % 2, ch, me, part, body],
+                   send_sem.at[index], recv_sem.at[index]).start()
+
+        loop(last, one)
+        to(sibling, send.at[slot, sibling, part, body], recv.at[stage % 2, ch, me, part, body],
+           send_sem.at[index], recv_sem.at[index]).start()
         recv[stage % 2, ch, me, part, body] = send[slot, me, part, body]
 
     def arrived(stage, ch):
@@ -989,7 +997,7 @@
                 pltpu.SemaphoreType.DMA((chunks,)),
             ],
             compiler_params=pltpu.CompilerParams(
-                collective_id=0, has_side_effects=True, vmem_limit_bytes=43 * 1024 * 1024),
+                collective_id=0, has_side_effects=True, vmem_limit_bytes=43 << 20),
         )(
             field_loc.transpose(0, 2, 3, 1), grad_loc.transpose(0, 2, 3, 1),
             w_mix.transpose(0, 1, 3, 2).reshape(degs * 2 * chans, chans),
@@ -1004,7 +1012,7 @@
             in_specs=[vmem] * 2,
             out_specs=(anywhere, anywhere),
             scratch_shapes=[pltpu.SemaphoreType.DMA((18,))],
-            compiler_params=pltpu.CompilerParams(vmem_limit_bytes=1024 * 1024),
+            compiler_params=pltpu.CompilerParams(vmem_limit_bytes=1 << 20),
         )(grad_field, grad_w)
         return grad_field.transpose(0, 3, 1, 2), grad_w.reshape(degs, chans, 2, chans).transpose(0, 1, 3, 2)
 

time: 408 us -> 407 us (level)
  no operation moved by 1% of the time
where the time goes in v14:
time: 407 us; the launch traced here: 406 us
  Pallas kernels  405 us (100%)
    pallas_call x1, Pallas kernels, local_step(): pl.pallas_call(functools.partial(layer_kernel, 'lat', n, nb, pieces, per,...  398 us

profile of v14, /device:TPU:21, one launch (start us, length us, event | category | flops | bytes accessed | tf_op | source)
XLA Modules:
  0.0 405.8 jit_solution(9637159578659380288)
XLA Ops:
  0.6 398.3 %layer.1 = (f32[12,6,192,128]{3,2,1,0:T(8,128)S(1)}, f32[24576,128]{1,0:T(8,128)S(1)}) custom-call(f32[12,6,192,128]{3,2,1,0:T(8,128)} %bitcast.10, f32[12,6,192,128]{3,2,1,0:T(8,128)} %bitcast.11, f32[24576,128]{1,0:T(8,128)} %bitcast.9, f32[96,96,96]{2,1,0:T(8,128)} %pf_hbm.1, f32[96,96,96]{2,1,0:T(8,128)} %pv_hbm.1, bf16[8,192,192]{2,1,0:T(8,128)(2,1)} %constant.34.tab_hbm), custom_call_target="tpu_custom_call" | custom-call | tf_op jit(solution)/shard_map/layer/pallas_call | solution.py:920
  398.9 6.9 %put.1 = (f32[12,6,192,128]{3,2,1,0:T(8,128)}, f32[24576,128]{1,0:T(8,128)}) custom-call(f32[12,6,192,128]{3,2,1,0:T(8,128)S(1)} %get-tuple-element.6.df_ref, f32[24576,128]{1,0:T(8,128)S(1)} %get-tuple-element.7.dw_ref), custom_call_target="tpu_custom_call" | custom-call | tf_op jit(solution)/shard_map/put/pallas_call | solution.py:1005

commit v15 on v14

--- a/solution.py
+++ b/solution.py
@@ -38,12 +38,12 @@
     return cumulative + values * density
 
 
-def loop(stop, step, start=0, unroll=None):
+def loop(stop, step, start=0, **options):
     def one(i, carry):
         step(i)
         return carry
 
-    lax.fori_loop(start, stop, one, 0, unroll=unroll)
+    lax.fori_loop(start, stop, one, 0, **options)
 
 
 def head(size):
@@ -62,7 +62,7 @@
     topin, partial, mid, sums, sumin, joined, handed, second,
     send_sem, recv_sem, in_sem, w_sem, p_sem, band_sem, pair_send, pair_recv, rs_send, rs_recv, ag_send, ag_recv,
     free_sem, pub_send, pub_recv, own_send, own_recv, pack_send, pack_recv, share_send, share_recv,
-    tab_sem, top_send, near_recv, far_recv, swap_send, swap_recv,
+    tab_sem, top_send, near_recv, far_recv, next_recv, swap_send, swap_recv,
     row_send, row_recv, mid_send, mid_recv, sum_send, sum_recv, join_send, join_recv,
     always_send, always_recv, some_send, some_recv, hand_recv,
 ):
@@ -86,6 +86,7 @@
     chips = n // 2
     last = chips - 1
     way = 1 - 2 * core
+    sides = (-1, 1)
     sibling = me + way
 
     def chip_at(away):
@@ -315,13 +316,13 @@
             pltpu.make_async_copy(sums.at[ch], sums.at[ch], sum_send.at[ch]).wait()
         swap.wait()
         sums[ch] = partial[core] + mid[ch]
-        for side, away in enumerate((-1, 1)):
+        for side, away in enumerate(sides):
             to(across(away, core), sums.at[ch, 2 + side], handed.at[ch, side],
                sum_send.at[ch], hand_recv.at[ch]).start()
 
     def pass_sums(ch):
         pltpu.make_async_copy(handed.at[ch], handed.at[ch], hand_recv.at[ch]).wait()
-        for side, away in enumerate((-1, 1)):
+        for side, away in enumerate(sides):
             sums[ch, side] += handed[ch, side]
             to(across(away, core), sums.at[ch, side], sumin.at[ch, side],
                sum_send.at[ch], sum_recv.at[ch]).start()
@@ -463,11 +464,11 @@
             swap.wait()
             packs[core, chip, 2, ch] = (own[core, 2, ch].astype(F32) + other[2, ch].astype(F32)).astype(BF16)
 
-            @pl.when(ch >= 2)
-            def _():
-                relay_top(ch - 2)
-
-            for away in (2, -2):
+            @pl.when(ch == final - 1)
+            def _():
+                relay_near(ch - 1)
+
+            for away in sides:
                 top_copy(0, away, ch, near_recv).start()
         else:
             @pl.when(ch == 0)
@@ -479,7 +480,12 @@
             def _():
                 pass_sums(final)
 
-        ship(stage, ch, 0, tl)
+        if stage == 1:
+            @pl.when(ch < final)
+            def _():
+                ship(stage, ch, 0, tl)
+        else:
+            ship(stage, ch, 0, tl)
 
     def top_copy(source, away, ch, got):
         block = packs.at[core, chip_at(source), 2, ch]
@@ -488,11 +494,15 @@
     def top_blocks(count, ch):
         return packs.at[core, head(count), 2, ch]
 
-    def relay_top(ch):
+    def relay_near(ch):
         pltpu.make_async_copy(top_blocks(2, ch), top_blocks(2, ch), near_recv.at[ch]).wait()
-        for source in (2, -2):
-            for away in (1, -1):
-                top_copy(source, away, ch, far_recv).start()
+        for side in sides:
+            top_copy(-side, side, ch, next_recv).start()
+
+    def relay_next(ch):
+        pltpu.make_async_copy(top_blocks(2, ch), top_blocks(2, ch), next_recv.at[ch]).wait()
+        for side in sides:
+            top_copy(-2 * side, side, ch, far_recv).start()
         top_copy(-2 * way, 2 * way, ch, far_recv).start()
 
     def apply_top(which, ch, z):
@@ -520,7 +530,9 @@
         spectral(1, ch, 0, coef, mix_forward)
 
     loop(chunks, step2_chunk)
-    relay_top(chunks - 2)
+    relay_next(final - 2)
+    relay_near(final - 1)
+    ship(1, final, 0, tl)
 
     def fetch_rows(stage, ch, t):
         for src in range(n):
@@ -532,13 +544,19 @@
 
     def step3_chunk(ch):
         arrived(1, ch)
-        pltpu.make_async_copy(top_blocks(5, ch), top_blocks(5, ch), far_recv.at[ch]).wait()
+
+        @pl.when(ch == 0)
+        def _():
+            relay_near(final)
+            relay_next(final - 1)
+
+        pltpu.make_async_copy(top_blocks(3, ch), top_blocks(3, ch), far_recv.at[ch]).wait()
         swap = to(sibling, top_blocks(chips, ch), top_blocks(chips, ch), swap_send.at[ch], swap_recv.at[ch])
         swap.start()
 
-        @pl.when(ch == 0)
-        def _():
-            relay_top(final)
+        @pl.when(ch == 1)
+        def _():
+            relay_next(final)
 
         swap.wait()
 
@@ -896,7 +914,7 @@
 
 def solution(mesh):
     n = mesh.shape['lat']
-    field_spec = P('member', None, 'lat', None)
+    field_spec = P('member', None, 'lat')
 
     def local_step(field_loc, grad_loc, p_fwd, p_inv, w_mix):
         batch, chans, tl, lons = field_loc.shape
@@ -990,6 +1008,7 @@
                 pltpu.SemaphoreType.DMA((chunks,)),
                 pltpu.SemaphoreType.DMA((chunks,)),
                 pltpu.SemaphoreType.DMA((chunks,)),
+                pltpu.SemaphoreType.DMA((chunks,)),
                 pltpu.SemaphoreType.DMA,
                 pltpu.SemaphoreType.DMA,
                 pltpu.SemaphoreType.DMA,
@@ -1018,4 +1037,4 @@
 
     return jax.shard_map(
         local_step, mesh=mesh, in_specs=(field_spec, field_spec, P(), P(), P()),
-        out_specs=(field_spec, P('member', None, None, None)), check_vma=False)
+        out_specs=(field_spec, P('member')), check_vma=False)

time: 407 us -> 408 us (level)
  no operation moved by 1% of the time
where the time goes in v15:
time: 408 us; the launch traced here: 407 us
  Pallas kernels  406 us (100%)
    pallas_call x1, Pallas kernels, local_step(): pl.pallas_call(functools.partial(layer_kernel, 'lat', n, nb, pieces, per,...  399 us

profile of v15, /device:TPU:21, one launch (start us, length us, event | category | flops | bytes accessed | tf_op | source)
XLA Modules:
  0.0 407.0 jit_solution(17872383722363771192)
XLA Ops:
  0.6 399.5 %layer.1 = (f32[12,6,192,128]{3,2,1,0:T(8,128)S(1)}, f32[24576,128]{1,0:T(8,128)S(1)}) custom-call(f32[12,6,192,128]{3,2,1,0:T(8,128)} %bitcast.10, f32[12,6,192,128]{3,2,1,0:T(8,128)} %bitcast.11, f32[24576,128]{1,0:T(8,128)} %bitcast.9, f32[96,96,96]{2,1,0:T(8,128)} %pf_hbm.1, f32[96,96,96]{2,1,0:T(8,128)} %pv_hbm.1, bf16[8,192,192]{2,1,0:T(8,128)(2,1)} %constant.34.tab_hbm), custom_call_target="tpu_custom_call" | custom-call | tf_op jit(solution)/shard_map/layer/pallas_call | solution.py:938
  400.1 6.9 %put.1 = (f32[12,6,192,128]{3,2,1,0:T(8,128)}, f32[24576,128]{1,0:T(8,128)}) custom-call(f32[12,6,192,128]{3,2,1,0:T(8,128)S(1)} %get-tuple-element.6.df_ref, f32[24576,128]{1,0:T(8,128)S(1)} %get-tuple-element.7.dw_ref), custom_call_target="tpu_custom_call" | custom-call | tf_op jit(solution)/shard_map/put/pallas_call | solution.py:1024

commit v16 on v15

--- a/solution.py
+++ b/solution.py
@@ -136,11 +136,11 @@
             for its_core in (core, other_core):
                 peer = across(away, its_core)
                 to(peer, send.at[slot, peer, part, body], recv.at[stage % 2, ch, me, part, body],
-                   send_sem.at[index], recv_sem.at[index]).start()
+                   send_sem.at[slot], recv_sem.at[index]).start()
 
         loop(last, one)
         to(sibling, send.at[slot, sibling, part, body], recv.at[stage % 2, ch, me, part, body],
-           send_sem.at[index], recv_sem.at[index]).start()
+           send_sem.at[slot], recv_sem.at[index]).start()
         recv[stage % 2, ch, me, part, body] = send[slot, me, part, body]
 
     def arrived(stage, ch):
@@ -151,8 +151,9 @@
         return send.at[0, head(n - 5), :, peak]
 
     def wait_sent(index, stage):
-        others = send.at[lax.rem(index, slots), head(n - 1), :, body]
-        pltpu.make_async_copy(others, others, send_sem.at[index]).wait()
+        slot = lax.rem(index, slots)
+        others = send.at[slot, head(n - 1), :, body]
+        pltpu.make_async_copy(others, others, send_sem.at[slot]).wait()
         if stage % 2 == 0:
             ch = index - stage * chunks
             pltpu.make_async_copy(peaks(), peaks(), row_send.at[ch]).wait()
@@ -310,7 +311,7 @@
                 partial[half_at, target, row] = jnp.where(ours, values, jnp.zeros_like(values))
 
             pack(chip_at(away), keep)
-        swap = to(sibling, partial.at[other_core], mid.at[ch], mid_send.at[ch], mid_recv.at[ch])
+        swap = to(sibling, partial.at[other_core], mid.at[ch], mid_send, mid_recv.at[ch])
         swap.start()
         if which == 1:
             pltpu.make_async_copy(sums.at[ch], sums.at[ch], sum_send.at[ch]).wait()
@@ -330,7 +331,7 @@
     def finish_peak(which, ch):
         pltpu.make_async_copy(sumin.at[ch], sumin.at[ch], sum_recv.at[ch]).wait()
         joined[ch, core] = sumin[ch, 0] + sumin[ch, 1]
-        swap = to(sibling, joined.at[ch, core], joined.at[ch, core], join_send.at[ch], join_recv.at[ch])
+        swap = to(sibling, joined.at[ch, core], joined.at[ch, core], join_send, join_recv.at[ch])
         swap.start()
         project(which, ch, 0, me)
         swap.wait()
@@ -456,7 +457,7 @@
 
         pack(chip, keep_top)
         if stage == 1:
-            swap = to(sibling, own.at[other_core, 2, ch], other.at[2, ch], swap_send.at[ch], swap_recv.at[ch])
+            swap = to(sibling, own.at[other_core, 2, ch], other.at[2, ch], swap_send, swap_recv.at[ch])
             swap.start()
         legendre(0, area, 1 - into, 0)
         load(free_slot(stage, ch))
@@ -551,7 +552,7 @@
             relay_next(final - 1)
 
         pltpu.make_async_copy(top_blocks(3, ch), top_blocks(3, ch), far_recv.at[ch]).wait()
-        swap = to(sibling, top_blocks(chips, ch), top_blocks(chips, ch), swap_send.at[ch], swap_recv.at[ch])
+        swap = to(sibling, top_blocks(chips, ch), top_blocks(chips, ch), swap_send, swap_recv.at[ch])
         swap.start()
 
         @pl.when(ch == 1)
@@ -973,7 +974,7 @@
                 pltpu.VMEM((chunks, 2, held, 2 * nb, chans), F32),
                 pltpu.VMEM((chunks, 2, held, 2 * nb, chans), F32),
                 pltpu.VMEM((2, n, chunks, 4 * nb, chans), BF16),
-                pltpu.SemaphoreType.DMA((4 * chunks,)),
+                pltpu.SemaphoreType.DMA((chunks + 1,)),
                 pltpu.SemaphoreType.DMA((4 * chunks,)),
                 pltpu.SemaphoreType.DMA((2,)),
                 pltpu.SemaphoreType.DMA((depth,)),
@@ -999,15 +1000,15 @@
                 pltpu.SemaphoreType.DMA((chunks,)),
                 pltpu.SemaphoreType.DMA((chunks,)),
                 pltpu.SemaphoreType.DMA((chunks,)),
+                pltpu.SemaphoreType.DMA,
                 pltpu.SemaphoreType.DMA((chunks,)),
                 pltpu.SemaphoreType.DMA((chunks,)),
                 pltpu.SemaphoreType.DMA((chunks,)),
+                pltpu.SemaphoreType.DMA,
                 pltpu.SemaphoreType.DMA((chunks,)),
                 pltpu.SemaphoreType.DMA((chunks,)),
                 pltpu.SemaphoreType.DMA((chunks,)),
-                pltpu.SemaphoreType.DMA((chunks,)),
-                pltpu.SemaphoreType.DMA((chunks,)),
-                pltpu.SemaphoreType.DMA((chunks,)),
+                pltpu.SemaphoreType.DMA,
                 pltpu.SemaphoreType.DMA((chunks,)),
                 pltpu.SemaphoreType.DMA,
                 pltpu.SemaphoreType.DMA,

time: 408 us -> 406 us (level)
  no operation moved by 1% of the time
where the time goes in v16:
time: 406 us
  Pallas kernels  405 us (100%)
    pallas_call x1, Pallas kernels, local_step(): pl.pallas_call(functools.partial(layer_kernel, 'lat', n, nb, pieces, per,...  398 us

profile of v16, /device:TPU:21, one launch (start us, length us, event | category | flops | bytes accessed | tf_op | source)
XLA Modules:
  0.0 405.7 jit_solution(17256682180061161556)
XLA Ops:
  0.6 398.2 %layer.1 = (f32[12,6,192,128]{3,2,1,0:T(8,128)S(1)}, f32[24576,128]{1,0:T(8,128)S(1)}) custom-call(f32[12,6,192,128]{3,2,1,0:T(8,128)} %bitcast.10, f32[12,6,192,128]{3,2,1,0:T(8,128)} %bitcast.11, f32[24576,128]{1,0:T(8,128)} %bitcast.9, f32[96,96,96]{2,1,0:T(8,128)} %pf_hbm.1, f32[96,96,96]{2,1,0:T(8,128)} %pv_hbm.1, bf16[8,192,192]{2,1,0:T(8,128)(2,1)} %constant.34.tab_hbm), custom_call_target="tpu_custom_call" | custom-call | tf_op jit(solution)/shard_map/layer/pallas_call | solution.py:939
  398.8 6.9 %put.1 = (f32[12,6,192,128]{3,2,1,0:T(8,128)}, f32[24576,128]{1,0:T(8,128)}) custom-call(f32[12,6,192,128]{3,2,1,0:T(8,128)S(1)} %get-tuple-element.6.df_ref, f32[24576,128]{1,0:T(8,128)S(1)} %get-tuple-element.7.dw_ref), custom_call_target="tpu_custom_call" | custom-call | tf_op jit(solution)/shard_map/put/pallas_call | solution.py:1025

commit v17 on v16

--- a/solution.py
+++ b/solution.py
@@ -851,6 +851,8 @@
         def _():
             low_degree(i)
 
+    share_of = -(-(chips + units) // hops)
+
     def ag_step(i):
         ag_copy(i, i).wait_recv()
 
@@ -871,14 +873,10 @@
 
             second_publish(k)
 
-        task(i)
+        for j in range(share_of):
+            task(i * share_of + j)
 
     loop(hops, ag_step)
-
-    def rest(i):
-        task(i)
-
-    loop(max(hops, chips + units, n), rest, hops)
 
     wait_sent(2 * chunks + final, 2)
     for ch in range(chunks):
@@ -926,7 +924,7 @@
         rows = ml * 2 * nb
         pitch = rows + 1
         half = degs // n - 2
-        pieces = 4 if half * 2 * chans % 32 == 0 else 1
+        pieces = 2 if half * 2 * chans % 32 == 0 else 1
         hops = (n // 2 - 1) * pieces
         per = 4
         area = max(2 * lats * pitch, n // 2 * half * 2 * chans)

time: 406 us -> 406 us (level)
  no operation moved by 1% of the time
where the time goes in v17:
time: 406 us; the launch traced here: 405 us
  Pallas kernels  405 us (100%)
    pallas_call x1, Pallas kernels, local_step(): pl.pallas_call(functools.partial(layer_kernel, 'lat', n, nb, pieces, per,...  398 us

profile of v17, /device:TPU:21, one launch (start us, length us, event | category | flops | bytes accessed | tf_op | source)
XLA Modules:
  0.0 405.4 jit_solution(1518752044382139986)
XLA Ops:
  0.6 397.9 %layer.1 = (f32[12,6,192,128]{3,2,1,0:T(8,128)S(1)}, f32[24576,128]{1,0:T(8,128)S(1)}) custom-call(f32[12,6,192,128]{3,2,1,0:T(8,128)} %bitcast.10, f32[12,6,192,128]{3,2,1,0:T(8,128)} %bitcast.11, f32[24576,128]{1,0:T(8,128)} %bitcast.9, f32[96,96,96]{2,1,0:T(8,128)} %pf_hbm.1, f32[96,96,96]{2,1,0:T(8,128)} %pv_hbm.1, bf16[8,192,192]{2,1,0:T(8,128)(2,1)} %constant.34.tab_hbm), custom_call_target="tpu_custom_call" | custom-call | tf_op jit(solution)/shard_map/layer/pallas_call | solution.py:937
  398.5 6.9 %put.1 = (f32[12,6,192,128]{3,2,1,0:T(8,128)}, f32[24576,128]{1,0:T(8,128)}) custom-call(f32[12,6,192,128]{3,2,1,0:T(8,128)S(1)} %get-tuple-element.6.df_ref, f32[24576,128]{1,0:T(8,128)S(1)} %get-tuple-element.7.dw_ref), custom_call_target="tpu_custom_call" | custom-call | tf_op jit(solution)/shard_map/put/pallas_call | solution.py:1023

commit v18 on v17

--- a/solution.py
+++ b/solution.py
@@ -210,7 +210,7 @@
 
     first_tables.wait()
 
-    group = max(1, tl // 3)
+    group = 1
 
     parts = degs // per
 

time: 406 us -> 409 us (level)
  no operation moved by 1% of the time
where the time goes in v18:
time: 409 us; the launch traced here: 406 us
  Pallas kernels  405 us (99%)
    pallas_call x1, Pallas kernels, local_step(): pl.pallas_call(functools.partial(layer_kernel, 'lat', n, nb, pieces, per,...  398 us

profile of v18, /device:TPU:21, one launch (start us, length us, event | category | flops | bytes accessed | tf_op | source)
XLA Modules:
  0.0 406.0 jit_solution(4478221916072623336)
XLA Ops:
  0.6 398.5 %layer.1 = (f32[12,6,192,128]{3,2,1,0:T(8,128)S(1)}, f32[24576,128]{1,0:T(8,128)S(1)}) custom-call(f32[12,6,192,128]{3,2,1,0:T(8,128)} %bitcast.10, f32[12,6,192,128]{3,2,1,0:T(8,128)} %bitcast.11, f32[24576,128]{1,0:T(8,128)} %bitcast.9, f32[96,96,96]{2,1,0:T(8,128)} %pf_hbm.1, f32[96,96,96]{2,1,0:T(8,128)} %pv_hbm.1, bf16[8,192,192]{2,1,0:T(8,128)(2,1)} %constant.34.tab_hbm), custom_call_target="tpu_custom_call" | custom-call | tf_op jit(solution)/shard_map/layer/pallas_call | solution.py:937
  399.1 6.9 %put.1 = (f32[12,6,192,128]{3,2,1,0:T(8,128)}, f32[24576,128]{1,0:T(8,128)}) custom-call(f32[12,6,192,128]{3,2,1,0:T(8,128)S(1)} %get-tuple-element.6.df_ref, f32[24576,128]{1,0:T(8,128)S(1)} %get-tuple-element.7.dw_ref), custom_call_target="tpu_custom_call" | custom-call | tf_op jit(solution)/shard_map/put/pallas_call | solution.py:1023
